TPU v7x, 512 devices: a whole 4x8x8 slice. The times are simulated.
512 devices in a mesh: py: 16 (over y_hi, z), px: 32 (over x, y_lo, core).
Axes of the slice: x: 4, y: 8 (y_hi: 2, y_lo: 4; y = y_hi * 4 + y_lo), z: 8, core: 2. Of those that a mesh axis runs over, the one named last changes fastest.
Arguments:
- residual: bfloat16 [16, 32, 4096, 128], P('py', 'px'), may hold values from -10 to 75
- footprints: bfloat16 [16, 32, 40, 4096], P('py', 'px'), may hold values from 0.049804688 to 1
- traces: bfloat16 [16, 32, 40, 128], P('py', 'px'), may hold values from 0.099609375 to 2
- merge_pairs: int32 [16, 32, 16, 3], P('py', 'px'), may hold values from 0 to 39, as said below
- pair_counts: int32 [16, 32], P('py', 'px'), may hold values from 1 to 16, as said below
- comp_counts: int32 [16, 32], P('py', 'px'), may hold values from 27 to 40, as said below
- row_intersections: int32 [15], replicated, may hold values from 8 to 24
- col_intersections: int32 [31], replicated, may hold values from 8 to 24
Outputs:
- new_footprints: bfloat16 [16, 32, 40, 4096], P('py', 'px')
- new_traces: bfloat16 [16, 32, 40, 128], P('py', 'px')
- correlations: float32 [16, 32, 40, 24], P('py', 'px')
Inputs may be any that keep to these rules, and one draw needn't show every extreme that they name: `merge_pairs`: in slot m < pair_counts[p]: a component id i with 24 <= i < comp_counts[p], a direction d whose neighbour patch exists, and a slot s < 3; ids and (d, s) are distinct within a patch. Later slots are unused. `pair_counts`: at most 3 times the number of neighbours of the patch; some patch has 16. `comp_counts`: at least 24 + pair_counts[p]; components from comp_counts[p] on are unused; some patch has 40.
All inputs are finite; a program needn't handle non-finite values.
Results may differ from a plain program's by a relative error of at most 0.0026.
Values may be sent and summed in bfloat16 or wider, within the bound.
No kernel may reach another device: no remote copies, remote signals or barrier semaphores. Data moves between devices by JAX's collectives and lax.ppermute only.
A program may use at most 64 MiB of HBM per device.

v0:
```python
import jax
import jax.numpy as jnp
from jax import lax
from jax.sharding import PartitionSpec as P

PH = 64
PW = 64
K = 40
NBR = 3
BORDER = 24
MP = 16
ITERS = 4


epsilon = 1e-05


def shifted(value, axis, steps):
    count = lax.axis_size(axis)
    leading, last = (max(0, -steps), min(count, count - steps))
    return lax.ppermute(value, axis, [(source, source + steps) for source in range(leading, last)])


def direction_steps(direction):
    flat_index = direction + (direction >= 4).astype(jnp.int32)
    return (flat_index // 3 - 1, flat_index % 3 - 1)


def lookup_table(table, index):
    places = jnp.arange(table.shape[0], dtype=jnp.int32)
    return jnp.sum(jnp.where(places[None, :] == index[:, None], table[None, :], 0), axis=1)


def pair_offsets(direction, grid_row, grid_col, row_intersections, col_intersections):
    step_y, step_x = direction_steps(direction)
    band_y = jnp.clip(grid_row + jnp.minimum(step_y, 0), 0, row_intersections.shape[0] - 1)
    band_x = jnp.clip(grid_col + jnp.minimum(step_x, 0), 0, col_intersections.shape[0] - 1)
    shift_y = step_y * (PH - lookup_table(row_intersections, band_y))
    shift_x = step_x * (PW - lookup_table(col_intersections, band_x))
    return (shift_y, shift_x)


def move_pixels(values, shift_y, shift_x, filler):
    count = values.shape[0]
    row_ids = jnp.arange(PH, dtype=jnp.int32)
    col_ids = jnp.arange(PW, dtype=jnp.int32)
    pick_rows = (row_ids[None, None, :] == row_ids[None, :, None] - shift_y[:, None, None]).astype(
        jnp.float32
    )
    pick_cols = (col_ids[None, :, None] == col_ids[None, None, :] - shift_x[:, None, None]).astype(
        jnp.float32
    )
    image = values.reshape(count, PH, PW)
    moved = jnp.einsum("myk,mkx->myx", pick_rows, image, precision=lax.Precision.HIGHEST)
    moved = jnp.einsum("myk,mkx->myx", moved, pick_cols, precision=lax.Precision.HIGHEST)
    moved = moved.reshape(count, PH * PW)
    pixels = jnp.arange(PH * PW, dtype=jnp.int32)
    source_y = pixels[None, :] // PW - shift_y[:, None]
    source_x = pixels[None, :] % PW - shift_x[:, None]
    inside = (source_y >= 0) & (source_y < PH) & (source_x >= 0) & (source_x < PW)
    return jnp.where(inside, moved, filler)


def direction_index(step_y, step_x):
    flat_index = (step_y + 1) * 3 + step_x + 1
    return flat_index - (1 if flat_index > 4 else 0)


def block_rows(rows, which):
    return rows[NBR * which : NBR * (which + 1)]


def column_packet(packed, offset):
    return jnp.concatenate(
        [block_rows(packed, direction_index(vertical, offset)) for vertical in (-1, 0, 1)], axis=0
    )


def row_packet(packed, sideways, offset):
    return jnp.concatenate(
        [
            block_rows(packed, direction_index(offset, 0)),
            block_rows(sideways[1], offset + 1),
            block_rows(sideways[-1], offset + 1),
        ],
        axis=0,
    )


def direct_pieces(sideways, upright):
    pieces = []
    for direction in range(8):
        flat_index = direction + (1 if direction >= 4 else 0)
        step_y = flat_index // 3 - 1
        step_x = flat_index % 3 - 1
        if step_y == 0:
            pieces.append(block_rows(sideways[-step_x], 1))
        elif step_x == 0:
            pieces.append(block_rows(upright[-step_y], 0))
        else:
            pieces.append(block_rows(upright[-step_y], 1 if step_x == -1 else 2))
    return jnp.concatenate(pieces, axis=0)


def border_rows(packed):
    sideways = {}
    for offset in (1, -1):
        sideways[offset] = shifted(column_packet(packed, offset), "px", offset)
    upright = {}
    for offset in (1, -1):
        upright[offset] = shifted(row_packet(packed, sideways, offset), "py", offset)
    return direct_pieces(sideways, upright)


def refit_outgoing(sending, border_index, in_use, border):
    border_mask = (border_index[None, :] == jnp.arange(BORDER, dtype=jnp.int32)[:, None]) & in_use[
        None, :
    ]
    border_hit = jnp.any(border_mask, axis=1)
    merged_rows = jnp.dot(
        border_mask.astype(jnp.bfloat16), sending, preferred_element_type=jnp.float32
    ).astype(jnp.bfloat16)
    return jnp.where(border_hit[:, None], merged_rows, border)


def returned_rows(sending, border_index, in_use, border, packed, exists):
    outgoing = refit_outgoing(sending, border_index, in_use, border)
    sideways = {}
    for offset in (1, -1):
        sideways[offset] = shifted(column_packet(outgoing, offset), "px", offset)
    upright = {}
    for offset in (1, -1):
        upright[offset] = shifted(row_packet(outgoing, sideways, offset), "py", offset)
    returned = direct_pieces(sideways, upright)
    return jnp.where(exists[:, None], returned, packed)


def neighbour_exists(grid_row, grid_col, grid_rows, grid_cols):
    flags = []
    for direction in range(8):
        flat_index = direction + (1 if direction >= 4 else 0)
        target_y = grid_row + flat_index // 3 - 1
        target_x = grid_col + flat_index % 3 - 1
        flags.append(
            (target_y >= 0) & (target_y < grid_rows) & (target_x >= 0) & (target_x < grid_cols)
        )
    return jnp.repeat(jnp.stack(flags), NBR)


def refit_pairs(
    residue,
    own_footprints,
    own_traces,
    pair_table,
    pair_total,
    border,
    grid_row,
    grid_col,
    row_intersections,
    col_intersections,
    first_product,
):
    pixel_count = PH * PW
    frame_count = own_traces.shape[1]
    owned_ids = pair_table[:, 0]
    direction = pair_table[:, 1]
    border_index = NBR * direction + pair_table[:, 2]
    in_use = jnp.arange(MP, dtype=jnp.int32) < pair_total
    a_own = jnp.take(own_footprints, owned_ids, axis=0).astype(jnp.float32)
    c_own = jnp.take(own_traces, owned_ids, axis=0).astype(jnp.float32)
    remote = jnp.take(border, border_index, axis=0)
    a_remote_raw = remote[:, :pixel_count].astype(jnp.float32)
    c_remote = remote[:, pixel_count:].astype(jnp.float32)
    shift_y, shift_x = pair_offsets(
        direction, grid_row, grid_col, row_intersections, col_intersections
    )
    a_remote = move_pixels(a_remote_raw, shift_y, shift_x, 0.0)
    trace_now = c_own
    shape_now = a_own
    for iteration in range(ITERS):
        if iteration == 0:
            across = first_product
        else:
            across = lax.dot_general(
                trace_now.astype(jnp.bfloat16),
                residue,
                (((1,), (1,)), ((), ())),
                preferred_element_type=jnp.float32,
            )
        across = (
            across
            + a_own * jnp.sum(c_own * trace_now, axis=1, keepdims=True)
            + a_remote * jnp.sum(c_remote * trace_now, axis=1, keepdims=True)
        )
        shape_now = jnp.maximum(across, 0.0) / (
            jnp.sum(trace_now * trace_now, axis=1, keepdims=True) + epsilon * frame_count
        )
        downward = jnp.dot(
            shape_now.astype(jnp.bfloat16), residue, preferred_element_type=jnp.float32
        )
        downward = (
            downward
            + c_own * jnp.sum(a_own * shape_now, axis=1, keepdims=True)
            + c_remote * jnp.sum(a_remote * shape_now, axis=1, keepdims=True)
        )
        trace_now = jnp.maximum(downward, 0.0) / (
            jnp.sum(shape_now * shape_now, axis=1, keepdims=True) + epsilon * pixel_count
        )
    footprint_out = shape_now.astype(jnp.bfloat16)
    trace_out = trace_now.astype(jnp.bfloat16)
    remote_new = move_pixels(
        footprint_out.astype(jnp.float32), -shift_y, -shift_x, a_remote_raw
    ).astype(jnp.bfloat16)
    owner_mask = (owned_ids[None, :] == jnp.arange(K, dtype=jnp.int32)[:, None]) & in_use[None, :]
    owner_hot = owner_mask.astype(jnp.bfloat16)
    owner_hit = jnp.any(owner_mask, axis=1)
    new_foot = jnp.where(
        owner_hit[:, None],
        jnp.dot(owner_hot, footprint_out, preferred_element_type=jnp.float32).astype(jnp.bfloat16),
        own_footprints,
    )
    new_trace = jnp.where(
        owner_hit[:, None],
        jnp.dot(owner_hot, trace_out, preferred_element_type=jnp.float32).astype(jnp.bfloat16),
        own_traces,
    )
    sending = jnp.concatenate([remote_new, trace_out], axis=1)
    return (new_foot, new_trace, sending, border_index, in_use)


def shards(
    residual,
    footprints,
    traces,
    merge_pairs,
    pair_counts,
    comp_counts,
    row_intersections,
    col_intersections,
):
    residue = residual[0, 0]
    own_footprints = footprints[0, 0]
    own_traces = traces[0, 0]
    pair_table = merge_pairs[0, 0]
    pair_total = pair_counts[0, 0]
    component_total = comp_counts[0, 0]
    grid_row = lax.axis_index("py")
    grid_col = lax.axis_index("px")
    grid_rows = lax.axis_size("py")
    grid_cols = lax.axis_size("px")
    pixel_count = PH * PW
    first_traces = jnp.take(own_traces, pair_table[:, 0], axis=0)
    first_product = lax.dot_general(
        first_traces, residue, (((1,), (1,)), ((), ())), preferred_element_type=jnp.float32
    )
    packed = jnp.concatenate([own_footprints[:BORDER], own_traces[:BORDER]], axis=1)
    border = border_rows(packed)
    local = own_traces.astype(jnp.float32)
    local = local - jnp.mean(local, axis=-1, keepdims=True)
    remote = border[:, pixel_count:].astype(jnp.float32)
    remote = remote - jnp.mean(remote, axis=-1, keepdims=True)
    covariance = jnp.dot(local, remote.T, precision=lax.Precision.HIGHEST) / local.shape[1]
    spread_local = jnp.mean(local * local, axis=-1)
    spread_remote = jnp.mean(remote * remote, axis=-1)
    correlation = covariance / jnp.sqrt(
        (spread_local[:, None] + epsilon) * (spread_remote[None, :] + epsilon)
    )
    new_foot, new_trace, sending, border_index, in_use = refit_pairs(
        residue,
        own_footprints,
        own_traces,
        pair_table,
        pair_total,
        border,
        grid_row,
        grid_col,
        row_intersections,
        col_intersections,
        first_product,
    )
    exists = neighbour_exists(grid_row, grid_col, grid_rows, grid_cols)
    reserved = returned_rows(sending, border_index, in_use, border, packed, exists)
    reserved_foot = reserved[:, :pixel_count]
    reserved_trace = reserved[:, pixel_count:]
    alive = jnp.arange(K, dtype=jnp.int32) < component_total
    zero_value = jnp.zeros((), jnp.bfloat16)
    footprints_out = jnp.where(
        alive[:, None], jnp.concatenate([reserved_foot, new_foot[BORDER:]], axis=0), zero_value
    )
    traces_out = jnp.where(
        alive[:, None], jnp.concatenate([reserved_trace, new_trace[BORDER:]], axis=0), zero_value
    )
    correlations_out = jnp.where(alive[:, None], correlation, 0.0)
    return (footprints_out[None, None], traces_out[None, None], correlations_out[None, None])


def solution(mesh):
    in_specs = (
        P("py", "px", None, None),
        P("py", "px", None, None),
        P("py", "px", None, None),
        P("py", "px", None, None),
        P("py", "px"),
        P("py", "px"),
        P(),
        P(),
    )
    out_specs = (P("py", "px", None, None), P("py", "px", None, None), P("py", "px", None, None))
    return jax.shard_map(shards, mesh=mesh, in_specs=in_specs, out_specs=out_specs, check_vma=False)
```

profile of v0, /device:TPU:57, one launch (start us, length us, event | category | flops | bytes accessed | tf_op | source)
XLA Modules:
  0.0 84.8 jit_solution(5990869232642741490)
XLA Ops:
  0.7 1.0 %slice_bitcast_fusion.1 = bf16[24,4096]{1,0:T(8,128)(2,1)S(1)} fusion(bf16[1,1,40,4096]{3,2,1,0:T(8,128)(2,1)} %param.11), kind=kLoop, calls=%fused_computation.111 | loop fusion | bytes 393216 | tf_op jit(solution)/shard_map/slice | solution.py:256
  2.0 6.2 %collective-permute-start = (bf16[9,4224]{1,0:T(8,128)(2,1)S(1)}, bf16[9,4224]{1,0:T(8,128)(2,1)S(1)}, u32[]{:S(2)}, u32[]{:S(2)}) collective-permute-start(bf16[9,4224]{1,0:T(8,128)(2,1)S(1)} %pad_maximum_fusion.1), channel_id=1, source_target_pairs={{0,1},{1,2},{2,3},{3,4},{4,5},{5,6},{6,7},{7,8},{8,9},{9,10},{10,1... | collective-permute-start | bytes 228104 | tf_op jit(solution)/shard_map/ppermute | solution.py:21
  8.2 1.9 %collective-permute-start.1 = (bf16[9,4224]{1,0:T(8,128)(2,1)S(1)}, bf16[9,4224]{1,0:T(8,128)(2,1)S(1)}, u32[]{:S(2)}, u32[]{:S(2)}) collective-permute-start(bf16[9,4224]{1,0:T(8,128)(2,1)S(1)} %pad_maximum_fusion.2), channel_id=1, source_target_pairs={{1,0},{2,1},{3,2},{4,3},{5,4},{6,5},{7,6},{8,7},{9,8},{10,9},{11,1... | collective-permute-start | bytes 228104 | tf_op jit(solution)/shard_map/ppermute | solution.py:21
  11.4 0.7 copy-done.4
  12.1 0.2 select_reduce_fusion
  12.2 0.7 copy-done.5
  12.9 0.2 select_reduce_fusion.1
  14.4 0.6 gather_fusion.2
  15.0 0.6 gather_fusion
  15.7 1.6 %collective-permute-done.1 = bf16[9,4224]{1,0:T(8,128)(2,1)S(1)} collective-permute-done((bf16[9,4224]{1,0:T(8,128)(2,1)S(1)}, bf16[9,4224]{1,0:T(8,128)(2,1)S(1)}, u32[]{:S(2)}, u32[]{:S(2)}) %collective-permute-start.1) | collective-permute-done | bytes 76064 | tf_op jit(solution)/shard_map/ppermute | solution.py:21
  17.4 10.2 %collective-permute-start.3 = (bf16[9,4224]{1,0:T(8,128)(2,1)S(1)}, bf16[9,4224]{1,0:T(8,128)(2,1)S(1)}, u32[]{:S(2)}, u32[]{:S(2)}) collective-permute-start(bf16[9,4224]{1,0:T(8,128)(2,1)S(1)} %pad_maximum_fusion.4), channel_id=1, source_target_pairs={{32,0},{64,32},{96,64},{128,96},{160,128},{192,160},{224,192},{256... | collective-permute-start | bytes 228104 | tf_op jit(solution)/shard_map/ppermute | solution.py:21
  27.7 1.9 %collective-permute-start.2 = (bf16[9,4224]{1,0:T(8,128)(2,1)S(1)}, bf16[9,4224]{1,0:T(8,128)(2,1)S(1)}, u32[]{:S(2)}, u32[]{:S(2)}) collective-permute-start(bf16[9,4224]{1,0:T(8,128)(2,1)S(1)} %pad_maximum_fusion.3), channel_id=1, source_target_pairs={{0,32},{32,64},{64,96},{96,128},{128,160},{160,192},{192,224},{224... | collective-permute-start | bytes 228104 | tf_op jit(solution)/shard_map/ppermute | solution.py:21
  29.6 1.3 %collective-permute-done.3 = bf16[9,4224]{1,0:T(8,128)(2,1)S(1)} collective-permute-done((bf16[9,4224]{1,0:T(8,128)(2,1)S(1)}, bf16[9,4224]{1,0:T(8,128)(2,1)S(1)}, u32[]{:S(2)}, u32[]{:S(2)}) %collective-permute-start.3) | collective-permute-done | bytes 76064 | tf_op jit(solution)/shard_map/ppermute | solution.py:21
  31.0 10.0 %collective-permute-done.2 = bf16[9,4224]{1,0:T(8,128)(2,1)S(1)} collective-permute-done((bf16[9,4224]{1,0:T(8,128)(2,1)S(1)}, bf16[9,4224]{1,0:T(8,128)(2,1)S(1)}, u32[]{:S(2)}, u32[]{:S(2)}) %collective-permute-start.2) | collective-permute-done | bytes 76064 | tf_op jit(solution)/shard_map/ppermute | solution.py:21
  41.1 2.1 %concatenate.69 = bf16[24,4224]{1,0:T(8,128)(2,1)S(1)} concatenate(bf16[3,4224]{1,0:T(4,128)(2,1)S(1)} %get-tuple-element.79, bf16[3,4224]{1,0:T(4,128)(2,1)S(1)} %get-tuple-element.78, bf16[3,4224]{1,0:T(4,128)(2,1)S(1)} %get-tuple-element.77, bf16[3,4224]{1,0:T(4,128)(2,1)S(1)} %get-tuple-element.72, bf16[3,4224]{1,0:T(4,128)(2,1)S(1)} %get-tuple-element.75, ...), dimensions={0} | concatenate | bytes 405504 | tf_op jit(solution)/shard_map/concatenate | solution.py:102
  43.2 0.6 gather_fusion.1
  44.0 0.2 reshape.430
  44.2 0.3 fusion.38
  44.6 0.5 fusion.39
  45.0 0.2 reshape.431
  45.2 0.2 fusion.89
  45.4 0.6 fusion.41
  46.0 0.4 fusion.90
  46.4 0.6 fusion.42
  47.0 0.4 fusion.91
  47.4 0.6 fusion.43
  48.0 0.4 fusion.92
  48.4 0.6 fusion.44
  48.9 0.2 reshape.432
  49.2 0.4 fusion.99
  49.7 0.3 fusion.37
  50.0 0.5 fusion.40
  50.4 0.3 reshape.433
  50.7 0.3 fusion.28
  51.0 0.3 fusion.97
  51.4 0.3 fusion
  52.0 4.7 %collective-permute-start.4 = (bf16[9,4224]{1,0:T(8,128)(2,1)S(1)}, bf16[9,4224]{1,0:T(8,128)(2,1)S(1)}, u32[]{:S(2)}, u32[]{:S(2)}) collective-permute-start(bf16[9,4224]{1,0:T(8,128)(2,1)S(1)} %pad_maximum_fusion.5), channel_id=1, source_target_pairs={{0,1},{1,2},{2,3},{3,4},{4,5},{5,6},{6,7},{7,8},{8,9},{9,10},{10,1... | collective-permute-start | bytes 228104 | tf_op jit(solution)/shard_map/ppermute | solution.py:21
  56.8 1.9 %collective-permute-start.5 = (bf16[9,4224]{1,0:T(8,128)(2,1)S(1)}, bf16[9,4224]{1,0:T(8,128)(2,1)S(1)}, u32[]{:S(2)}, u32[]{:S(2)}) collective-permute-start(bf16[9,4224]{1,0:T(8,128)(2,1)S(1)} %pad_maximum_fusion.6), channel_id=1, source_target_pairs={{1,0},{2,1},{3,2},{4,3},{5,4},{6,5},{7,6},{8,7},{9,8},{10,9},{11,1... | collective-permute-start | bytes 228104 | tf_op jit(solution)/shard_map/ppermute | solution.py:21
  58.9 0.2 fusion.83
  59.1 0.8 fusion.15
  60.0 7.0 %collective-permute-done.5 = bf16[9,4224]{1,0:T(8,128)(2,1)S(1)} collective-permute-done((bf16[9,4224]{1,0:T(8,128)(2,1)S(1)}, bf16[9,4224]{1,0:T(8,128)(2,1)S(1)}, u32[]{:S(2)}, u32[]{:S(2)}) %collective-permute-start.5) | collective-permute-done | bytes 76064 | tf_op jit(solution)/shard_map/ppermute | solution.py:21
  67.1 1.9 %collective-permute-start.7 = (bf16[9,4224]{1,0:T(8,128)(2,1)S(1)}, bf16[9,4224]{1,0:T(8,128)(2,1)S(1)}, u32[]{:S(2)}, u32[]{:S(2)}) collective-permute-start(bf16[9,4224]{1,0:T(8,128)(2,1)S(1)} %pad_maximum_fusion.8), channel_id=1, source_target_pairs={{32,0},{64,32},{96,64},{128,96},{160,128},{192,160},{224,192},{256... | collective-permute-start | bytes 228104 | tf_op jit(solution)/shard_map/ppermute | solution.py:21
  69.1 3.4 %collective-permute-start.6 = (bf16[9,4224]{1,0:T(8,128)(2,1)S(1)}, bf16[9,4224]{1,0:T(8,128)(2,1)S(1)}, u32[]{:S(2)}, u32[]{:S(2)}) collective-permute-start(bf16[9,4224]{1,0:T(8,128)(2,1)S(1)} %pad_maximum_fusion.7), channel_id=1, source_target_pairs={{0,32},{32,64},{64,96},{96,128},{128,160},{160,192},{192,224},{224... | collective-permute-start | bytes 228104 | tf_op jit(solution)/shard_map/ppermute | solution.py:21
  72.5 0.7 collective-permute-done.7
  73.2 7.7 %collective-permute-done.6 = bf16[9,4224]{1,0:T(8,128)(2,1)S(1)} collective-permute-done((bf16[9,4224]{1,0:T(8,128)(2,1)S(1)}, bf16[9,4224]{1,0:T(8,128)(2,1)S(1)}, u32[]{:S(2)}, u32[]{:S(2)}) %collective-permute-start.6) | collective-permute-done | bytes 76064 | tf_op jit(solution)/shard_map/ppermute | solution.py:21
  81.0 2.1 %concatenate.75 = bf16[24,4224]{1,0:T(8,128)(2,1)S(1)} concatenate(bf16[3,4224]{1,0:T(4,128)(2,1)S(1)} %get-tuple-element.67, bf16[3,4224]{1,0:T(4,128)(2,1)S(1)} %get-tuple-element.66, bf16[3,4224]{1,0:T(4,128)(2,1)S(1)} %get-tuple-element.65, bf16[3,4224]{1,0:T(4,128)(2,1)S(1)} %get-tuple-element.60, bf16[3,4224]{1,0:T(4,128)(2,1)S(1)} %get-tuple-element.63, ...), dimensions={0} | concatenate | bytes 405504 | tf_op jit(solution)/shard_map/concatenate | solution.py:102
  83.2 0.7 maximum_select_fusion.1
  83.9 0.8 %maximum_select_fusion = bf16[1,1,40,4096]{3,2,1,0:T(8,128)(2,1)} fusion(bf16[1,1,16,4096]{3,2,1,0:T(8,128)(2,1)S(1)} %fusion.61, bf16[1,1,24,4096]{3,2,1,0:T(8,128)(2,1)S(1)} %slice_bitcast_fusion, pred[40]{0:T(512)(128)(4,1)S(1)} %iota_compare_fusion.13), kind=kLoop, calls=%fused_computation.83 | loop fusion | flops 819200 | bytes 655400 | tf_op jit(solution)/shard_map/jit(_where)/select_n | solution.py:287
  (74 shorter events, 3.1 us)
Async XLA Ops:
  0.6 44.8 %copy-start = (bf16[1,1,4096,128]{3,2,1,0:T(8,128)(2,1)S(1)}, bf16[1,1,4096,128]{3,2,1,0:T(8,128)(2,1)}, u32[]{:S(2)}) copy-start(bf16[1,1,4096,128]{3,2,1,0:T(8,128)(2,1)} %param.10) | copy-start | bytes 3145732
  0.6 1.0 %copy-start.2 = (bf16[1,1,40,128]{3,2,1,0:T(8,128)(2,1)S(1)}, bf16[1,1,40,128]{3,2,1,0:T(8,128)(2,1)}, u32[]{:S(2)}) copy-start(bf16[1,1,40,128]{3,2,1,0:T(8,128)(2,1)} %param.12) | copy-start | bytes 30724
  1.8 8.3 %copy-start.3 = (s32[1,1,16,3]{2,1,3,0:T(1,128)S(1)}, s32[1,1,16,3]{2,1,3,0:T(1,128)}, u32[]{:S(2)}) copy-start(s32[1,1,16,3]{2,1,3,0:T(1,128)} %param.13) | copy-start | bytes 580
  1.9 13.0 %copy-start.1 = (bf16[1,1,40,4096]{3,2,1,0:T(8,128)(2,1)S(1)}, bf16[1,1,40,4096]{3,2,1,0:T(8,128)(2,1)}, u32[]{:S(2)}) copy-start(bf16[1,1,40,4096]{3,2,1,0:T(8,128)(2,1)} %param.11) | copy-start | bytes 983044
  2.0 13.7 %collective-permute-start = (bf16[9,4224]{1,0:T(8,128)(2,1)S(1)}, bf16[9,4224]{1,0:T(8,128)(2,1)S(1)}, u32[]{:S(2)}, u32[]{:S(2)}) collective-permute-start(bf16[9,4224]{1,0:T(8,128)(2,1)S(1)} %pad_maximum_fusion.1), channel_id=1, source_target_pairs={{0,1},{1,2},{2,3},{3,4},{4,5},{5,6},{6,7},{7,8},{8,9},{9,10},{10,1... | collective-permute-start | bytes 228104 | tf_op jit(solution)/shard_map/ppermute | solution.py:21
  8.2 9.0 %collective-permute-start.1 = (bf16[9,4224]{1,0:T(8,128)(2,1)S(1)}, bf16[9,4224]{1,0:T(8,128)(2,1)S(1)}, u32[]{:S(2)}, u32[]{:S(2)}) collective-permute-start(bf16[9,4224]{1,0:T(8,128)(2,1)S(1)} %pad_maximum_fusion.2), channel_id=1, source_target_pairs={{1,0},{2,1},{3,2},{4,3},{5,4},{6,5},{7,6},{8,7},{9,8},{10,9},{11,1... | collective-permute-start | bytes 228104 | tf_op jit(solution)/shard_map/ppermute | solution.py:21
  11.4 0.7 copy-start.4
  12.2 0.7 copy-start.5
  17.4 13.6 %collective-permute-start.3 = (bf16[9,4224]{1,0:T(8,128)(2,1)S(1)}, bf16[9,4224]{1,0:T(8,128)(2,1)S(1)}, u32[]{:S(2)}, u32[]{:S(2)}) collective-permute-start(bf16[9,4224]{1,0:T(8,128)(2,1)S(1)} %pad_maximum_fusion.4), channel_id=1, source_target_pairs={{32,0},{64,32},{96,64},{128,96},{160,128},{192,160},{224,192},{256... | collective-permute-start | bytes 228104 | tf_op jit(solution)/shard_map/ppermute | solution.py:21
  27.7 13.4 %collective-permute-start.2 = (bf16[9,4224]{1,0:T(8,128)(2,1)S(1)}, bf16[9,4224]{1,0:T(8,128)(2,1)S(1)}, u32[]{:S(2)}, u32[]{:S(2)}) collective-permute-start(bf16[9,4224]{1,0:T(8,128)(2,1)S(1)} %pad_maximum_fusion.3), channel_id=1, source_target_pairs={{0,32},{32,64},{64,96},{96,128},{128,160},{160,192},{192,224},{224... | collective-permute-start | bytes 228104 | tf_op jit(solution)/shard_map/ppermute | solution.py:21
  52.0 8.0 %collective-permute-start.4 = (bf16[9,4224]{1,0:T(8,128)(2,1)S(1)}, bf16[9,4224]{1,0:T(8,128)(2,1)S(1)}, u32[]{:S(2)}, u32[]{:S(2)}) collective-permute-start(bf16[9,4224]{1,0:T(8,128)(2,1)S(1)} %pad_maximum_fusion.5), channel_id=1, source_target_pairs={{0,1},{1,2},{2,3},{3,4},{4,5},{5,6},{6,7},{7,8},{8,9},{9,10},{10,1... | collective-permute-start | bytes 228104 | tf_op jit(solution)/shard_map/ppermute | solution.py:21
  56.8 10.2 %collective-permute-start.5 = (bf16[9,4224]{1,0:T(8,128)(2,1)S(1)}, bf16[9,4224]{1,0:T(8,128)(2,1)S(1)}, u32[]{:S(2)}, u32[]{:S(2)}) collective-permute-start(bf16[9,4224]{1,0:T(8,128)(2,1)S(1)} %pad_maximum_fusion.6), channel_id=1, source_target_pairs={{1,0},{2,1},{3,2},{4,3},{5,4},{6,5},{7,6},{8,7},{9,8},{10,9},{11,1... | collective-permute-start | bytes 228104 | tf_op jit(solution)/shard_map/ppermute | solution.py:21
  67.1 6.1 %collective-permute-start.7 = (bf16[9,4224]{1,0:T(8,128)(2,1)S(1)}, bf16[9,4224]{1,0:T(8,128)(2,1)S(1)}, u32[]{:S(2)}, u32[]{:S(2)}) collective-permute-start(bf16[9,4224]{1,0:T(8,128)(2,1)S(1)} %pad_maximum_fusion.8), channel_id=1, source_target_pairs={{32,0},{64,32},{96,64},{128,96},{160,128},{192,160},{224,192},{256... | collective-permute-start | bytes 228104 | tf_op jit(solution)/shard_map/ppermute | solution.py:21
  69.1 11.8 %collective-permute-start.6 = (bf16[9,4224]{1,0:T(8,128)(2,1)S(1)}, bf16[9,4224]{1,0:T(8,128)(2,1)S(1)}, u32[]{:S(2)}, u32[]{:S(2)}) collective-permute-start(bf16[9,4224]{1,0:T(8,128)(2,1)S(1)} %pad_maximum_fusion.7), channel_id=1, source_target_pairs={{0,32},{32,64},{64,96},{96,128},{128,160},{160,192},{192,224},{224... | collective-permute-start | bytes 228104 | tf_op jit(solution)/shard_map/ppermute | solution.py:21
where the time goes:
time: 85.1 us; the launch traced here: 84.8 us
  starting transfers between devices  32.2 us (38%)
  waiting for transfers between devices  28.3 us (33%)
  local copies, waits for them, and re-layouts  10.3 us (12%)
  matrix products  7.1 us (8%)
  other arithmetic  4.46 us (5%)
  between operations  2.52 us (3%)
    ppermute x8, starting transfers between devices, shifted(): lax.ppermute(value, axis, [(source, source + steps) for source in range(l...  32.2 us
    ppermute x8, waiting for transfers between devices, shifted(): lax.ppermute(value, axis, [(source, source + steps) for source in range(l...  28.3 us
    concatenate x2, local copies, waits for them, and re-layouts, direct_pieces(): return jnp.concatenate(pieces, axis=0)  4.26 us
  transfers between devices with their start and end apart: 8, of which 6 were waited for; matrix products, arithmetic and copies ran while one was open for 5% of the time, Pallas kernels for 0%

commit v1 on v0

v1 whole, which is shorter than its diff:
```python
import jax
import jax.numpy as jnp
from jax import lax
from jax.experimental import pallas as pl
from jax.experimental.pallas import tpu as pltpu
from jax.sharding import PartitionSpec as P

PH = 64
PW = 64
NPIX = PH * PW
K = 40
NBR = 3
BORDER = 24
MP = 16
F = 128
ITERS = 4
OV_HI = 24
epsilon = 1e-05

BAND = OV_HI * PW
LOW = NPIX - BAND
CW = BAND // 4
EW = 896
XW = 2 * CW + EW
YW = 3 * CW
CH = 128
PAD = 9
PBW = (PAD + 12 + PAD) * CH

f32 = jnp.float32
bf16 = jnp.bfloat16


def iota(shape, dim):
    return lax.broadcasted_iota(jnp.int32, shape, dim)


def sides():
    row = lax.axis_index("py")
    col = lax.axis_index("px")
    sy = 1 - 2 * lax.rem(row, 2)
    sx = 1 - 2 * lax.rem(col, 2)
    return row, col, (sy, -sy), (sx, -sx)


def direction(dy, dx):
    flat = (dy + 1) * 3 + dx + 1
    return flat - (flat > 4).astype(jnp.int32) if not isinstance(flat, int) else flat - (flat > 4)


def hot(mask):
    return jnp.where(mask, 1.0, 0.0).astype(bf16)


def dot(a, b):
    return jnp.dot(a, b, preferred_element_type=f32)


def band_start(dy):
    return jnp.where(dy > 0, LOW, 0)


def pack_rows(pick, pieces, tail, width):
    return dot(pick, jnp.concatenate(pieces + [tail], axis=0)).astype(bf16)


def pixel_shift(dy, dx, row, col, row_ref, col_ref, rows, cols):
    ri = row_ref[jnp.clip(row + jnp.minimum(dy, 0), 0, rows - 2)]
    ci = col_ref[jnp.clip(col + jnp.minimum(dx, 0), 0, cols - 2)]
    return dy * (OV_HI - ri), dx * (PW - ci), ri, ci


def column_matrix(ox):
    i = iota((CH, CH), 0)
    o = iota((CH, CH), 1)
    x = (o & (PW - 1)) - ox
    return hot((i == o - ox) & (x >= 0) & (x < PW))


def band_matrix(odd, ox):
    i = iota((2 * CH, CH), 0)
    o = iota((2 * CH, CH), 1)
    x = (o & (PW - 1)) - ox
    return hot((i == o + CH - PW * odd - ox) & (x >= 0) & (x < PW))


def place_band(pbuf, at, band, shift, ox, rows):
    pbuf[at, :, PAD * CH : PAD * CH + BAND] = band.astype(bf16)
    chunks = shift >> 1
    first = pl.multiple_of((PAD - 1 - chunks) * CH, CH)
    stack = jnp.concatenate(
        [pbuf[at, :, pl.ds(pl.multiple_of(first + CH * m, CH), 2 * CH)] for m in range(12)], axis=0
    )
    return dot(stack, band_matrix(shift & 1, ox))


def place_whole(whole, ox, rows):
    stack = jnp.concatenate(
        [whole[:, CH * m : CH * (m + 1)] for m in range(32)], axis=0
    ).astype(bf16)
    return dot(stack, column_matrix(ox))


def receive(select, n, xs, ys, acc, pbuf, row, col, sy, sx, row_ref, col_ref, rows, cols):
    pbuf[...] = jnp.zeros(pbuf.shape, bf16)
    tail = jnp.zeros((n, 2 * CH), f32)
    whole = None
    for t in range(2):
        picked = dot(select(direction(0, sx[t])), xs[t][:, 2 * CW : XW])
        full = jnp.concatenate(
            [picked[n * g : n * (g + 1)] for g in range(4)] + [picked[4 * n :, 0:512]], axis=1
        )
        tail = tail + picked[4 * n :, 512 : 512 + 2 * CH]
        _, ox, _, _ = pixel_shift(0, sx[t], row, col, row_ref, col_ref, rows, cols)
        moved = place_whole(full, ox, n)
        whole = moved if whole is None else whole + moved
    for m in range(32):
        acc[:, CH * m : CH * (m + 1)] = whole[n * m : n * (m + 1)]
    for u in range(2):
        moved = None
        for j, dx in enumerate((0, sx[0], sx[1])):
            picked = dot(select(direction(sy[u], dx)), ys[u][:, CW * j : CW * (j + 1)])
            band = jnp.concatenate([picked[n * g : n * (g + 1)] for g in range(4)], axis=1)
            tail = tail + picked[4 * n :, 0 : 2 * CH]
            shift, ox, _, _ = pixel_shift(sy[u], dx, row, col, row_ref, col_ref, rows, cols)
            one = place_band(pbuf, 3 * u + j, band, shift, ox, n)
            moved = one if moved is None else moved + one
        start = band_start(sy[u])
        for m in range(12):
            lanes = pl.ds(pl.multiple_of(start + CH * m, CH), CH)
            acc[:, lanes] += moved[n * m : n * (m + 1)]
    return tail


def send_all(pick, src, tail_narrow, tail_wide, outs, sy, sx):
    xa, xb, va, vb = outs

    def band_seg(dy, dx):
        start = band_start(dy)
        pieces = [
            src[:, pl.ds(pl.multiple_of(start + CW * g, CH), CW)] for g in range(4)
        ]
        return pack_rows(pick(direction(dy, dx)), pieces, tail_narrow, CW)

    def whole_seg(dx):
        pieces = [src[:, EW * g : EW * (g + 1)] for g in range(4)]
        last = jnp.concatenate([src[:, 4 * EW : NPIX], tail_wide], axis=1)
        return pack_rows(pick(direction(0, dx)), pieces, last, EW)

    for t, out in enumerate((xa, xb)):
        out[:, 0:CW] = band_seg(sy[0], sx[t])
        out[:, CW : 2 * CW] = band_seg(sy[1], sx[t])
        out[:, 2 * CW : XW] = whole_seg(sx[t])
    va[...] = band_seg(sy[0], 0)
    vb[...] = band_seg(sy[1], 0)


def group_of(j):
    g = (j >= 3).astype(jnp.int32) + (j >= 6) + (j >= 9) + (j >= 12)
    return g, j - 3 * g


def pack_kernel(foot, tr, xa, xb, va, vb, src):
    _, _, sy, sx = sides()
    src[...] = foot[0:32, :]
    trace = tr[0:32, :]
    blank = jnp.zeros((32, 2 * CH), bf16)
    tail = jnp.concatenate([trace, blank], axis=1)
    j = iota((16, 160), 0)
    kk = iota((16, 160), 1)
    g, s = group_of(j)
    same = ((kk >> 5) == g) & (j < 15)
    comp = (kk & 31) - s

    def pick(d):
        return hot(same & (comp == 3 * d))

    send_all(pick, src, tail, tail, (xa, xb, va, vb), sy, sx)


def slot_masks(table, total):
    own = table[:, 0:1]
    idx = NBR * table[:, 1:2] + table[:, 2:3]
    live = iota((MP, 1), 0) < total
    return own, idx, live


def refit_kernel(
    rows, cols, count, row_ref, col_ref, res, foot, tr, table, wide, rxa, rxb, rya, ryb,
    xa, xb, va, vb, merged, mtrace, acc, own, pbuf,
):
    row, col, sy, sx = sides()
    total = count[0, 0]
    ids, idx, live = slot_masks(table, total)
    own_hot = hot(ids == iota((MP, K), 1))
    own[...] = dot(own_hot, foot[...])
    c_own = dot(own_hot, tr[...])
    j5 = iota((5 * MP, 16), 1)
    g5 = iota((5 * MP, 16), 0) >> 4
    s5 = j5 - 3 * g5
    idx5 = jnp.concatenate([jnp.where(live, idx, -100)] * 5, axis=0)
    fits = (s5 >= 0) & (s5 < 3)

    def select(d):
        return hot(fits & (idx5 == 3 * d + s5))

    tail = receive(
        select, MP, (rxa, rxb), (rya, ryb), acc, pbuf, row, col, sy, sx, row_ref, col_ref, rows, cols
    )
    c_rem = tail[:, 0:F]
    trace = c_own
    step = 512
    for it in range(ITERS):
        tb = trace.astype(bf16)
        co = jnp.sum(c_own * trace, axis=1, keepdims=True)
        cr = jnp.sum(c_rem * trace, axis=1, keepdims=True)
        scale = 1.0 / (jnp.sum(trace * trace, axis=1, keepdims=True) + epsilon * F)
        down = jnp.zeros((MP, F), f32)
        sa = jnp.zeros((MP, CH), f32)
        sr = jnp.zeros((MP, CH), f32)
        ss = jnp.zeros((MP, CH), f32)
        for n in range(NPIX // step):
            lanes = slice(step * n, step * (n + 1))
            part = res[lanes, :]
            across = lax.dot_general(
                tb, part, (((1,), (1,)), ((), ())), preferred_element_type=f32
            )
            ao = own[:, lanes]
            ar = acc[:, lanes]
            now = jnp.maximum(across + ao * co + ar * cr, 0.0) * scale
            nb = now.astype(bf16)
            if it == ITERS - 1:
                merged[:, lanes] = jnp.where(live, now, 0.0).astype(bf16)
            down = down + dot(nb, part)
            pa = ao * now
            pr = ar * now
            ps = now * now
            for q in range(step // CH):
                cut = slice(CH * q, CH * (q + 1))
                sa = sa + pa[:, cut]
                sr = sr + pr[:, cut]
                ss = ss + ps[:, cut]
        down = (
            down
            + c_own * jnp.sum(sa, axis=1, keepdims=True)
            + c_rem * jnp.sum(sr, axis=1, keepdims=True)
        )
        trace = jnp.maximum(down, 0.0) / (jnp.sum(ss, axis=1, keepdims=True) + epsilon * NPIX)
    tout = jnp.where(live, trace, 0.0).astype(bf16)
    mtrace[...] = tout
    j = iota((16, 5 * MP), 0)
    kk = iota((16, 5 * MP), 1)
    g, s = group_of(j)
    slot = kk & 15
    same = ((kk >> 4) == g) & (j < 15) & (slot < total)
    comp = NBR * wide[1:2, :] + wide[2:3, :] - s

    def pick(d):
        return hot(same & (comp == 3 * d))

    ones = jnp.ones((MP, CH), bf16)
    blank = jnp.zeros((MP, CH), bf16)
    tail = jnp.concatenate([tout, ones, blank], axis=1)
    send_all(pick, merged, tail, tail, (xa, xb, va, vb), sy, sx)


def corr_kernel(comp, tr, rxa, rxb, rya, ryb, out):
    _, _, sy, sx = sides()
    k = iota((BORDER, 16), 0)
    j = iota((BORDER, 16), 1)
    s = j - 12
    fits = (s >= 0) & (s < 3)
    z = jnp.zeros((BORDER, F), f32)
    for t, ref in enumerate((rxa, rxb)):
        at = 2 * CW + 512
        z = z + dot(hot(fits & (k == 3 * direction(0, sx[t]) + s)), ref[:, at : at + F])
    for u, ref in enumerate((rya, ryb)):
        for q, dx in enumerate((0, sx[0], sx[1])):
            z = z + dot(hot(fits & (k == 3 * direction(sy[u], dx) + s)), ref[:, CW * q : CW * q + F])
    x = tr[...].astype(f32)
    x = x - jnp.mean(x, axis=1, keepdims=True)
    z = z - jnp.mean(z, axis=1, keepdims=True)
    nt = (((1,), (1,)), ((), ()))
    cov = lax.dot_general(x, z, nt, precision=lax.Precision.HIGHEST, preferred_element_type=f32) / F
    vx = jnp.mean(x * x, axis=1, keepdims=True)
    vz = lax.dot_general(
        jnp.ones((8, F), f32), z * z, nt, precision=lax.Precision.HIGHEST, preferred_element_type=f32
    )[0:1] / F
    alive = iota((K, 1), 0) < comp[0, 0]
    out[...] = jnp.where(alive, cov / jnp.sqrt((vx + epsilon) * (vz + epsilon)), 0.0)


def final_kernel(
    rows, cols, count, compc, row_ref, col_ref, foot, tr, wide, merged, mtrace, rxa, rxb, rya, ryb,
    nfoot, ntrace, acc, pbuf,
):
    row, col, sy, sx = sides()
    n = 32
    j5 = iota((5 * n, 16), 1)
    r5 = iota((5 * n, 16), 0)
    s5 = j5 - 3 * (r5 >> 5)
    k5 = r5 & 31
    fits = (s5 >= 0) & (s5 < 3)

    def select(d):
        return hot(fits & (k5 == 3 * d + s5))

    tail = receive(
        select, n, (rxa, rxb), (rya, ryb), acc, pbuf, row, col, sy, sx, row_ref, col_ref, rows, cols
    )
    flag = tail[0:BORDER, CH : CH + 1] > 0.5
    k = iota((BORDER, 1), 0)
    up = k < 9
    down = k >= 15
    left = (k < 3) | ((k >= 9) & (k < 12)) | ((k >= 15) & (k < 18))
    right = ((k >= 6) & (k < 9)) | ((k >= 12) & (k < 15)) | (k >= 21)
    _, _, r_up, _ = pixel_shift(-1, 0, row, col, row_ref, col_ref, rows, cols)
    _, _, r_dn, _ = pixel_shift(1, 0, row, col, row_ref, col_ref, rows, cols)
    _, _, _, c_lf = pixel_shift(0, -1, row, col, row_ref, col_ref, rows, cols)
    _, _, _, c_rt = pixel_shift(0, 1, row, col, row_ref, col_ref, rows, cols)
    y_lo = jnp.where(down, PH - r_dn, 0)
    y_hi = jnp.where(flag, jnp.where(up, r_up, PH), 0)
    x_lo = jnp.where(right, PW - c_rt, 0)
    x_hi = jnp.where(left, c_lf, PW)
    total = count[0, 0]
    own_id = wide[0:1, 0:MP]
    own_mask = (iota((K - BORDER, MP), 0) + BORDER == own_id) & (iota((K - BORDER, MP), 1) < total)
    own_hot = hot(own_mask)
    hit = jnp.sum(own_hot.astype(f32), axis=1, keepdims=True) > 0.5
    alive = iota((K - BORDER, 1), 0) + BORDER < compc[0, 0]
    step = 512
    for b in range(NPIX // step):
        lanes = slice(step * b, step * (b + 1))
        pix = iota((1, step), 1) + step * b
        y = pix >> 6
        x = pix & (PW - 1)
        mine = foot[:, lanes].astype(f32)
        inside = (y >= y_lo) & (y < y_hi) & (x >= x_lo) & (x < x_hi)
        top = jnp.where(inside, acc[0:BORDER, lanes], mine[0:BORDER])
        got = dot(own_hot, merged[:, lanes])
        low = jnp.where(alive, jnp.where(hit, got, mine[BORDER:]), 0.0)
        nfoot[:, lanes] = jnp.concatenate([top, low], axis=0).astype(bf16)
    mine = tr[...].astype(f32)
    top = jnp.where(flag, tail[0:BORDER, 0:F], mine[0:BORDER])
    low = jnp.where(alive, jnp.where(hit, dot(own_hot, mtrace[...]), mine[BORDER:]), 0.0)
    ntrace[...] = jnp.concatenate([top, low], axis=0).astype(bf16)


SMEM = pl.BlockSpec(memory_space=pltpu.SMEM)
VMEM = pl.BlockSpec(memory_space=pltpu.VMEM)
LIMIT = 24 * 1024 * 1024


def shape(*dims, dtype=bf16):
    return jax.ShapeDtypeStruct(dims, dtype)


PACKETS = (shape(16, XW), shape(16, XW), shape(16, CW), shape(16, CW))


def call(kernel, outs, scalars, arrays, scratch, flops, name):
    return pl.pallas_call(
        kernel,
        out_shape=outs,
        in_specs=[SMEM] * scalars + [VMEM] * arrays,
        out_specs=jax.tree.map(lambda _: VMEM, outs),
        scratch_shapes=scratch,
        compiler_params=pltpu.CompilerParams(vmem_limit_bytes=LIMIT),
        cost_estimate=pl.CostEstimate(flops=flops, bytes_accessed=1 << 20, transcendentals=0),
        name=name,
    )


def swap(value, axis, parity):
    count = lax.axis_size(axis)
    pairs = []
    for i in range(parity, count - 1, 2):
        pairs += [(i, i + 1), (i + 1, i)]
    return lax.ppermute(value, axis, pairs)


def exchange(xa, xb, va, vb):
    rxb = swap(xb, "px", 1)
    rxa = swap(xa, "px", 0)
    yb = jnp.concatenate([vb, rxa[:, CW : 2 * CW], rxb[:, CW : 2 * CW]], axis=1)
    ya = jnp.concatenate([va, rxa[:, 0:CW], rxb[:, 0:CW]], axis=1)
    ryb = swap(yb, "py", 1)
    rya = swap(ya, "py", 0)
    return rxa, rxb, rya, ryb


def shards(
    residual, footprints, traces, merge_pairs, pair_counts, comp_counts, row_inter, col_inter
):
    res = residual[0, 0]
    foot = footprints[0, 0]
    tr = traces[0, 0]
    table = merge_pairs[0, 0]
    wide = jnp.tile(table.T, (1, 5))
    rows, cols = lax.axis_size("py"), lax.axis_size("px")

    packets = call(
        pack_kernel, PACKETS, 0, 2, [pltpu.VMEM((32, NPIX), bf16)], 1 << 24, "pack"
    )(foot, tr)
    got = exchange(*packets)

    def refit(*refs):
        refit_kernel(rows, cols, *refs)

    xa, xb, va, vb, merged, mtrace = call(
        refit,
        PACKETS + (shape(MP, NPIX), shape(MP, F)),
        3,
        9,
        [
            pltpu.VMEM((MP, NPIX), f32),
            pltpu.VMEM((MP, NPIX), f32),
            pltpu.VMEM((6, MP, PBW), bf16),
        ],
        1 << 28,
        "refit",
    )(pair_counts, row_inter, col_inter, res, foot, tr, table, wide, *got)
    back = exchange(xa, xb, va, vb)

    corr = call(corr_kernel, shape(K, BORDER, dtype=f32), 1, 5, [], 1 << 22, "corr")(
        comp_counts, tr, *got
    )

    def final(*refs):
        final_kernel(rows, cols, *refs)

    nfoot, ntrace = call(
        final,
        (shape(K, NPIX), shape(K, F)),
        4,
        9,
        [pltpu.VMEM((32, NPIX), f32), pltpu.VMEM((6, 32, PBW), bf16)],
        1 << 26,
        "final",
    )(pair_counts, comp_counts, row_inter, col_inter, foot, tr, wide, merged, mtrace, *back)
    return nfoot[None, None], ntrace[None, None], corr[None, None]


def solution(mesh):
    in_specs = (
        P("py", "px", None, None),
        P("py", "px", None, None),
        P("py", "px", None, None),
        P("py", "px", None, None),
        P("py", "px"),
        P("py", "px"),
        P(),
        P(),
    )
    out_specs = (P("py", "px", None, None), P("py", "px", None, None), P("py", "px", None, None))
    return jax.shard_map(shards, mesh=mesh, in_specs=in_specs, out_specs=out_specs, check_vma=False)
```

time: 85.1 us -> 64.7 us (0.76)
  waiting for transfers between devices: 28.3 us -> 6.43 us
  Pallas kernels: 0 us -> 10.7 us
  starting transfers between devices: 32.2 us -> 41.1 us
  matrix products: 7.1 us -> 0 us
  local copies, waits for them, and re-layouts: 10.3 us -> 3.93 us
  other arithmetic: 4.46 us -> 0.02 us
    ppermute x8, waiting for transfers between devices: 28.3 us -> 6.43 us  [swap(): return lax.ppermute(value, axis, pairs)]
    pallas_call x0 -> x4, Pallas kernels: none -> 10.7 us  [the longest x1 7.08 us: shards(): call(refit, PACKETS + (shape(MP, NPIX), shape(MP, F)), 3, 9, [pltpu.VMEM(...]
    ppermute x8, starting transfers between devices: 32.2 us -> 41.1 us  [swap(): return lax.ppermute(value, axis, pairs)]
    dot_general x16 -> x0, matrix products: 7.1 us -> none  [the longest x3 1.67 us: refit_pairs(): lax.dot_general(trace_now.astype(jnp.bfloat16), residue, (((1,), (1,)), (...]
    concatenate x4 -> x0, local copies, waits for them, and re-layouts: 4.27 us -> none  [the longest x2 4.26 us: direct_pieces(): return jnp.concatenate(pieces, axis=0)]
    unnamed x13 -> x18, local copies, waits for them, and re-layouts: 1.34 us -> 3.75 us
    gather x3 -> x0, local copies, waits for them, and re-layouts: 1.85 us -> none  [the longest x1 0.64 us: refit_pairs(): remote = jnp.take(border, border_index, axis=0)]
    select_n x5 -> x0, other arithmetic: 1.74 us -> none  [the longest x1 0.85 us: shards(): jnp.where(alive[:, None], jnp.concatenate([reserved_foot, new_foot[BORDER...]
  transfers between devices with their start and end apart: 8 -> 8, of which waited for: 6 -> 3; matrix products, arithmetic and copies ran while one was open for 5% -> 1% of each run, Pallas kernels for 0% -> 1%
where the time goes in v1:
time: 64.7 us; the launch traced here: 64.2 us
  starting transfers between devices  41.1 us (64%)
  Pallas kernels  10.7 us (17%)
  waiting for transfers between devices  6.43 us (10%)
  local copies, waits for them, and re-layouts  3.93 us (6%)
  between operations  2.09 us (3%)
    ppermute x8, starting transfers between devices, swap(): return lax.ppermute(value, axis, pairs)  41.1 us
    pallas_call x1, Pallas kernels, shards(): call(refit, PACKETS + (shape(MP, NPIX), shape(MP, F)), 3, 9, [pltpu.VMEM(...  7.08 us
    ppermute x8, waiting for transfers between devices, swap(): return lax.ppermute(value, axis, pairs)  6.43 us
    unnamed x18, local copies, waits for them, and re-layouts  3.75 us
    pallas_call x1, Pallas kernels, shards(): call(final, (shape(K, NPIX), shape(K, F)), 4, 9, [pltpu.VMEM((32, NPIX),...  2.84 us
  transfers between devices with their start and end apart: 8, of which 3 were waited for; matrix products, arithmetic and copies ran while one was open for 1% of the time, Pallas kernels for 1%

profile of v1, /device:TPU:57, one launch (start us, length us, event | category | flops | bytes accessed | tf_op | source)
XLA Modules:
  0.0 64.2 jit_solution(2820701409418461590)
XLA Ops:
  0.6 0.0 copy-start
  0.6 1.0 %copy-done = bf16[1,1,40,4096]{3,2,1,0:T(8,128)(2,1)S(1)} copy-done((bf16[1,1,40,4096]{3,2,1,0:T(8,128)(2,1)S(1)}, bf16[1,1,40,4096]{3,2,1,0:T(8,128)(2,1)}, u32[]{:S(2)}) %copy-start) | copy-done | bytes 327704
  1.6 0.0 copy-start.3
  1.6 0.7 %copy-done.3 = bf16[1,1,40,128]{3,2,1,0:T(8,128)(2,1)S(1)} copy-done((bf16[1,1,40,128]{3,2,1,0:T(8,128)(2,1)S(1)}, bf16[1,1,40,128]{3,2,1,0:T(8,128)(2,1)}, u32[]{:S(2)}) %copy-start.3) | copy-done | bytes 10264
  2.3 0.0 copy-start.1
  2.3 0.3 pack.1
  2.6 2.6 %collective-permute-start = (bf16[16,1664]{1,0:T(8,128)(2,1)S(1)}, bf16[16,1664]{1,0:T(8,128)(2,1)S(1)}, u32[]{:S(2)}, u32[]{:S(2)}) collective-permute-start(bf16[16,1664]{1,0:T(8,128)(2,1)S(1)} %get-tuple-element.15), channel_id=1, source_target_pairs={{0,1},{1,0},{2,3},{3,2},{4,5},{5,4},{6,7},{7,6},{8,9},{9,8},{10,11... | collective-permute-start | bytes 159752 | tf_op jit(solution)/shard_map/ppermute | solution.py:379
  5.2 5.4 %collective-permute-start.1 = (bf16[16,1664]{1,0:T(8,128)(2,1)S(1)}, bf16[16,1664]{1,0:T(8,128)(2,1)S(1)}, u32[]{:S(2)}, u32[]{:S(2)}) collective-permute-start(bf16[16,1664]{1,0:T(8,128)(2,1)S(1)} %get-tuple-element.16), channel_id=1, source_target_pairs={{1,2},{2,1},{3,4},{4,3},{5,6},{6,5},{7,8},{8,7},{9,10},{10,9},{11,... | collective-permute-start | bytes 159752 | tf_op jit(solution)/shard_map/ppermute | solution.py:379
  10.6 0.0 collective-permute-done.refs_8_.rxa
  10.6 2.7 %collective-permute-done.1.refs_9_.rxb = bf16[16,1664]{1,0:T(8,128)(2,1)S(1)} collective-permute-done((bf16[16,1664]{1,0:T(8,128)(2,1)S(1)}, bf16[16,1664]{1,0:T(8,128)(2,1)S(1)}, u32[]{:S(2)}, u32[]{:S(2)}) %collective-permute-start.1) | collective-permute-done | bytes 53280 | tf_op jit(solution)/shard_map/ppermute | solution.py:379
  13.4 4.0 %collective-permute-start.2 = (bf16[16,1152]{1,0:T(8,128)(2,1)S(1)}, bf16[16,1152]{1,0:T(8,128)(2,1)S(1)}, u32[]{:S(2)}, u32[]{:S(2)}) collective-permute-start(bf16[16,1152]{1,0:T(8,128)(2,1)S(1)} %pad_maximum_fusion), channel_id=1, source_target_pairs={{0,32},{32,0},{64,96},{96,64},{128,160},{160,128},{192,224},{224,1... | collective-permute-start | bytes 110600 | tf_op jit(solution)/shard_map/ppermute | solution.py:379
  17.4 0.0 copy-start.7
  17.4 11.1 %collective-permute-start.3 = (bf16[16,1152]{1,0:T(8,128)(2,1)S(1)}, bf16[16,1152]{1,0:T(8,128)(2,1)S(1)}, u32[]{:S(2)}, u32[]{:S(2)}) collective-permute-start(bf16[16,1152]{1,0:T(8,128)(2,1)S(1)} %pad_maximum_fusion.1), channel_id=1, source_target_pairs={{32,64},{64,32},{96,128},{128,96},{160,192},{192,160},{224,256},{2... | collective-permute-start | bytes 110600 | tf_op jit(solution)/shard_map/ppermute | solution.py:379
  29.2 0.0 copy-done.7
  29.2 0.1 copy.13.refs_6_
  29.3 0.0 copy-start.4
  29.3 0.1 tile.10.refs_7_.refs_6_
  29.4 0.0 copy-start.5
  29.4 0.0 copy-start.6
  29.4 0.0 collective-permute-done.2.refs_10_.rya
  29.4 0.5 collective-permute-done.3.refs_11_.ryb
  29.9 0.0 copy-done.1
  29.9 0.1 copy-done.4
  30.0 0.0 copy-done.5
  30.0 0.0 copy-done.6
  30.0 0.0 copy-start.2
  30.0 1.2 %copy-done.2 = bf16[1,1,4096,128]{3,2,1,0:T(8,128)(2,1)S(1)} copy-done((bf16[1,1,4096,128]{3,2,1,0:T(8,128)(2,1)S(1)}, bf16[1,1,4096,128]{3,2,1,0:T(8,128)(2,1)}, u32[]{:S(2)}) %copy-start.2) | copy-done | bytes 1048600
  31.3 7.1 %refit.1 = (bf16[16,1664]{1,0:T(8,128)(2,1)S(1)}, bf16[16,1664]{1,0:T(8,128)(2,1)S(1)}, bf16[16,384]{1,0:T(8,128)(2,1)S(1)}, bf16[16,384]{1,0:T(8,128)(2,1)S(1)}...) custom-call(s32[1,1]{1,0:T(1,128)S(6)} %copy.19.refs_0_, s32[15]{0:T(128)S(1)} %copy-done.5, s32[31]{0:T(128)S(1)} %copy-done.6, ...), custom_call_target="tpu_custom_call" | custom-call | flops 268435456 | bytes 1048576 | tf_op jit(solution)/shard_map/refit/pallas_call | solution.py:410
  38.3 1.9 %collective-permute-start.4 = (bf16[16,1664]{1,0:T(8,128)(2,1)S(1)}, bf16[16,1664]{1,0:T(8,128)(2,1)S(1)}, u32[]{:S(2)}, u32[]{:S(2)}) collective-permute-start(bf16[16,1664]{1,0:T(8,128)(2,1)S(1)} %get-tuple-element.21), channel_id=1, source_target_pairs={{0,1},{1,0},{2,3},{3,2},{4,5},{5,4},{6,7},{7,6},{8,9},{9,8},{10,11... | collective-permute-start | bytes 159752 | tf_op jit(solution)/shard_map/ppermute | solution.py:379
  40.3 4.9 %collective-permute-start.5 = (bf16[16,1664]{1,0:T(8,128)(2,1)S(1)}, bf16[16,1664]{1,0:T(8,128)(2,1)S(1)}, u32[]{:S(2)}, u32[]{:S(2)}) collective-permute-start(bf16[16,1664]{1,0:T(8,128)(2,1)S(1)} %get-tuple-element.22), channel_id=1, source_target_pairs={{1,2},{2,1},{3,4},{4,3},{5,6},{6,5},{7,8},{8,7},{9,10},{10,9},{11,... | collective-permute-start | bytes 159752 | tf_op jit(solution)/shard_map/ppermute | solution.py:379
  45.2 0.0 collective-permute-done.4.refs_9_
  45.2 3.2 %collective-permute-done.5.refs_10_ = bf16[16,1664]{1,0:T(8,128)(2,1)S(1)} collective-permute-done((bf16[16,1664]{1,0:T(8,128)(2,1)S(1)}, bf16[16,1664]{1,0:T(8,128)(2,1)S(1)}, u32[]{:S(2)}, u32[]{:S(2)}) %collective-permute-start.5) | collective-permute-done | bytes 53280 | tf_op jit(solution)/shard_map/ppermute | solution.py:379
  48.4 1.9 %collective-permute-start.6 = (bf16[16,1152]{1,0:T(8,128)(2,1)S(1)}, bf16[16,1152]{1,0:T(8,128)(2,1)S(1)}, u32[]{:S(2)}, u32[]{:S(2)}) collective-permute-start(bf16[16,1152]{1,0:T(8,128)(2,1)S(1)} %pad_maximum_fusion.2), channel_id=1, source_target_pairs={{0,32},{32,0},{64,96},{96,64},{128,160},{160,128},{192,224},{224,1... | collective-permute-start | bytes 110600 | tf_op jit(solution)/shard_map/ppermute | solution.py:379
  50.4 9.2 %collective-permute-start.7 = (bf16[16,1152]{1,0:T(8,128)(2,1)S(1)}, bf16[16,1152]{1,0:T(8,128)(2,1)S(1)}, u32[]{:S(2)}, u32[]{:S(2)}) collective-permute-start(bf16[16,1152]{1,0:T(8,128)(2,1)S(1)} %pad_maximum_fusion.3), channel_id=1, source_target_pairs={{32,64},{64,32},{96,128},{128,96},{160,192},{192,160},{224,256},{2... | collective-permute-start | bytes 110600 | tf_op jit(solution)/shard_map/ppermute | solution.py:379
  60.3 0.4 corr.1
  60.7 0.7 %copy.14 = f32[1,1,40,24]{2,3,1,0:T(8,128)} copy(f32[1,1,40,24]{3,2,1,0:T(8,128)S(1)} %bitcast.20) | data formatting | bytes 7680
  61.4 0.0 collective-permute-done.6.refs_11_
  61.4 0.0 collective-permute-done.7.refs_12_
  61.4 2.8 %final.1 = (bf16[40,4096]{1,0:T(8,128)(2,1)}, bf16[40,128]{1,0:T(8,128)(2,1)}) custom-call(s32[1,1]{1,0:T(1,128)S(6)} %copy.19.refs_0_, s32[1,1]{1,0:T(1,128)S(6)} %copy.20.refs_1_.comp, s32[15]{0:T(128)S(1)} %copy-done.5, s32[31]{0:T(128)S(1)} %copy-done.6, bf16[40,4096]{1,0:T(8,128)(2,1)S(1)} %bitcast.14, bf16[40,128]{1,0:T(8,128)(2,1)S(1)} %bitcast.19, ...), custom_call_target="tpu_custom_call" | custom-call | flops 67108864 | bytes 1048576 | tf_op jit(solution)/shard_map/final/pallas_call | solution.py:432
  (10 shorter events, 0.0 us)
Async XLA Ops:
  0.6 1.0 %copy-start = (bf16[1,1,40,4096]{3,2,1,0:T(8,128)(2,1)S(1)}, bf16[1,1,40,4096]{3,2,1,0:T(8,128)(2,1)}, u32[]{:S(2)}) copy-start(bf16[1,1,40,4096]{3,2,1,0:T(8,128)(2,1)} %param.9) | copy-start | bytes 983044
  1.6 0.7 %copy-start.3 = (bf16[1,1,40,128]{3,2,1,0:T(8,128)(2,1)S(1)}, bf16[1,1,40,128]{3,2,1,0:T(8,128)(2,1)}, u32[]{:S(2)}) copy-start(bf16[1,1,40,128]{3,2,1,0:T(8,128)(2,1)} %param.10) | copy-start | bytes 30724
  2.3 27.5 %copy-start.1 = (bf16[1,1,40,4096]{3,2,1,0:T(8,128)(2,1)S(1)}, bf16[1,1,40,4096]{3,2,1,0:T(8,128)(2,1)}, u32[]{:S(2)}) copy-start(bf16[1,1,40,4096]{3,2,1,0:T(8,128)(2,1)} %param.9) | copy-start | bytes 983044
  2.6 8.0 %collective-permute-start = (bf16[16,1664]{1,0:T(8,128)(2,1)S(1)}, bf16[16,1664]{1,0:T(8,128)(2,1)S(1)}, u32[]{:S(2)}, u32[]{:S(2)}) collective-permute-start(bf16[16,1664]{1,0:T(8,128)(2,1)S(1)} %get-tuple-element.15), channel_id=1, source_target_pairs={{0,1},{1,0},{2,3},{3,2},{4,5},{5,4},{6,7},{7,6},{8,9},{9,8},{10,11... | collective-permute-start | bytes 159752 | tf_op jit(solution)/shard_map/ppermute | solution.py:379
  5.2 8.2 %collective-permute-start.1 = (bf16[16,1664]{1,0:T(8,128)(2,1)S(1)}, bf16[16,1664]{1,0:T(8,128)(2,1)S(1)}, u32[]{:S(2)}, u32[]{:S(2)}) collective-permute-start(bf16[16,1664]{1,0:T(8,128)(2,1)S(1)} %get-tuple-element.16), channel_id=1, source_target_pairs={{1,2},{2,1},{3,4},{4,3},{5,6},{6,5},{7,8},{8,7},{9,10},{10,9},{11,... | collective-permute-start | bytes 159752 | tf_op jit(solution)/shard_map/ppermute | solution.py:379
  13.4 16.0 %collective-permute-start.2 = (bf16[16,1152]{1,0:T(8,128)(2,1)S(1)}, bf16[16,1152]{1,0:T(8,128)(2,1)S(1)}, u32[]{:S(2)}, u32[]{:S(2)}) collective-permute-start(bf16[16,1152]{1,0:T(8,128)(2,1)S(1)} %pad_maximum_fusion), channel_id=1, source_target_pairs={{0,32},{32,0},{64,96},{96,64},{128,160},{160,128},{192,224},{224,1... | collective-permute-start | bytes 110600 | tf_op jit(solution)/shard_map/ppermute | solution.py:379
  17.4 11.8 %copy-start.7 = (s32[1,1,16,3]{2,1,3,0:T(1,128)S(1)}, s32[1,1,16,3]{2,1,3,0:T(1,128)}, u32[]{:S(2)}) copy-start(s32[1,1,16,3]{2,1,3,0:T(1,128)} %param.11) | copy-start | bytes 580
  17.4 12.4 %collective-permute-start.3 = (bf16[16,1152]{1,0:T(8,128)(2,1)S(1)}, bf16[16,1152]{1,0:T(8,128)(2,1)S(1)}, u32[]{:S(2)}, u32[]{:S(2)}) collective-permute-start(bf16[16,1152]{1,0:T(8,128)(2,1)S(1)} %pad_maximum_fusion.1), channel_id=1, source_target_pairs={{32,64},{64,32},{96,128},{128,96},{160,192},{192,160},{224,256},{2... | collective-permute-start | bytes 110600 | tf_op jit(solution)/shard_map/ppermute | solution.py:379
  29.3 0.7 %copy-start.4 = (bf16[1,1,40,128]{3,2,1,0:T(8,128)(2,1)S(1)}, bf16[1,1,40,128]{3,2,1,0:T(8,128)(2,1)}, u32[]{:S(2)}) copy-start(bf16[1,1,40,128]{3,2,1,0:T(8,128)(2,1)} %param.10) | copy-start | bytes 30724
  29.4 0.7 %copy-start.5 = (s32[15]{0:T(128)S(1)}, s32[15]{0:T(128)}, u32[]{:S(2)}) copy-start(s32[15]{0:T(128)} %refs_2_.3) | copy-start | bytes 184
  29.4 0.7 %copy-start.6 = (s32[31]{0:T(128)S(1)}, s32[31]{0:T(128)}, u32[]{:S(2)}) copy-start(s32[31]{0:T(128)} %refs_3_.1) | copy-start | bytes 376
  30.0 1.2 %copy-start.2 = (bf16[1,1,4096,128]{3,2,1,0:T(8,128)(2,1)S(1)}, bf16[1,1,4096,128]{3,2,1,0:T(8,128)(2,1)}, u32[]{:S(2)}) copy-start(bf16[1,1,4096,128]{3,2,1,0:T(8,128)(2,1)} %param.8) | copy-start | bytes 3145732
  38.3 6.9 %collective-permute-start.4 = (bf16[16,1664]{1,0:T(8,128)(2,1)S(1)}, bf16[16,1664]{1,0:T(8,128)(2,1)S(1)}, u32[]{:S(2)}, u32[]{:S(2)}) collective-permute-start(bf16[16,1664]{1,0:T(8,128)(2,1)S(1)} %get-tuple-element.21), channel_id=1, source_target_pairs={{0,1},{1,0},{2,3},{3,2},{4,5},{5,4},{6,7},{7,6},{8,9},{9,8},{10,11... | collective-permute-start | bytes 159752 | tf_op jit(solution)/shard_map/ppermute | solution.py:379
  40.3 8.2 %collective-permute-start.5 = (bf16[16,1664]{1,0:T(8,128)(2,1)S(1)}, bf16[16,1664]{1,0:T(8,128)(2,1)S(1)}, u32[]{:S(2)}, u32[]{:S(2)}) collective-permute-start(bf16[16,1664]{1,0:T(8,128)(2,1)S(1)} %get-tuple-element.22), channel_id=1, source_target_pairs={{1,2},{2,1},{3,4},{4,3},{5,6},{6,5},{7,8},{8,7},{9,10},{10,9},{11,... | collective-permute-start | bytes 159752 | tf_op jit(solution)/shard_map/ppermute | solution.py:379
  48.4 13.0 %collective-permute-start.6 = (bf16[16,1152]{1,0:T(8,128)(2,1)S(1)}, bf16[16,1152]{1,0:T(8,128)(2,1)S(1)}, u32[]{:S(2)}, u32[]{:S(2)}) collective-permute-start(bf16[16,1152]{1,0:T(8,128)(2,1)S(1)} %pad_maximum_fusion.2), channel_id=1, source_target_pairs={{0,32},{32,0},{64,96},{96,64},{128,160},{160,128},{192,224},{224,1... | collective-permute-start | bytes 110600 | tf_op jit(solution)/shard_map/ppermute | solution.py:379
  50.4 11.0 %collective-permute-start.7 = (bf16[16,1152]{1,0:T(8,128)(2,1)S(1)}, bf16[16,1152]{1,0:T(8,128)(2,1)S(1)}, u32[]{:S(2)}, u32[]{:S(2)}) collective-permute-start(bf16[16,1152]{1,0:T(8,128)(2,1)S(1)} %pad_maximum_fusion.3), channel_id=1, source_target_pairs={{32,64},{64,32},{96,128},{128,96},{160,192},{192,160},{224,256},{2... | collective-permute-start | bytes 110600 | tf_op jit(solution)/shard_map/ppermute | solution.py:379

commit v2 on v1

v2 whole, which is shorter than its diff:
```python
import jax
import jax.numpy as jnp
from jax import lax
from jax.experimental import pallas as pl
from jax.experimental.pallas import tpu as pltpu
from jax.sharding import PartitionSpec as P


PH = 64
PW = 64
NPIX = PH * PW
K = 40
NBR = 3
BORDER = 24
MP = 16
F = 128
ITERS = 4
OV_HI = 24
epsilon = 1e-05

BAND = OV_HI * PW
LOW = NPIX - BAND
CW = BAND // 4
EW = 896
XW = 2 * CW + EW
CH = 128
PAD = 9
PBW = (PAD + 12 + PAD) * CH

f32 = jnp.float32
bf16 = jnp.bfloat16


def iota(shape, dim):
    return lax.broadcasted_iota(jnp.int32, shape, dim)


def sides():
    row = lax.axis_index("py")
    col = lax.axis_index("px")
    sy = 1 - 2 * lax.rem(row, 2)
    sx = 1 - 2 * lax.rem(col, 2)
    return row, col, (sy, -sy), (sx, -sx)


def direction(dy, dx):
    flat = (dy + 1) * 3 + dx + 1
    return flat - (flat > 4).astype(jnp.int32) if not isinstance(flat, int) else flat - (flat > 4)


def hot(mask):
    return jnp.where(mask, 1.0, 0.0).astype(bf16)


def dot(a, b):
    return jnp.dot(a, b, preferred_element_type=f32)


def band_start(dy):
    return jnp.where(dy > 0, LOW, 0)


def pack_rows(pick, pieces, tail):
    return dot(pick, jnp.concatenate(pieces + [tail], axis=0)).astype(bf16)


def pixel_shift(dy, dx, row, col, row_ref, col_ref, rows, cols):
    ri = row_ref[jnp.clip(row + jnp.minimum(dy, 0), 0, rows - 2)]
    ci = col_ref[jnp.clip(col + jnp.minimum(dx, 0), 0, cols - 2)]
    return dy * (OV_HI - ri), dx * (PW - ci), ri, ci


def column_matrix(ox):
    i = iota((CH, CH), 0)
    o = iota((CH, CH), 1)
    x = (o & (PW - 1)) - ox
    return hot((i == o - ox) & (x >= 0) & (x < PW))


def band_matrix(odd, ox):
    i = iota((2 * CH, CH), 0)
    o = iota((2 * CH, CH), 1)
    x = (o & (PW - 1)) - ox
    return hot((i == o + CH - PW * odd - ox) & (x >= 0) & (x < PW))


def place_whole(whole, ox):
    stack = jnp.concatenate(
        [whole[:, CH * m : CH * (m + 1)] for m in range(32)], axis=0
    ).astype(bf16)
    return dot(stack, column_matrix(ox))


def receive_sides(select, n, xs, row, col, sx, row_ref, col_ref, rows, cols):
    tail = jnp.zeros((n, 2 * CH), f32)
    whole = None
    for t in range(2):
        picked = dot(select(direction(0, sx[t])), xs[t][:, 2 * CW : XW])
        full = jnp.concatenate(
            [picked[n * g : n * (g + 1)] for g in range(4)] + [picked[4 * n :, 0:512]], axis=1
        )
        tail = tail + picked[4 * n :, 512 : 512 + 2 * CH]
        _, ox, _, _ = pixel_shift(0, sx[t], row, col, row_ref, col_ref, rows, cols)
        moved = place_whole(full, ox)
        whole = moved if whole is None else whole + moved
    return whole, tail


def clear_pads(pbuf):
    pbuf[:, :, 0 : PAD * CH] = jnp.zeros(pbuf.shape[:2] + (PAD * CH,), bf16)
    pbuf[:, :, PAD * CH + BAND :] = jnp.zeros(pbuf.shape[:2] + (PBW - PAD * CH - BAND,), bf16)


def receive_bands(selects, n, ys, pbuf, row, col, sy, sx, row_ref, col_ref, rows, cols, ready):
    steps = (0, sx[0], sx[1])
    picked = [
        [
            dot(selects[u](direction(sy[u], dx)), ys[u][:, CW * j : CW * (j + 1)])
            for j, dx in enumerate(steps)
        ]
        for u in range(2)
    ]
    ready()
    clear_pads(pbuf)
    for u in range(2):
        for j in range(3):
            for g in range(4):
                at = PAD * CH + CW * g
                pbuf[3 * u + j, :, at : at + CW] = picked[u][j][n * g : n * (g + 1)].astype(bf16)
    out = []
    for u in range(2):
        moved = None
        tail = jnp.zeros((n, 2 * CH), f32)
        for j, dx in enumerate(steps):
            shift, ox, _, _ = pixel_shift(sy[u], dx, row, col, row_ref, col_ref, rows, cols)
            first = (PAD - 1 - (shift >> 1)) * CH
            stack = jnp.concatenate(
                [
                    pbuf[3 * u + j, :, pl.ds(pl.multiple_of(first + CH * m, CH), 2 * CH)]
                    for m in range(12)
                ],
                axis=0,
            )
            one = dot(stack, band_matrix(shift & 1, ox))
            moved = one if moved is None else moved + one
            tail = tail + picked[u][j][4 * n :, 0 : 2 * CH]
        out.append((moved, tail))
    return out


def fetch(row_in, col_in, row_ref, col_ref, sem):
    loads = (
        pltpu.make_async_copy(row_in, row_ref, sem.at[0]),
        pltpu.make_async_copy(col_in, col_ref, sem.at[1]),
    )
    for load in loads:
        load.start()

    def ready():
        for load in loads:
            load.wait()

    return ready


def send_all(pick, src, tail_narrow, tail_wide, outs, sy, sx):
    xa, xb, va, vb = outs

    def band_seg(dy, dx):
        start = band_start(dy)
        pieces = [
            src[:, pl.ds(pl.multiple_of(start + CW * g, CH), CW)] for g in range(4)
        ]
        return pack_rows(pick(direction(dy, dx)), pieces, tail_narrow)

    def whole_seg(dx):
        pieces = [src[:, EW * g : EW * (g + 1)] for g in range(4)]
        last = jnp.concatenate([src[:, 4 * EW : NPIX], tail_wide], axis=1)
        return pack_rows(pick(direction(0, dx)), pieces, last)

    for t, out in enumerate((xa, xb)):
        out[:, 0:CW] = band_seg(sy[0], sx[t])
        out[:, CW : 2 * CW] = band_seg(sy[1], sx[t])
        out[:, 2 * CW : XW] = whole_seg(sx[t])
    va[...] = band_seg(sy[0], 0)
    vb[...] = band_seg(sy[1], 0)


def group_of(j):
    g = (j >= 3).astype(jnp.int32) + (j >= 6) + (j >= 9) + (j >= 12)
    return g, j - 3 * g


def pack_kernel(foot, tail, xa, xb, va, vb):
    _, _, sy, sx = sides()
    j = iota((16, 160), 0)
    kk = iota((16, 160), 1)
    g, s = group_of(j)
    same = ((kk >> 5) == g) & (j < 15)
    comp = (kk & 31) - s

    def pick(d):
        return hot(same & (comp == 3 * d))

    last = tail[...]
    send_all(pick, foot.at[0:32, :], last, last, (xa, xb, va, vb), sy, sx)


def slot_masks(table, total):
    own = table[:, 0:1]
    idx = NBR * table[:, 1:2] + table[:, 2:3]
    live = iota((MP, 1), 0) < total
    return own, idx, live


def slot_select(table, total):
    ids, idx, live = slot_masks(table, total)
    j5 = iota((5 * MP, 16), 1)
    g5 = iota((5 * MP, 16), 0) >> 4
    s5 = j5 - 3 * g5
    idx5 = jnp.concatenate([jnp.where(live, idx, -100)] * 5, axis=0)
    fits = (s5 >= 0) & (s5 < 3)

    def select(d):
        return hot(fits & (idx5 == 3 * d + s5))

    return ids, live, select


NT = (((1,), (1,)), ((), ()))


def own_kernel(count, res, foot, tr, table, rest, first, own, ctr):
    ids, _, _ = slot_masks(table, count[...])
    own_hot = hot(ids == iota((MP, K), 1))
    c_own = dot(own_hot, tr[...])
    ctr[...] = c_own
    eye = hot(iota((CH, CH), 0) == iota((CH, CH), 1))
    both = jnp.concatenate([c_own.astype(bf16), eye], axis=0)
    width = 512
    for n in range(NPIX // width):
        lanes = slice(width * n, width * (n + 1))
        own[:, lanes] = dot(own_hot, foot[:, lanes])
        turned = lax.dot_general(both, res[lanes, :], NT, preferred_element_type=f32)
        first[:, lanes] = turned[0:MP]
        rest[:, lanes] = turned[MP:].astype(bf16)


def side_kernel(rows, cols, row_ref, col_ref, count, table, rxa, rxb, side, crem):
    row, col, _, sx = sides()
    _, _, select = slot_select(table, count[...])
    whole, tail = receive_sides(
        select, MP, (rxa, rxb), row, col, sx, row_ref, col_ref, rows, cols
    )
    crem[...] = tail[:, 0:F]
    for m in range(32):
        side[:, CH * m : CH * (m + 1)] = whole[MP * m : MP * (m + 1)]


def refit_kernel(
    rows, cols, row_in, col_in, count, res, rest, first, own, ctr, side, crem, table, wide, rya, ryb,
    xa, xb, va, vb, merged, mtrace, acc, pbuf, row_ref, col_ref, sem,
):
    ready = fetch(row_in, col_in, row_ref, col_ref, sem)
    row, col, sy, sx = sides()
    total = count[...]
    _, live, select = slot_select(table, total)
    acc[...] = side[...]
    c_own = ctr[...]
    c_rem = crem[...]
    bands = receive_bands(
        (select, select), MP, (rya, ryb), pbuf, row, col, sy, sx, row_ref, col_ref, rows, cols, ready
    )
    for u, (moved, tail) in enumerate(bands):
        c_rem = c_rem + tail[:, 0:F]
        start = band_start(sy[u])
        for m in range(12):
            lanes = pl.ds(pl.multiple_of(start + CH * m, CH), CH)
            acc[:, lanes] += moved[MP * m : MP * (m + 1)]
    trace = c_own
    step = 512
    for it in range(ITERS):
        tb = trace.astype(bf16)
        co = jnp.sum(c_own * trace, axis=1, keepdims=True)
        cr = jnp.sum(c_rem * trace, axis=1, keepdims=True)
        scale = 1.0 / (jnp.sum(trace * trace, axis=1, keepdims=True) + epsilon * F)
        lanes = [slice(step * n, step * (n + 1)) for n in range(NPIX // step)]
        if it == 0:
            across = [first[:, cut] for cut in lanes]
        else:
            across = [dot(tb, rest[:, cut]) for cut in lanes]
        sa = jnp.zeros((MP, CH), f32)
        sr = jnp.zeros((MP, CH), f32)
        ss = jnp.zeros((MP, CH), f32)
        shapes = []
        for n, cut in enumerate(lanes):
            ao = own[:, cut]
            ar = acc[:, cut]
            now = jnp.maximum(across[n] + ao * co + ar * cr, 0.0) * scale
            shapes.append(now.astype(bf16))
            if it == ITERS - 1:
                merged[:, cut] = jnp.where(live, now, 0.0).astype(bf16)
            pa = ao * now
            pr = ar * now
            ps = now * now
            for q in range(step // CH):
                part = slice(CH * q, CH * (q + 1))
                sa = sa + pa[:, part]
                sr = sr + pr[:, part]
                ss = ss + ps[:, part]
        down = sum(dot(shapes[n], res[cut, :]) for n, cut in enumerate(lanes))
        down = (
            down
            + c_own * jnp.sum(sa, axis=1, keepdims=True)
            + c_rem * jnp.sum(sr, axis=1, keepdims=True)
        )
        trace = jnp.maximum(down, 0.0) / (jnp.sum(ss, axis=1, keepdims=True) + epsilon * NPIX)
    tout = jnp.where(live, trace, 0.0).astype(bf16)
    mtrace[...] = tout
    j = iota((16, 5 * MP), 0)
    kk = iota((16, 5 * MP), 1)
    g, s = group_of(j)
    slot = kk & 15
    same = ((kk >> 4) == g) & (j < 15) & (slot < total)
    comp = NBR * wide[1:2, :] + wide[2:3, :] - s

    def pick(d):
        return hot(same & (comp == 3 * d))

    ones = jnp.ones((MP, CH), bf16)
    blank = jnp.zeros((MP, CH), bf16)
    tail = jnp.concatenate([tout, ones, blank], axis=1)
    send_all(pick, merged, tail, tail, (xa, xb, va, vb), sy, sx)


def corr_kernel(comp, tr, rxa, rxb, rya, ryb, out):
    _, _, sy, sx = sides()
    k = iota((BORDER, 16), 0)
    j = iota((BORDER, 16), 1)
    s = j - 12
    fits = (s >= 0) & (s < 3)
    z = jnp.zeros((BORDER, F), f32)
    for t, ref in enumerate((rxa, rxb)):
        at = 2 * CW + 512
        z = z + dot(hot(fits & (k == 3 * direction(0, sx[t]) + s)), ref[:, at : at + F])
    for u, ref in enumerate((rya, ryb)):
        for q, dx in enumerate((0, sx[0], sx[1])):
            z = z + dot(hot(fits & (k == 3 * direction(sy[u], dx) + s)), ref[:, CW * q : CW * q + F])
    x = tr[...].astype(f32)
    x = x - jnp.mean(x, axis=1, keepdims=True)
    z = z - jnp.mean(z, axis=1, keepdims=True)
    high = lax.Precision.HIGHEST
    cov = lax.dot_general(z, x, NT, precision=high, preferred_element_type=f32) / F
    vz = jnp.mean(z * z, axis=1, keepdims=True)
    ones = jnp.ones((8, F), f32)
    vx = lax.dot_general(ones, x * x, NT, precision=high, preferred_element_type=f32)[0:1] / F
    alive = iota((1, K), 1) < comp[...]
    out[...] = jnp.where(alive, cov / jnp.sqrt((vx + epsilon) * (vz + epsilon)), 0.0)


def row_select(n, first):
    j5 = iota((5 * n, 16), 1)
    r5 = iota((5 * n, 16), 0)
    s5 = j5 - 3 * (r5 >> 4)
    k5 = (r5 & 15) + first
    fits = (s5 >= 0) & (s5 < 3)

    def select(d):
        return hot(fits & (k5 == 3 * d + s5))

    return select


def before_kernel(
    rows, cols, row_ref, col_ref, count, compc, foot, tr, wide, merged, mtrace, rxa, rxb,
    base, tbase, upper, lower,
):
    row, col, _, sx = sides()
    n = 16
    whole, tail = receive_sides(
        row_select(n, 8), n, (rxa, rxb), row, col, sx, row_ref, col_ref, rows, cols
    )
    flag = tail[:, CH : CH + 1] > 0.5
    k = iota((n, 1), 0) + 8
    _, _, _, c_lf = pixel_shift(0, -1, row, col, row_ref, col_ref, rows, cols)
    _, _, _, c_rt = pixel_shift(0, 1, row, col, row_ref, col_ref, rows, cols)
    x_lo = jnp.where(k >= 12, PW - c_rt, 0)
    x_hi = jnp.where(flag, jnp.where(k < 12, c_lf, PW), 0)
    x = iota((1, CH), 1) & (PW - 1)
    inside = (x >= x_lo) & (x < x_hi)
    total = count[...]
    own_id = wide[0:1, 0:MP]
    own_mask = (iota((K - BORDER, MP), 0) + BORDER == own_id) & (iota((K - BORDER, MP), 1) < total)
    own_hot = hot(own_mask)
    hit = jnp.sum(own_hot.astype(f32), axis=1, keepdims=True) > 0.5
    alive = iota((K - BORDER, 1), 0) + BORDER < compc[...]
    step = 512
    for b in range(NPIX // step):
        lanes = slice(step * b, step * (b + 1))
        mine = foot[:, lanes].astype(f32)
        got = dot(own_hot, merged[:, lanes])
        low = jnp.where(alive, jnp.where(hit, got, mine[BORDER:]), 0.0)
        mid = []
        for q in range(step // CH):
            m = b * (step // CH) + q
            mid.append(
                jnp.where(
                    inside, whole[n * m : n * (m + 1)], mine[8:BORDER, CH * q : CH * (q + 1)]
                )
            )
        mid = jnp.concatenate(mid, axis=1)
        base[:, lanes] = jnp.concatenate([mine[0:8], mid, low], axis=0).astype(bf16)
        if step * b < BAND:
            upper[:, lanes] = jnp.concatenate([mine[0:8], mid[0:8]], axis=0)
        if step * b >= LOW:
            lower[:, step * b - LOW : step * (b + 1) - LOW] = mid
    mine = tr[...].astype(f32)
    mid = jnp.where(flag, tail[:, 0:F], mine[8:BORDER])
    low = jnp.where(alive, jnp.where(hit, dot(own_hot, mtrace[...]), mine[BORDER:]), 0.0)
    tbase[...] = jnp.concatenate([mine[0:8], mid, low], axis=0)


def final_kernel(
    rows, cols, row_in, col_in, base, tbase, upper, lower, rya, ryb,
    nfoot, ntrace, placed, tails, pbuf, out, row_ref, col_ref, sem,
):
    ready = fetch(row_in, col_in, row_ref, col_ref, sem)
    row, col, sy, sx = sides()
    n = 16
    downs = [jnp.where(sy[u] > 0, 1, 0) for u in range(2)]
    bands = receive_bands(
        [row_select(n, 8 * dn) for dn in downs],
        n, (rya, ryb), pbuf, row, col, sy, sx, row_ref, col_ref, rows, cols, ready,
    )
    for dn, (moved, tail) in zip(downs, bands):
        for m in range(12):
            placed[dn, :, CH * m : CH * (m + 1)] = moved[n * m : n * (m + 1)]
        tails[dn] = tail
    _, _, r_up, _ = pixel_shift(-1, 0, row, col, row_ref, col_ref, rows, cols)
    _, _, r_dn, _ = pixel_shift(1, 0, row, col, row_ref, col_ref, rows, cols)
    _, _, _, c_lf = pixel_shift(0, -1, row, col, row_ref, col_ref, rows, cols)
    _, _, _, c_rt = pixel_shift(0, 1, row, col, row_ref, col_ref, rows, cols)
    k = iota((n, 1), 0)
    pix = iota((1, BAND), 1)
    y = pix >> 6
    x = pix & (PW - 1)
    copies = []
    for dn, edge in enumerate((upper, lower)):
        j = k - 7 * dn
        flag = tails[dn, :, CH : CH + 1] > 0.5
        x_lo = jnp.where(j >= 6, PW - c_rt, 0)
        x_hi = jnp.where(flag, jnp.where(j < 3, c_lf, PW), 0)
        y_ok = (y < r_up) if dn == 0 else (y >= OV_HI - r_dn)
        inside = y_ok & (x >= x_lo) & (x < x_hi)
        out[dn] = jnp.where(inside, placed[dn], edge[...]).astype(bf16)
        copies.append(
            pltpu.make_async_copy(
                out.at[dn],
                nfoot.at[8 * dn : 8 * dn + 16, LOW * dn : LOW * dn + BAND],
                sem.at[2 + dn],
            )
        )
        copies[-1].start()
    mine = tbase[0:BORDER]
    gap = jnp.zeros((8, 2 * CH), f32)
    both = jnp.concatenate([tails[0], gap], axis=0) + jnp.concatenate([gap, tails[1]], axis=0)
    top = jnp.where(both[:, CH : CH + 1] > 0.5, both[:, 0:F], mine)
    ntrace[...] = jnp.concatenate([top, tbase[BORDER:]], axis=0).astype(bf16)
    for copy in copies:
        copy.wait()


SMEM = pl.BlockSpec(memory_space=pltpu.SMEM)
VMEM = pl.BlockSpec(memory_space=pltpu.VMEM)
LIMIT = 24 * 1024 * 1024


def shape(*dims, dtype=bf16):
    return jax.ShapeDtypeStruct(dims, dtype)


PACKETS = (shape(16, XW), shape(16, XW), shape(16, CW), shape(16, CW))
HBM = pl.BlockSpec(memory_space=pltpu.HBM)


def call(kernel, outs, ins, out_specs, scratch, flops, aliases={}):
    return pl.pallas_call(
        kernel,
        out_shape=outs,
        in_specs=ins,
        out_specs=out_specs,
        scratch_shapes=scratch,
        input_output_aliases=aliases,
        compiler_params=pltpu.CompilerParams(vmem_limit_bytes=LIMIT),
        cost_estimate=pl.CostEstimate(flops=flops, bytes_accessed=1 << 20, transcendentals=0),
    )


def swap(value, axis, parity):
    count = lax.axis_size(axis)
    pairs = []
    for i in range(parity, count - 1, 2):
        pairs += [(i, i + 1), (i + 1, i)]
    return lax.ppermute(value, axis, pairs)


def exchange(xa, xb, va, vb):
    rxb = swap(xb, "px", 1)
    rxa = swap(xa, "px", 0)
    yb = jnp.concatenate([vb, rxa[:, CW : 2 * CW], rxb[:, CW : 2 * CW]], axis=1)
    ya = jnp.concatenate([va, rxa[:, 0:CW], rxb[:, 0:CW]], axis=1)
    ryb = swap(yb, "py", 1)
    rya = swap(ya, "py", 0)
    return rxa, rxb, rya, ryb


def body(
    residual, footprints, traces, merge_pairs, pair_counts, comp_counts, row_inter, col_inter
):
    res = residual[0, 0]
    foot = footprints[0, 0]
    tr = traces[0, 0]
    table = merge_pairs[0, 0]
    wide = jnp.tile(table.T, (1, 5))
    rows, cols = lax.axis_size("py"), lax.axis_size("px")

    def geo(kernel):
        def run(*refs):
            kernel(rows, cols, *refs)

        return run

    packets = call(
        pack_kernel, PACKETS, [VMEM] * 2, (VMEM,) * 4, [], 1 << 24
    )(foot, jnp.pad(tr[:32], ((0, 0), (0, 2 * CH))))
    rxa, rxb, rya, ryb = exchange(*packets)

    prepared = call(
        own_kernel,
        (
            shape(F, NPIX),
            shape(MP, NPIX, dtype=f32),
            shape(MP, NPIX, dtype=f32),
            shape(MP, F, dtype=f32),
        ),
        [VMEM] * 5,
        (VMEM,) * 4,
        [],
        1 << 24,
    )(pair_counts, res, foot, tr, table)

    placed = call(
        geo(side_kernel),
        (shape(MP, NPIX, dtype=f32), shape(MP, F, dtype=f32)),
        [SMEM] * 2 + [VMEM] * 4,
        (VMEM,) * 2,
        [],
        1 << 24,
    )(row_inter, col_inter, pair_counts, table, rxa, rxb)

    xa, xb, va, vb, merged, mtrace = call(
        geo(refit_kernel),
        PACKETS + (shape(MP, NPIX), shape(MP, F)),
        [VMEM] * 14,
        (VMEM,) * 6,
        [
            pltpu.VMEM((MP, NPIX), f32),
            pltpu.VMEM((6, MP, PBW), bf16),
            pltpu.SMEM((rows - 1,), jnp.int32),
            pltpu.SMEM((cols - 1,), jnp.int32),
            pltpu.SemaphoreType.DMA((2,)),
        ],
        1 << 28,
    )(row_inter, col_inter, pair_counts, res, *prepared, *placed, table, wide, rya, ryb)
    back = exchange(xa, xb, va, vb)

    corr = call(
        corr_kernel, shape(BORDER, K, dtype=f32), [VMEM] * 6, VMEM, [], 1 << 22
    )(comp_counts, tr, rxa, rxb, rya, ryb)

    partial = call(
        geo(before_kernel),
        (
            shape(K, NPIX),
            shape(K, F, dtype=f32),
            shape(16, BAND, dtype=f32),
            shape(16, BAND, dtype=f32),
        ),
        [SMEM] * 2 + [VMEM] * 9,
        (VMEM,) * 4,
        [],
        1 << 24,
    )(row_inter, col_inter, pair_counts, comp_counts, foot, tr, wide, merged, mtrace, *back[:2])

    nfoot, ntrace = call(
        geo(final_kernel),
        (shape(K, NPIX), shape(K, F)),
        [VMEM] * 2 + [HBM] + [VMEM] * 5,
        (HBM, VMEM),
        [
            pltpu.VMEM((2, 16, BAND), f32),
            pltpu.VMEM((2, 16, 2 * CH), f32),
            pltpu.VMEM((6, 16, PBW), bf16),
            pltpu.VMEM((2, 16, BAND), bf16),
            pltpu.SMEM((rows - 1,), jnp.int32),
            pltpu.SMEM((cols - 1,), jnp.int32),
            pltpu.SemaphoreType.DMA((4,)),
        ],
        1 << 26,
        {2: 0},
    )(row_inter, col_inter, *partial, *back[2:])
    return nfoot[None, None], ntrace[None, None], corr.T[None, None]


def solution(mesh):
    in_specs = (
        P("py", "px", None, None),
        P("py", "px", None, None),
        P("py", "px", None, None),
        P("py", "px", None, None),
        P("py", "px"),
        P("py", "px"),
        P(),
        P(),
    )
    out_specs = (P("py", "px", None, None), P("py", "px", None, None), P("py", "px", None, None))
    return jax.shard_map(body, mesh=mesh, in_specs=in_specs, out_specs=out_specs, check_vma=False)
```

time: 64.7 us -> 61.8 us (0.955)
  starting transfers between devices: 41.1 us -> 36.5 us
  waiting for transfers between devices: 6.43 us -> 8.47 us
    ppermute x8, starting transfers between devices: 41.1 us -> 36.5 us  [swap(): return lax.ppermute(value, axis, pairs)]
    ppermute x8, waiting for transfers between devices: 6.43 us -> 8.47 us  [swap(): return lax.ppermute(value, axis, pairs)]
    unnamed x18 -> x17, local copies, waits for them, and re-layouts: 3.75 us -> 2.84 us
    slice x0 -> x1, local copies, waits for them, and re-layouts: none -> 0.7 us  [body(): tr[:32]]
    pallas_call x4 -> x7, Pallas kernels: 10.7 us -> 10.4 us  [the longest x1 2.87 us: body(): call(geo(refit_kernel), PACKETS + (shape(MP, NPIX), shape(MP, F)), [VMEM]...]
  transfers between devices with their start and end apart: 8 -> 8, of which waited for: 3 -> 3; matrix products, arithmetic and copies ran while one was open for 1% -> 0% of each run, Pallas kernels for 1% -> 8%
where the time goes in v2:
time: 61.8 us; the launch traced here: 61.3 us
  starting transfers between devices  36.5 us (59%)
  Pallas kernels  10.4 us (17%)
  waiting for transfers between devices  8.47 us (14%)
  local copies, waits for them, and re-layouts  3.73 us (6%)
  between operations  2.14 us (3%)
    ppermute x8, starting transfers between devices, swap(): return lax.ppermute(value, axis, pairs)  36.5 us
    ppermute x8, waiting for transfers between devices, swap(): return lax.ppermute(value, axis, pairs)  8.47 us
    pallas_call x1, Pallas kernels, body(): call(geo(refit_kernel), PACKETS + (shape(MP, NPIX), shape(MP, F)), [VMEM]...  2.87 us
    unnamed x17, local copies, waits for them, and re-layouts  2.84 us
    pallas_call x1, Pallas kernels, body(): call(geo(final_kernel), (shape(K, NPIX), shape(K, F)), [VMEM] * 2 + [HBM]...  2.27 us
    pallas_call x1, Pallas kernels, body(): call(geo(before_kernel), (shape(K, NPIX), shape(K, F, dtype=f32), shape(1...  1.72 us
  transfers between devices with their start and end apart: 8, of which 3 were waited for; matrix products, arithmetic and copies ran while one was open for 0% of the time, Pallas kernels for 8%

profile of v2, /device:TPU:57, one launch (start us, length us, event | category | flops | bytes accessed | tf_op | source)
XLA Modules:
  0.0 61.3 jit_solution(15967957937234483066)
XLA Ops:
  0.6 0.7 %slice_bitcast_fusion = bf16[32,128]{1,0:T(8,128)(2,1)S(1)} fusion(bf16[1,1,40,128]{3,2,1,0:T(8,128)(2,1)} %param.10), kind=kLoop, calls=%fused_computation.4 | loop fusion | bytes 16384 | tf_op jit(solution)/shard_map/slice | solution.py:535
  1.3 0.0 copy-start.2
  1.3 1.0 %copy-done.2 = bf16[1,1,40,4096]{3,2,1,0:T(8,128)(2,1)S(1)} copy-done((bf16[1,1,40,4096]{3,2,1,0:T(8,128)(2,1)S(1)}, bf16[1,1,40,4096]{3,2,1,0:T(8,128)(2,1)}, u32[]{:S(2)}) %copy-start.2) | copy-done | bytes 327704
  2.3 0.0 copy-start.3
  2.3 0.3 shard_map.104
  2.6 2.6 %collective-permute-start = (bf16[16,1664]{1,0:T(8,128)(2,1)S(1)}, bf16[16,1664]{1,0:T(8,128)(2,1)S(1)}, u32[]{:S(2)}, u32[]{:S(2)}) collective-permute-start(bf16[16,1664]{1,0:T(8,128)(2,1)S(1)} %get-tuple-element.29), channel_id=1, source_target_pairs={{0,1},{1,0},{2,3},{3,2},{4,5},{5,4},{6,7},{7,6},{8,9},{9,8},{10,11... | collective-permute-start | bytes 159752 | tf_op jit(solution)/shard_map/ppermute | solution.py:504
  5.2 5.4 %collective-permute-start.1 = (bf16[16,1664]{1,0:T(8,128)(2,1)S(1)}, bf16[16,1664]{1,0:T(8,128)(2,1)S(1)}, u32[]{:S(2)}, u32[]{:S(2)}) collective-permute-start(bf16[16,1664]{1,0:T(8,128)(2,1)S(1)} %get-tuple-element.30), channel_id=1, source_target_pairs={{1,2},{2,1},{3,4},{4,3},{5,6},{6,5},{7,8},{8,7},{9,10},{10,9},{11,... | collective-permute-start | bytes 159752 | tf_op jit(solution)/shard_map/ppermute | solution.py:504
  10.6 0.0 collective-permute-done.refs_4_.rxa
  10.6 2.7 %collective-permute-done.1.refs_5_.rxb = bf16[16,1664]{1,0:T(8,128)(2,1)S(1)} collective-permute-done((bf16[16,1664]{1,0:T(8,128)(2,1)S(1)}, bf16[16,1664]{1,0:T(8,128)(2,1)S(1)}, u32[]{:S(2)}, u32[]{:S(2)}) %collective-permute-start.1) | collective-permute-done | bytes 53280 | tf_op jit(solution)/shard_map/ppermute | solution.py:504
  13.4 4.0 %collective-permute-start.2 = (bf16[16,1152]{1,0:T(8,128)(2,1)S(1)}, bf16[16,1152]{1,0:T(8,128)(2,1)S(1)}, u32[]{:S(2)}, u32[]{:S(2)}) collective-permute-start(bf16[16,1152]{1,0:T(8,128)(2,1)S(1)} %pad_maximum_fusion), channel_id=1, source_target_pairs={{0,32},{32,0},{64,96},{96,64},{128,160},{160,128},{192,224},{224,1... | collective-permute-start | bytes 110600 | tf_op jit(solution)/shard_map/ppermute | solution.py:504
  17.4 0.0 copy-start.7
  17.4 11.1 %collective-permute-start.3 = (bf16[16,1152]{1,0:T(8,128)(2,1)S(1)}, bf16[16,1152]{1,0:T(8,128)(2,1)S(1)}, u32[]{:S(2)}, u32[]{:S(2)}) collective-permute-start(bf16[16,1152]{1,0:T(8,128)(2,1)S(1)} %pad_maximum_fusion.1), channel_id=1, source_target_pairs={{32,64},{64,32},{96,128},{128,96},{160,192},{192,160},{224,256},{2... | collective-permute-start | bytes 110600 | tf_op jit(solution)/shard_map/ppermute | solution.py:504
  29.2 0.0 copy-done.7
  29.2 0.1 copy.15.table.refs_3_.refs_10_
  29.3 0.0 copy-start.4
  29.3 0.1 tile.10.refs_11_.refs_6_
  29.4 0.0 copy-done.3
  29.4 0.6 %copy-done.4 = bf16[1,1,40,128]{3,2,1,0:T(8,128)(2,1)S(1)} copy-done((bf16[1,1,40,128]{3,2,1,0:T(8,128)(2,1)S(1)}, bf16[1,1,40,128]{3,2,1,0:T(8,128)(2,1)}, u32[]{:S(2)}) %copy-start.4) | copy-done | bytes 10264
  30.0 0.0 copy-start
  30.0 1.2 %copy-done = bf16[1,1,4096,128]{3,2,1,0:T(8,128)(2,1)S(1)} copy-done((bf16[1,1,4096,128]{3,2,1,0:T(8,128)(2,1)S(1)}, bf16[1,1,4096,128]{3,2,1,0:T(8,128)(2,1)}, u32[]{:S(2)}) %copy-start) | copy-done | bytes 1048600
  31.2 0.0 copy-start.5
  31.2 0.0 copy-start.6
  31.2 0.0 copy-start.1
  31.2 0.9 %shard_map.103 = (bf16[128,4096]{1,0:T(8,128)(2,1)S(1)}, f32[16,4096]{1,0:T(8,128)S(1)}, f32[16,4096]{1,0:T(8,128)S(1)}, f32[16,128]{1,0:T(8,128)S(1)}) custom-call(s32[1,1]{1,0:T(1,128)S(6)} %copy.23.count.refs_2_, bf16[4096,128]{1,0:T(8,128)(2,1)S(1)} %bitcast.16, bf16[40,4096]{1,0:T(8,128)(2,1)S(1)} %bitcast.19, bf16[40,128]{1,0:T(8,128)(2,1)S(1)} %bitcast.21, ...), custom_call_target="tpu_custom_call" | custom-call | flops 16777216 | bytes 1048576 | tf_op jit(solution)/shard_map/pallas_call | solution.py:538
  32.2 0.0 copy-done.5
  32.2 0.0 copy-done.6
  32.2 1.1 %shard_map.105 = (f32[16,4096]{1,0:T(8,128)S(1)}, f32[16,128]{1,0:T(8,128)S(1)}) custom-call(s32[15]{0:T(128)S(1)} %copy-done.5, s32[31]{0:T(128)S(1)} %copy-done.6, s32[1,1]{1,0:T(1,128)S(6)} %copy.23.count.refs_2_, s32[16,3]{1,0:T(8,128)S(1)} %copy.15.table.refs_3_.refs_10_, bf16[16,1664]{1,0:T(8,128)(2,1)S(1)} %collective-permute-done.refs_4_.rxa, ...), custom_call_target="tpu_custom_call" | custom-call | flops 16777216 | bytes 1048576 | tf_op jit(solution)/shard_map/pallas_call | solution.py:552
  33.3 0.0 collective-permute-done.2.refs_12_.rya
  33.3 0.0 collective-permute-done.3.refs_13_.ryb
  33.3 0.0 copy-done.1
  33.4 2.9 %shard_map.106 = (bf16[16,1664]{1,0:T(8,128)(2,1)S(1)}, bf16[16,1664]{1,0:T(8,128)(2,1)S(1)}, bf16[16,384]{1,0:T(8,128)(2,1)S(1)}, bf16[16,384]{1,0:T(8,128)(2,1...) custom-call(s32[15]{0:T(128)S(1)} %copy-done.5, s32[31]{0:T(128)S(1)} %copy-done.6, ...), custom_call_target="tpu_custom_call" | custom-call | flops 268435456 | bytes 1048576 | tf_op jit(solution)/shard_map/pallas_call | solution.py:561
  36.2 1.9 %collective-permute-start.4 = (bf16[16,1664]{1,0:T(8,128)(2,1)S(1)}, bf16[16,1664]{1,0:T(8,128)(2,1)S(1)}, u32[]{:S(2)}, u32[]{:S(2)}) collective-permute-start(bf16[16,1664]{1,0:T(8,128)(2,1)S(1)} %get-tuple-element.37), channel_id=1, source_target_pairs={{0,1},{1,0},{2,3},{3,2},{4,5},{5,4},{6,7},{7,6},{8,9},{9,8},{10,11... | collective-permute-start | bytes 159752 | tf_op jit(solution)/shard_map/ppermute | solution.py:504
  38.2 3.8 %collective-permute-start.5 = (bf16[16,1664]{1,0:T(8,128)(2,1)S(1)}, bf16[16,1664]{1,0:T(8,128)(2,1)S(1)}, u32[]{:S(2)}, u32[]{:S(2)}) collective-permute-start(bf16[16,1664]{1,0:T(8,128)(2,1)S(1)} %get-tuple-element.38), channel_id=1, source_target_pairs={{1,2},{2,1},{3,4},{4,3},{5,6},{6,5},{7,8},{8,7},{9,10},{10,9},{11,... | collective-permute-start | bytes 159752 | tf_op jit(solution)/shard_map/ppermute | solution.py:504
  42.0 0.0 collective-permute-done.4.refs_9_
  42.0 4.3 %collective-permute-done.5.refs_10_ = bf16[16,1664]{1,0:T(8,128)(2,1)S(1)} collective-permute-done((bf16[16,1664]{1,0:T(8,128)(2,1)S(1)}, bf16[16,1664]{1,0:T(8,128)(2,1)S(1)}, u32[]{:S(2)}, u32[]{:S(2)}) %collective-permute-start.5) | collective-permute-done | bytes 53280 | tf_op jit(solution)/shard_map/ppermute | solution.py:504
  46.3 1.9 %collective-permute-start.6 = (bf16[16,1152]{1,0:T(8,128)(2,1)S(1)}, bf16[16,1152]{1,0:T(8,128)(2,1)S(1)}, u32[]{:S(2)}, u32[]{:S(2)}) collective-permute-start(bf16[16,1152]{1,0:T(8,128)(2,1)S(1)} %pad_maximum_fusion.2), channel_id=1, source_target_pairs={{0,32},{32,0},{64,96},{96,64},{128,160},{160,128},{192,224},{224,1... | collective-permute-start | bytes 110600 | tf_op jit(solution)/shard_map/ppermute | solution.py:504
  48.3 5.9 %collective-permute-start.7 = (bf16[16,1152]{1,0:T(8,128)(2,1)S(1)}, bf16[16,1152]{1,0:T(8,128)(2,1)S(1)}, u32[]{:S(2)}, u32[]{:S(2)}) collective-permute-start(bf16[16,1152]{1,0:T(8,128)(2,1)S(1)} %pad_maximum_fusion.3), channel_id=1, source_target_pairs={{32,64},{64,32},{96,128},{128,96},{160,192},{192,160},{224,256},{2... | collective-permute-start | bytes 110600 | tf_op jit(solution)/shard_map/ppermute | solution.py:504
  54.8 1.1 %shard_map.109 = f32[24,40]{1,0:T(8,128)} custom-call(s32[1,1]{1,0:T(1,128)S(6)} %copy.24.refs_3_.comp, bf16[40,128]{1,0:T(8,128)(2,1)S(1)} %bitcast.22, bf16[16,1664]{1,0:T(8,128)(2,1)S(1)} %collective-permute-done.refs_4_.rxa, bf16[16,1664]{1,0:T(8,128)(2,1)S(1)} %collective-permute-done.1.refs_5_.rxb, ...), custom_call_target="tpu_custom_call" | custom-call | flops 4194304 | bytes 1048576 | tf_op jit(solution)/shard_map/pallas_call | solution.py:577
  55.9 1.7 %shard_map.107 = (bf16[40,4096]{1,0:T(8,128)(2,1)}, f32[40,128]{1,0:T(8,128)S(1)}, f32[16,1536]{1,0:T(8,128)S(1)}, f32[16,1536]{1,0:T(8,128)S(1)}) custom-call(s32[15]{0:T(128)S(1)} %copy-done.5, s32[31]{0:T(128)S(1)} %copy-done.6, s32[1,1]{1,0:T(1,128)S(6)} %copy.23.count.refs_2_, s32[1,1]{1,0:T(1,128)S(6)} %copy.24.refs_3_.comp, ...), custom_call_target="tpu_custom_call" | custom-call | flops 16777216 | bytes 1048576 | tf_op jit(solution)/shard_map/pallas_call | solution.py:581
  57.6 0.0 collective-permute-done.6.refs_6_
  57.6 1.4 %collective-permute-done.7.refs_7_ = bf16[16,1152]{1,0:T(8,128)(2,1)S(1)} collective-permute-done((bf16[16,1152]{1,0:T(8,128)(2,1)S(1)}, bf16[16,1152]{1,0:T(8,128)(2,1)S(1)}, u32[]{:S(2)}, u32[]{:S(2)}) %collective-permute-start.7) | collective-permute-done | bytes 36896 | tf_op jit(solution)/shard_map/ppermute | solution.py:504
  59.0 2.3 %shard_map.108 = (bf16[40,4096]{1,0:T(8,128)(2,1)}, bf16[40,128]{1,0:T(8,128)(2,1)}) custom-call(s32[15]{0:T(128)S(1)} %copy-done.5, s32[31]{0:T(128)S(1)} %copy-done.6, bf16[40,4096]{1,0:T(8,128)(2,1)} %get-tuple-element.39.refs_2_, f32[40,128]{1,0:T(8,128)S(1)} %get-tuple-element.40.refs_3_, ...), custom_call_target="tpu_custom_call", output_to_operand_aliasing={{0}: (2, {})} | custom-call | flops 67108864 | bytes 1048576 | tf_op jit(solution)/shard_map/pallas_call | solution.py:595
  (11 shorter events, 0.1 us)
Async XLA Ops:
  1.3 1.0 %copy-start.2 = (bf16[1,1,40,4096]{3,2,1,0:T(8,128)(2,1)S(1)}, bf16[1,1,40,4096]{3,2,1,0:T(8,128)(2,1)}, u32[]{:S(2)}) copy-start(bf16[1,1,40,4096]{3,2,1,0:T(8,128)(2,1)} %param.9) | copy-start | bytes 983044
  2.3 27.1 %copy-start.3 = (bf16[1,1,40,4096]{3,2,1,0:T(8,128)(2,1)S(1)}, bf16[1,1,40,4096]{3,2,1,0:T(8,128)(2,1)}, u32[]{:S(2)}) copy-start(bf16[1,1,40,4096]{3,2,1,0:T(8,128)(2,1)} %param.9) | copy-start | bytes 983044
  2.6 8.0 %collective-permute-start = (bf16[16,1664]{1,0:T(8,128)(2,1)S(1)}, bf16[16,1664]{1,0:T(8,128)(2,1)S(1)}, u32[]{:S(2)}, u32[]{:S(2)}) collective-permute-start(bf16[16,1664]{1,0:T(8,128)(2,1)S(1)} %get-tuple-element.29), channel_id=1, source_target_pairs={{0,1},{1,0},{2,3},{3,2},{4,5},{5,4},{6,7},{7,6},{8,9},{9,8},{10,11... | collective-permute-start | bytes 159752 | tf_op jit(solution)/shard_map/ppermute | solution.py:504
  5.2 8.2 %collective-permute-start.1 = (bf16[16,1664]{1,0:T(8,128)(2,1)S(1)}, bf16[16,1664]{1,0:T(8,128)(2,1)S(1)}, u32[]{:S(2)}, u32[]{:S(2)}) collective-permute-start(bf16[16,1664]{1,0:T(8,128)(2,1)S(1)} %get-tuple-element.30), channel_id=1, source_target_pairs={{1,2},{2,1},{3,4},{4,3},{5,6},{6,5},{7,8},{8,7},{9,10},{10,9},{11,... | collective-permute-start | bytes 159752 | tf_op jit(solution)/shard_map/ppermute | solution.py:504
  13.4 19.9 %collective-permute-start.2 = (bf16[16,1152]{1,0:T(8,128)(2,1)S(1)}, bf16[16,1152]{1,0:T(8,128)(2,1)S(1)}, u32[]{:S(2)}, u32[]{:S(2)}) collective-permute-start(bf16[16,1152]{1,0:T(8,128)(2,1)S(1)} %pad_maximum_fusion), channel_id=1, source_target_pairs={{0,32},{32,0},{64,96},{96,64},{128,160},{160,128},{192,224},{224,1... | collective-permute-start | bytes 110600 | tf_op jit(solution)/shard_map/ppermute | solution.py:504
  17.4 11.8 %copy-start.7 = (s32[1,1,16,3]{2,1,3,0:T(1,128)S(1)}, s32[1,1,16,3]{2,1,3,0:T(1,128)}, u32[]{:S(2)}) copy-start(s32[1,1,16,3]{2,1,3,0:T(1,128)} %param.11) | copy-start | bytes 580
  17.4 15.9 %collective-permute-start.3 = (bf16[16,1152]{1,0:T(8,128)(2,1)S(1)}, bf16[16,1152]{1,0:T(8,128)(2,1)S(1)}, u32[]{:S(2)}, u32[]{:S(2)}) collective-permute-start(bf16[16,1152]{1,0:T(8,128)(2,1)S(1)} %pad_maximum_fusion.1), channel_id=1, source_target_pairs={{32,64},{64,32},{96,128},{128,96},{160,192},{192,160},{224,256},{2... | collective-permute-start | bytes 110600 | tf_op jit(solution)/shard_map/ppermute | solution.py:504
  29.3 0.7 %copy-start.4 = (bf16[1,1,40,128]{3,2,1,0:T(8,128)(2,1)S(1)}, bf16[1,1,40,128]{3,2,1,0:T(8,128)(2,1)}, u32[]{:S(2)}) copy-start(bf16[1,1,40,128]{3,2,1,0:T(8,128)(2,1)} %param.10) | copy-start | bytes 30724
  30.0 1.2 %copy-start = (bf16[1,1,4096,128]{3,2,1,0:T(8,128)(2,1)S(1)}, bf16[1,1,4096,128]{3,2,1,0:T(8,128)(2,1)}, u32[]{:S(2)}) copy-start(bf16[1,1,4096,128]{3,2,1,0:T(8,128)(2,1)} %param.8) | copy-start | bytes 3145732
  31.2 1.0 %copy-start.5 = (s32[15]{0:T(128)S(1)}, s32[15]{0:T(128)}, u32[]{:S(2)}) copy-start(s32[15]{0:T(128)} %refs_0_.7) | copy-start | bytes 184
  31.2 1.0 %copy-start.6 = (s32[31]{0:T(128)S(1)}, s32[31]{0:T(128)}, u32[]{:S(2)}) copy-start(s32[31]{0:T(128)} %refs_1_.7) | copy-start | bytes 376
  31.2 2.1 %copy-start.1 = (bf16[1,1,4096,128]{3,2,1,0:T(8,128)(2,1)S(1)}, bf16[1,1,4096,128]{3,2,1,0:T(8,128)(2,1)}, u32[]{:S(2)}) copy-start(bf16[1,1,4096,128]{3,2,1,0:T(8,128)(2,1)} %param.8) | copy-start | bytes 3145732
  36.2 5.7 %collective-permute-start.4 = (bf16[16,1664]{1,0:T(8,128)(2,1)S(1)}, bf16[16,1664]{1,0:T(8,128)(2,1)S(1)}, u32[]{:S(2)}, u32[]{:S(2)}) collective-permute-start(bf16[16,1664]{1,0:T(8,128)(2,1)S(1)} %get-tuple-element.37), channel_id=1, source_target_pairs={{0,1},{1,0},{2,3},{3,2},{4,5},{5,4},{6,7},{7,6},{8,9},{9,8},{10,11... | collective-permute-start | bytes 159752 | tf_op jit(solution)/shard_map/ppermute | solution.py:504
  38.2 8.2 %collective-permute-start.5 = (bf16[16,1664]{1,0:T(8,128)(2,1)S(1)}, bf16[16,1664]{1,0:T(8,128)(2,1)S(1)}, u32[]{:S(2)}, u32[]{:S(2)}) collective-permute-start(bf16[16,1664]{1,0:T(8,128)(2,1)S(1)} %get-tuple-element.38), channel_id=1, source_target_pairs={{1,2},{2,1},{3,4},{4,3},{5,6},{6,5},{7,8},{8,7},{9,10},{10,9},{11,... | collective-permute-start | bytes 159752 | tf_op jit(solution)/shard_map/ppermute | solution.py:504
  46.3 11.3 %collective-permute-start.6 = (bf16[16,1152]{1,0:T(8,128)(2,1)S(1)}, bf16[16,1152]{1,0:T(8,128)(2,1)S(1)}, u32[]{:S(2)}, u32[]{:S(2)}) collective-permute-start(bf16[16,1152]{1,0:T(8,128)(2,1)S(1)} %pad_maximum_fusion.2), channel_id=1, source_target_pairs={{0,32},{32,0},{64,96},{96,64},{128,160},{160,128},{192,224},{224,1... | collective-permute-start | bytes 110600 | tf_op jit(solution)/shard_map/ppermute | solution.py:504
  48.3 10.7 %collective-permute-start.7 = (bf16[16,1152]{1,0:T(8,128)(2,1)S(1)}, bf16[16,1152]{1,0:T(8,128)(2,1)S(1)}, u32[]{:S(2)}, u32[]{:S(2)}) collective-permute-start(bf16[16,1152]{1,0:T(8,128)(2,1)S(1)} %pad_maximum_fusion.3), channel_id=1, source_target_pairs={{32,64},{64,32},{96,128},{128,96},{160,192},{192,160},{224,256},{2... | collective-permute-start | bytes 110600 | tf_op jit(solution)/shard_map/ppermute | solution.py:504

commit v3 on v2

--- a/solution.py
+++ b/solution.py
@@ -64,10 +64,10 @@
     return dot(pick, jnp.concatenate(pieces + [tail], axis=0)).astype(bf16)
 
 
-def pixel_shift(dy, dx, row, col, row_ref, col_ref, rows, cols):
-    ri = row_ref[jnp.clip(row + jnp.minimum(dy, 0), 0, rows - 2)]
-    ci = col_ref[jnp.clip(col + jnp.minimum(dx, 0), 0, cols - 2)]
-    return dy * (OV_HI - ri), dx * (PW - ci), ri, ci
+def pixel_shift(dy, dx, geo):
+    ri = jnp.where(dy > 0, geo[0, 1], geo[0, 0])
+    ci = jnp.where(dx > 0, geo[0, 3], geo[0, 2])
+    return dy * (OV_HI - ri), dx * (PW - ci)
 
 
 def column_matrix(ox):
@@ -91,16 +91,17 @@
     return dot(stack, column_matrix(ox))
 
 
-def receive_sides(select, n, xs, row, col, sx, row_ref, col_ref, rows, cols):
+def receive_sides(select, n, xs, sx, geo, ready):
     tail = jnp.zeros((n, 2 * CH), f32)
     whole = None
-    for t in range(2):
-        picked = dot(select(direction(0, sx[t])), xs[t][:, 2 * CW : XW])
+    taken = [dot(select(direction(0, sx[t])), xs[t][:, 2 * CW : XW]) for t in range(2)]
+    ready()
+    for t, picked in enumerate(taken):
         full = jnp.concatenate(
             [picked[n * g : n * (g + 1)] for g in range(4)] + [picked[4 * n :, 0:512]], axis=1
         )
         tail = tail + picked[4 * n :, 512 : 512 + 2 * CH]
-        _, ox, _, _ = pixel_shift(0, sx[t], row, col, row_ref, col_ref, rows, cols)
+        _, ox = pixel_shift(0, sx[t], geo)
         moved = place_whole(full, ox)
         whole = moved if whole is None else whole + moved
     return whole, tail
@@ -111,7 +112,7 @@
     pbuf[:, :, PAD * CH + BAND :] = jnp.zeros(pbuf.shape[:2] + (PBW - PAD * CH - BAND,), bf16)
 
 
-def receive_bands(selects, n, ys, pbuf, row, col, sy, sx, row_ref, col_ref, rows, cols, ready):
+def receive_bands(selects, n, ys, pbuf, sy, sx, geo, ready):
     steps = (0, sx[0], sx[1])
     picked = [
         [
@@ -120,8 +121,8 @@
         ]
         for u in range(2)
     ]
+    clear_pads(pbuf)
     ready()
-    clear_pads(pbuf)
     for u in range(2):
         for j in range(3):
             for g in range(4):
@@ -132,7 +133,7 @@
         moved = None
         tail = jnp.zeros((n, 2 * CH), f32)
         for j, dx in enumerate(steps):
-            shift, ox, _, _ = pixel_shift(sy[u], dx, row, col, row_ref, col_ref, rows, cols)
+            shift, ox = pixel_shift(sy[u], dx, geo)
             first = (PAD - 1 - (shift >> 1)) * CH
             stack = jnp.concatenate(
                 [
@@ -148,11 +149,8 @@
     return out
 
 
-def fetch(row_in, col_in, row_ref, col_ref, sem):
-    loads = (
-        pltpu.make_async_copy(row_in, row_ref, sem.at[0]),
-        pltpu.make_async_copy(col_in, col_ref, sem.at[1]),
-    )
+def begin(*copies):
+    loads = [pltpu.make_async_copy(*copy) for copy in copies]
     for load in loads:
         load.start()
 
@@ -191,7 +189,10 @@
     return g, j - 3 * g
 
 
-def pack_kernel(foot, tail, xa, xb, va, vb):
+def pack_kernel(foot, tr, xa, xb, va, vb, src, trs, sem):
+    ready = begin(
+        (foot.at[0:32, :], src, sem.at[0]), (tr.at[0:32, :], trs, sem.at[1])
+    )
     _, _, sy, sx = sides()
     j = iota((16, 160), 0)
     kk = iota((16, 160), 1)
@@ -202,75 +203,120 @@
     def pick(d):
         return hot(same & (comp == 3 * d))
 
-    last = tail[...]
-    send_all(pick, foot.at[0:32, :], last, last, (xa, xb, va, vb), sy, sx)
-
-
-def slot_masks(table, total):
-    own = table[:, 0:1]
-    idx = NBR * table[:, 1:2] + table[:, 2:3]
-    live = iota((MP, 1), 0) < total
-    return own, idx, live
-
-
-def slot_select(table, total):
-    ids, idx, live = slot_masks(table, total)
+    ready()
+    tail = jnp.concatenate([trs[...], jnp.zeros((32, 2 * CH), bf16)], axis=1)
+    send_all(pick, src, tail, tail, (xa, xb, va, vb), sy, sx)
+
+
+def slot_select(table):
     j5 = iota((5 * MP, 16), 1)
     g5 = iota((5 * MP, 16), 0) >> 4
     s5 = j5 - 3 * g5
-    idx5 = jnp.concatenate([jnp.where(live, idx, -100)] * 5, axis=0)
+    idx5 = jnp.concatenate([table[:, 1:2]] * 5, axis=0)
     fits = (s5 >= 0) & (s5 < 3)
 
     def select(d):
         return hot(fits & (idx5 == 3 * d + s5))
 
-    return ids, live, select
+    return select
 
 
 NT = (((1,), (1,)), ((), ()))
 
 
-def own_kernel(count, res, foot, tr, table, rest, first, own, ctr):
-    ids, _, _ = slot_masks(table, count[...])
-    own_hot = hot(ids == iota((MP, K), 1))
-    c_own = dot(own_hot, tr[...])
-    ctr[...] = c_own
+HALF = NPIX // 2
+
+
+def load_half(res_in, start, res, sem):
+    width = 512
+    return [
+        begin(
+            (
+                res_in.at[start + width * n : start + width * (n + 1), :],
+                res.at[width * n : width * (n + 1), :],
+                sem.at[n],
+            )
+        )
+        for n in range(HALF // width)
+    ]
+
+
+def turn_half(loads, c_own, res, rest, first):
+    width = 512
     eye = hot(iota((CH, CH), 0) == iota((CH, CH), 1))
     both = jnp.concatenate([c_own.astype(bf16), eye], axis=0)
-    width = 512
-    for n in range(NPIX // width):
+    for n, load in enumerate(loads):
         lanes = slice(width * n, width * (n + 1))
-        own[:, lanes] = dot(own_hot, foot[:, lanes])
+        load()
         turned = lax.dot_general(both, res[lanes, :], NT, preferred_element_type=f32)
         first[:, lanes] = turned[0:MP]
         rest[:, lanes] = turned[MP:].astype(bf16)
 
 
-def side_kernel(rows, cols, row_ref, col_ref, count, table, rxa, rxb, side, crem):
-    row, col, _, sx = sides()
-    _, _, select = slot_select(table, count[...])
-    whole, tail = receive_sides(
-        select, MP, (rxa, rxb), row, col, sx, row_ref, col_ref, rows, cols
+def own_kernel(
+    rows, cols, count, row_in, col_in, res_in, tr_in, table, wide,
+    res, rest, first, ctr, slots, across, geo, tr, row_ref, col_ref, sem, rsem,
+):
+    small = begin((tr_in, tr, sem.at[0]))
+    loads = load_half(res_in, 0, res, rsem)
+    scalars = begin((row_in, row_ref, sem.at[1]), (col_in, col_ref, sem.at[2]))
+    row, col, _, _ = sides()
+    total = count[0, 0]
+    ids = table[:, 0:1]
+    live = iota((MP, CH), 0) < total
+    idx = NBR * table[:, 1:2] + table[:, 2:3]
+    place = iota((MP, CH), 1)
+    dead = jnp.where(live, jnp.where(place == 0, ids, idx), -100)
+    slots[...] = jnp.where(place == 2, ids, dead)
+    line = iota((8, CH), 0)
+    alive = (iota((8, CH), 1) & 15) < total
+    pair = NBR * wide[1:2, :] + wide[2:3, :]
+    across[...] = jnp.where(alive, jnp.where(line == 0, wide[0:1, :], pair), -100)
+    own_hot = hot(ids == iota((MP, K), 1))
+    small()
+    c_own = dot(own_hot, tr[...])
+    ctr[...] = c_own
+    turn_half(loads, c_own, res, rest, first)
+    scalars()
+    up = row_ref[jnp.clip(row - 1, 0, rows - 2)]
+    down = row_ref[jnp.clip(row, 0, rows - 2)]
+    left = col_ref[jnp.clip(col - 1, 0, cols - 2)]
+    right = col_ref[jnp.clip(col, 0, cols - 2)]
+    lane = iota((1, CH), 1)
+    geo[...] = jnp.where(
+        lane == 0, up, jnp.where(lane == 1, down, jnp.where(lane == 2, left, right))
     )
+
+
+def side_kernel(
+    res_in, foot_in, geo_in, ctr, slots, rxa, rxb, res, rest, first, own, side, crem, foot, geo, sem, rsem
+):
+    loads = load_half(res_in, HALF, res, rsem)
+    load = begin((foot_in, foot, sem.at[1]))
+    ready = begin((geo_in, geo, sem.at[0]))
+    _, _, _, sx = sides()
+    own_hot = hot(slots[:, 2:3] == iota((MP, K), 1))
+    whole, tail = receive_sides(slot_select(slots), MP, (rxa, rxb), sx, geo, ready)
     crem[...] = tail[:, 0:F]
     for m in range(32):
         side[:, CH * m : CH * (m + 1)] = whole[MP * m : MP * (m + 1)]
+    turn_half(loads, ctr[...], res, rest, first)
+    load()
+    own[...] = dot(own_hot, foot[...])
 
 
 def refit_kernel(
-    rows, cols, row_in, col_in, count, res, rest, first, own, ctr, side, crem, table, wide, rya, ryb,
-    xa, xb, va, vb, merged, mtrace, acc, pbuf, row_ref, col_ref, sem,
+    geo_in, res_l, rest_l, first_l, ctr, slots, wide, res_h, rest_h, first_h, own, side, crem, rya, ryb,
+    xa, xb, va, vb, merged, mtrace, acc, pbuf, geo, sem,
 ):
-    ready = fetch(row_in, col_in, row_ref, col_ref, sem)
-    row, col, sy, sx = sides()
-    total = count[...]
-    _, live, select = slot_select(table, total)
+    ready = begin((geo_in, geo, sem.at[0]))
+    _, _, sy, sx = sides()
+    live = slots[:, 1:2] >= 0
+    select = slot_select(slots)
     acc[...] = side[...]
     c_own = ctr[...]
     c_rem = crem[...]
-    bands = receive_bands(
-        (select, select), MP, (rya, ryb), pbuf, row, col, sy, sx, row_ref, col_ref, rows, cols, ready
-    )
+    bands = receive_bands((select, select), MP, (rya, ryb), pbuf, sy, sx, geo, ready)
     for u, (moved, tail) in enumerate(bands):
         c_rem = c_rem + tail[:, 0:F]
         start = band_start(sy[u])
@@ -285,10 +331,11 @@
         cr = jnp.sum(c_rem * trace, axis=1, keepdims=True)
         scale = 1.0 / (jnp.sum(trace * trace, axis=1, keepdims=True) + epsilon * F)
         lanes = [slice(step * n, step * (n + 1)) for n in range(NPIX // step)]
+        halves = [slice(step * n, step * (n + 1)) for n in range(HALF // step)]
         if it == 0:
-            across = [first[:, cut] for cut in lanes]
+            across = [f[:, cut] for f in (first_l, first_h) for cut in halves]
         else:
-            across = [dot(tb, rest[:, cut]) for cut in lanes]
+            across = [dot(tb, r[:, cut]) for r in (rest_l, rest_h) for cut in halves]
         sa = jnp.zeros((MP, CH), f32)
         sr = jnp.zeros((MP, CH), f32)
         ss = jnp.zeros((MP, CH), f32)
@@ -308,7 +355,8 @@
                 sa = sa + pa[:, part]
                 sr = sr + pr[:, part]
                 ss = ss + ps[:, part]
-        down = sum(dot(shapes[n], res[cut, :]) for n, cut in enumerate(lanes))
+        parts = [r[cut, :] for r in (res_l, res_h) for cut in halves]
+        down = sum(dot(now, part) for now, part in zip(shapes, parts))
         down = (
             down
             + c_own * jnp.sum(sa, axis=1, keepdims=True)
@@ -320,9 +368,8 @@
     j = iota((16, 5 * MP), 0)
     kk = iota((16, 5 * MP), 1)
     g, s = group_of(j)
-    slot = kk & 15
-    same = ((kk >> 4) == g) & (j < 15) & (slot < total)
-    comp = NBR * wide[1:2, :] + wide[2:3, :] - s
+    same = ((kk >> 4) == g) & (j < 15)
+    comp = wide[1:2, 0 : 5 * MP] - s
 
     def pick(d):
         return hot(same & (comp == 3 * d))
@@ -333,8 +380,7 @@
     send_all(pick, merged, tail, tail, (xa, xb, va, vb), sy, sx)
 
 
-def corr_kernel(comp, tr, rxa, rxb, rya, ryb, out):
-    _, _, sy, sx = sides()
+def correlate(alive, tr, rxa, rxb, rya, ryb, out, sy, sx):
     k = iota((BORDER, 16), 0)
     j = iota((BORDER, 16), 1)
     s = j - 12
@@ -346,7 +392,7 @@
     for u, ref in enumerate((rya, ryb)):
         for q, dx in enumerate((0, sx[0], sx[1])):
             z = z + dot(hot(fits & (k == 3 * direction(sy[u], dx) + s)), ref[:, CW * q : CW * q + F])
-    x = tr[...].astype(f32)
+    x = tr.astype(f32)
     x = x - jnp.mean(x, axis=1, keepdims=True)
     z = z - jnp.mean(z, axis=1, keepdims=True)
     high = lax.Precision.HIGHEST
@@ -354,7 +400,6 @@
     vz = jnp.mean(z * z, axis=1, keepdims=True)
     ones = jnp.ones((8, F), f32)
     vx = lax.dot_general(ones, x * x, NT, precision=high, preferred_element_type=f32)[0:1] / F
-    alive = iota((1, K), 1) < comp[...]
     out[...] = jnp.where(alive, cov / jnp.sqrt((vx + epsilon) * (vz + epsilon)), 0.0)
 
 
@@ -372,28 +417,25 @@
 
 
 def before_kernel(
-    rows, cols, row_ref, col_ref, count, compc, foot, tr, wide, merged, mtrace, rxa, rxb,
-    base, tbase, upper, lower,
+    comp, foot_in, tr_in, geo_in, wide, merged, mtrace, oxa, oxb, oya, oyb, rxa, rxb,
+    base, tbase, upper, lower, corr, foot, tr, geo, sem,
 ):
-    row, col, _, sx = sides()
+    quick = begin((geo_in, geo, sem.at[0]))
+    ready = begin((tr_in, tr, sem.at[1]), (foot_in, foot, sem.at[2]))
+    _, _, sy, sx = sides()
     n = 16
-    whole, tail = receive_sides(
-        row_select(n, 8), n, (rxa, rxb), row, col, sx, row_ref, col_ref, rows, cols
-    )
+    whole, tail = receive_sides(row_select(n, 8), n, (rxa, rxb), sx, geo, quick)
     flag = tail[:, CH : CH + 1] > 0.5
     k = iota((n, 1), 0) + 8
-    _, _, _, c_lf = pixel_shift(0, -1, row, col, row_ref, col_ref, rows, cols)
-    _, _, _, c_rt = pixel_shift(0, 1, row, col, row_ref, col_ref, rows, cols)
-    x_lo = jnp.where(k >= 12, PW - c_rt, 0)
-    x_hi = jnp.where(flag, jnp.where(k < 12, c_lf, PW), 0)
+    x_lo = jnp.where(k >= 12, PW - geo[0, 3], 0)
+    x_hi = jnp.where(flag, jnp.where(k < 12, geo[0, 2], PW), 0)
     x = iota((1, CH), 1) & (PW - 1)
     inside = (x >= x_lo) & (x < x_hi)
-    total = count[...]
-    own_id = wide[0:1, 0:MP]
-    own_mask = (iota((K - BORDER, MP), 0) + BORDER == own_id) & (iota((K - BORDER, MP), 1) < total)
-    own_hot = hot(own_mask)
+    own_hot = hot(iota((K - BORDER, MP), 0) + BORDER == wide[0:1, 0:MP])
     hit = jnp.sum(own_hot.astype(f32), axis=1, keepdims=True) > 0.5
-    alive = iota((K - BORDER, 1), 0) + BORDER < compc[...]
+    ready()
+    correlate(iota((1, K), 1) < comp[0, 0], tr[...], oxa, oxb, oya, oyb, corr, sy, sx)
+    alive = iota((K - BORDER, 1), 0) + BORDER < comp[0, 0]
     step = 512
     for b in range(NPIX // step):
         lanes = slice(step * b, step * (b + 1))
@@ -421,30 +463,32 @@
 
 
 def final_kernel(
-    rows, cols, row_in, col_in, base, tbase, upper, lower, rya, ryb,
-    nfoot, ntrace, placed, tails, pbuf, out, row_ref, col_ref, sem,
+    geo_in, base, tbase, upper, lower, rya, ryb,
+    nfoot, ntrace, placed, tails, pbuf, out, tout, geo, sem,
 ):
-    ready = fetch(row_in, col_in, row_ref, col_ref, sem)
-    row, col, sy, sx = sides()
+    ready = begin((geo_in, geo, sem.at[0]))
+    _, _, sy, sx = sides()
     n = 16
     downs = [jnp.where(sy[u] > 0, 1, 0) for u in range(2)]
     bands = receive_bands(
-        [row_select(n, 8 * dn) for dn in downs],
-        n, (rya, ryb), pbuf, row, col, sy, sx, row_ref, col_ref, rows, cols, ready,
+        [row_select(n, 8 * dn) for dn in downs], n, (rya, ryb), pbuf, sy, sx, geo, ready
     )
     for dn, (moved, tail) in zip(downs, bands):
         for m in range(12):
             placed[dn, :, CH * m : CH * (m + 1)] = moved[n * m : n * (m + 1)]
         tails[dn] = tail
-    _, _, r_up, _ = pixel_shift(-1, 0, row, col, row_ref, col_ref, rows, cols)
-    _, _, r_dn, _ = pixel_shift(1, 0, row, col, row_ref, col_ref, rows, cols)
-    _, _, _, c_lf = pixel_shift(0, -1, row, col, row_ref, col_ref, rows, cols)
-    _, _, _, c_rt = pixel_shift(0, 1, row, col, row_ref, col_ref, rows, cols)
+    mine = tbase[0:BORDER]
+    gap = jnp.zeros((8, 2 * CH), f32)
+    both = jnp.concatenate([tails[0], gap], axis=0) + jnp.concatenate([gap, tails[1]], axis=0)
+    top = jnp.where(both[:, CH : CH + 1] > 0.5, both[:, 0:F], mine)
+    tout[...] = jnp.concatenate([top, tbase[BORDER:]], axis=0).astype(bf16)
+    copies = [pltpu.make_async_copy(tout, ntrace, sem.at[1])]
+    copies[0].start()
+    r_up, r_dn, c_lf, c_rt = (geo[0, i] for i in range(4))
     k = iota((n, 1), 0)
     pix = iota((1, BAND), 1)
     y = pix >> 6
     x = pix & (PW - 1)
-    copies = []
     for dn, edge in enumerate((upper, lower)):
         j = k - 7 * dn
         flag = tails[dn, :, CH : CH + 1] > 0.5
@@ -461,11 +505,6 @@
             )
         )
         copies[-1].start()
-    mine = tbase[0:BORDER]
-    gap = jnp.zeros((8, 2 * CH), f32)
-    both = jnp.concatenate([tails[0], gap], axis=0) + jnp.concatenate([gap, tails[1]], axis=0)
-    top = jnp.where(both[:, CH : CH + 1] > 0.5, both[:, 0:F], mine)
-    ntrace[...] = jnp.concatenate([top, tbase[BORDER:]], axis=0).astype(bf16)
     for copy in copies:
         copy.wait()
 
@@ -521,94 +560,108 @@
     foot = footprints[0, 0]
     tr = traces[0, 0]
     table = merge_pairs[0, 0]
-    wide = jnp.tile(table.T, (1, 5))
+    wide = jnp.tile(table.T, (1, CH // MP))
     rows, cols = lax.axis_size("py"), lax.axis_size("px")
-
-    def geo(kernel):
-        def run(*refs):
-            kernel(rows, cols, *refs)
-
-        return run
+    res, foot, tr, row_far, col_far = (
+        pltpu.with_memory_space_constraint(v, pltpu.HBM)
+        for v in (res, foot, tr, row_inter, col_inter)
+    )
+    dma = pltpu.SemaphoreType.DMA
+    i32 = jnp.int32
+    geo_scratch = [pltpu.SMEM((1, CH), i32), dma((1,))]
 
     packets = call(
-        pack_kernel, PACKETS, [VMEM] * 2, (VMEM,) * 4, [], 1 << 24
-    )(foot, jnp.pad(tr[:32], ((0, 0), (0, 2 * CH))))
+        pack_kernel,
+        PACKETS,
+        [HBM] * 2,
+        (VMEM,) * 4,
+        [pltpu.VMEM((32, NPIX), bf16), pltpu.VMEM((32, F), bf16), dma((2,))],
+        1 << 24,
+    )(foot, tr)
     rxa, rxb, rya, ryb = exchange(*packets)
 
-    prepared = call(
-        own_kernel,
-        (
-            shape(F, NPIX),
-            shape(MP, NPIX, dtype=f32),
-            shape(MP, NPIX, dtype=f32),
+    def own(*refs):
+        own_kernel(rows, cols, *refs)
+
+    half = (shape(HALF, F), shape(F, HALF), shape(MP, HALF, dtype=f32))
+    *prepared, slots, across, geo = call(
+        own,
+        half
+        + (
             shape(MP, F, dtype=f32),
+            shape(MP, CH, dtype=i32),
+            shape(8, CH, dtype=i32),
+            shape(1, CH, dtype=i32),
         ),
-        [VMEM] * 5,
-        (VMEM,) * 4,
-        [],
+        [SMEM] + [HBM] * 4 + [VMEM] * 2,
+        (VMEM,) * 7,
+        [
+            pltpu.VMEM((K, F), bf16),
+            pltpu.SMEM((rows - 1,), i32),
+            pltpu.SMEM((cols - 1,), i32),
+            dma((3,)),
+            dma((4,)),
+        ],
         1 << 24,
-    )(pair_counts, res, foot, tr, table)
+    )(pair_counts, row_far, col_far, res, tr, table, wide)
 
     placed = call(
-        geo(side_kernel),
-        (shape(MP, NPIX, dtype=f32), shape(MP, F, dtype=f32)),
-        [SMEM] * 2 + [VMEM] * 4,
-        (VMEM,) * 2,
-        [],
+        side_kernel,
+        half
+        + (shape(MP, NPIX, dtype=f32), shape(MP, NPIX, dtype=f32), shape(MP, F, dtype=f32)),
+        [HBM] * 2 + [VMEM] * 5,
+        (VMEM,) * 6,
+        [pltpu.VMEM((K, NPIX), bf16), pltpu.SMEM((1, CH), i32), dma((2,)), dma((4,))],
         1 << 24,
-    )(row_inter, col_inter, pair_counts, table, rxa, rxb)
+    )(res, foot, geo, prepared[-1], slots, rxa, rxb)
 
     xa, xb, va, vb, merged, mtrace = call(
-        geo(refit_kernel),
+        refit_kernel,
         PACKETS + (shape(MP, NPIX), shape(MP, F)),
-        [VMEM] * 14,
+        [VMEM] * 15,
         (VMEM,) * 6,
-        [
-            pltpu.VMEM((MP, NPIX), f32),
-            pltpu.VMEM((6, MP, PBW), bf16),
-            pltpu.SMEM((rows - 1,), jnp.int32),
-            pltpu.SMEM((cols - 1,), jnp.int32),
-            pltpu.SemaphoreType.DMA((2,)),
-        ],
+        [pltpu.VMEM((MP, NPIX), f32), pltpu.VMEM((6, MP, PBW), bf16)] + geo_scratch,
         1 << 28,
-    )(row_inter, col_inter, pair_counts, res, *prepared, *placed, table, wide, rya, ryb)
-    back = exchange(xa, xb, va, vb)
-
-    corr = call(
-        corr_kernel, shape(BORDER, K, dtype=f32), [VMEM] * 6, VMEM, [], 1 << 22
-    )(comp_counts, tr, rxa, rxb, rya, ryb)
-
-    partial = call(
-        geo(before_kernel),
+    )(geo, *prepared, slots, across, *placed, rya, ryb)
+    oxa, oxb, oya, oyb = exchange(xa, xb, va, vb)
+
+    *partial, corr = call(
+        before_kernel,
         (
             shape(K, NPIX),
             shape(K, F, dtype=f32),
             shape(16, BAND, dtype=f32),
             shape(16, BAND, dtype=f32),
+            shape(BORDER, K, dtype=f32),
         ),
-        [SMEM] * 2 + [VMEM] * 9,
-        (VMEM,) * 4,
-        [],
+        [SMEM] + [HBM] * 2 + [VMEM] * 10,
+        (VMEM,) * 5,
+        [
+            pltpu.VMEM((K, NPIX), bf16),
+            pltpu.VMEM((K, F), bf16),
+            pltpu.SMEM((1, CH), i32),
+            dma((3,)),
+        ],
         1 << 24,
-    )(row_inter, col_inter, pair_counts, comp_counts, foot, tr, wide, merged, mtrace, *back[:2])
+    )(comp_counts, foot, tr, geo, across, merged, mtrace, rxa, rxb, rya, ryb, oxa, oxb)
 
     nfoot, ntrace = call(
-        geo(final_kernel),
+        final_kernel,
         (shape(K, NPIX), shape(K, F)),
-        [VMEM] * 2 + [HBM] + [VMEM] * 5,
-        (HBM, VMEM),
+        [VMEM, HBM] + [VMEM] * 5,
+        (HBM, HBM),
         [
             pltpu.VMEM((2, 16, BAND), f32),
             pltpu.VMEM((2, 16, 2 * CH), f32),
             pltpu.VMEM((6, 16, PBW), bf16),
             pltpu.VMEM((2, 16, BAND), bf16),
-            pltpu.SMEM((rows - 1,), jnp.int32),
-            pltpu.SMEM((cols - 1,), jnp.int32),
-            pltpu.SemaphoreType.DMA((4,)),
+            pltpu.VMEM((K, F), bf16),
+            pltpu.SMEM((1, CH), i32),
+            dma((4,)),
         ],
         1 << 26,
-        {2: 0},
-    )(row_inter, col_inter, *partial, *back[2:])
+        {1: 0},
+    )(geo, *partial, oya, oyb)
     return nfoot[None, None], ntrace[None, None], corr.T[None, None]
 
 

time: 61.8 us -> 58.3 us (0.943)
  local copies, waits for them, and re-layouts: 3.73 us -> 0.19 us
  waiting for transfers between devices: 8.47 us -> 7.11 us
  Pallas kernels: 10.4 us -> 11.7 us
    unnamed x17 -> x3, local copies, waits for them, and re-layouts: 2.84 us -> 0.01 us
    pallas_call x7 -> x6, Pallas kernels: 10.4 us -> 11.7 us  [the longest x1 2.69 us: body(): call(refit_kernel, PACKETS + (shape(MP, NPIX), shape(MP, F)), [VMEM] * 15...]
    ppermute x8, waiting for transfers between devices: 8.47 us -> 7.11 us  [swap(): return lax.ppermute(value, axis, pairs)]
    slice x1 -> x0, local copies, waits for them, and re-layouts: 0.7 us -> none  [body(): tr[:32]]
  transfers between devices with their start and end apart: 8 -> 8, of which waited for: 3 -> 2; matrix products, arithmetic and copies ran while one was open for 0% -> 0% of each run, Pallas kernels for 8% -> 11%
where the time goes in v3:
time: 58.3 us; the launch traced here: 57.9 us
  starting transfers between devices  36.6 us (63%)
  Pallas kernels  11.7 us (20%)
  waiting for transfers between devices  7.11 us (12%)
  between operations  2.15 us (4%)
    ppermute x8, starting transfers between devices, swap(): return lax.ppermute(value, axis, pairs)  36.6 us
    ppermute x8, waiting for transfers between devices, swap(): return lax.ppermute(value, axis, pairs)  7.11 us
    pallas_call x1, Pallas kernels, body(): call(refit_kernel, PACKETS + (shape(MP, NPIX), shape(MP, F)), [VMEM] * 15...  2.69 us
    pallas_call x1, Pallas kernels, body(): call(before_kernel, (shape(K, NPIX), shape(K, F, dtype=f32), shape(16, BA...  2.29 us
    pallas_call x1, Pallas kernels, body(): call(side_kernel, half + (shape(MP, NPIX, dtype=f32), shape(MP, NPIX, dty...  2.02 us
    pallas_call x1, Pallas kernels, body(): call(own, half + (shape(MP, F, dtype=f32), shape(MP, CH, dtype=i32), shap...  1.81 us
    pallas_call x1, Pallas kernels, body(): call(final_kernel, (shape(K, NPIX), shape(K, F)), [VMEM, HBM] + [VMEM] *...  1.65 us
    pallas_call x1, Pallas kernels, body(): call(pack_kernel, PACKETS, [HBM] * 2, (VMEM,) * 4, [pltpu.VMEM((32, NPIX)...  1.29 us
  transfers between devices with their start and end apart: 8, of which 2 were waited for; matrix products, arithmetic and copies ran while one was open for 0% of the time, Pallas kernels for 11%

profile of v3, /device:TPU:57, one launch (start us, length us, event | category | flops | bytes accessed | tf_op | source)
XLA Modules:
  0.0 57.9 jit_solution(1441120579094884114)
XLA Ops:
  0.6 1.3 %shard_map.104 = (bf16[16,1664]{1,0:T(8,128)(2,1)S(1)}, bf16[16,1664]{1,0:T(8,128)(2,1)S(1)}, bf16[16,384]{1,0:T(8,128)(2,1)S(1)}, bf16[16,384]{1,0:T(8,128)(2,1)S(1)}) custom-call(bf16[40,4096]{1,0:T(8,128)(2,1)} %bitcast.16, bf16[40,128]{1,0:T(8,128)(2,1)} %bitcast.20), custom_call_target="tpu_custom_call" | custom-call | flops 16777216 | bytes 1048576 | tf_op jit(solution)/shard_map/pallas_call | solution.py:573
  1.9 2.6 %collective-permute-start = (bf16[16,1664]{1,0:T(8,128)(2,1)S(1)}, bf16[16,1664]{1,0:T(8,128)(2,1)S(1)}, u32[]{:S(2)}, u32[]{:S(2)}) collective-permute-start(bf16[16,1664]{1,0:T(8,128)(2,1)S(1)} %get-tuple-element.40), channel_id=1, source_target_pairs={{0,1},{1,0},{2,3},{3,2},{4,5},{5,4},{6,7},{7,6},{8,9},{9,8},{10,11... | collective-permute-start | bytes 159752 | tf_op jit(solution)/shard_map/ppermute | solution.py:543
  4.5 5.4 %collective-permute-start.1 = (bf16[16,1664]{1,0:T(8,128)(2,1)S(1)}, bf16[16,1664]{1,0:T(8,128)(2,1)S(1)}, u32[]{:S(2)}, u32[]{:S(2)}) collective-permute-start(bf16[16,1664]{1,0:T(8,128)(2,1)S(1)} %get-tuple-element.41), channel_id=1, source_target_pairs={{1,2},{2,1},{3,4},{4,3},{5,6},{6,5},{7,8},{8,7},{9,10},{10,9},{11,... | collective-permute-start | bytes 159752 | tf_op jit(solution)/shard_map/ppermute | solution.py:543
  9.9 0.0 collective-permute-done.rxa.oxa
  9.9 2.7 %collective-permute-done.1.rxb.oxb = bf16[16,1664]{1,0:T(8,128)(2,1)S(1)} collective-permute-done((bf16[16,1664]{1,0:T(8,128)(2,1)S(1)}, bf16[16,1664]{1,0:T(8,128)(2,1)S(1)}, u32[]{:S(2)}, u32[]{:S(2)}) %collective-permute-start.1) | collective-permute-done | bytes 53280 | tf_op jit(solution)/shard_map/ppermute | solution.py:543
  12.7 4.0 %collective-permute-start.2 = (bf16[16,1152]{1,0:T(8,128)(2,1)S(1)}, bf16[16,1152]{1,0:T(8,128)(2,1)S(1)}, u32[]{:S(2)}, u32[]{:S(2)}) collective-permute-start(bf16[16,1152]{1,0:T(8,128)(2,1)S(1)} %pad_maximum_fusion), channel_id=1, source_target_pairs={{0,32},{32,0},{64,96},{96,64},{128,160},{160,128},{192,224},{224,1... | collective-permute-start | bytes 110600 | tf_op jit(solution)/shard_map/ppermute | solution.py:543
  16.7 0.0 copy-start
  16.7 11.1 %collective-permute-start.3 = (bf16[16,1152]{1,0:T(8,128)(2,1)S(1)}, bf16[16,1152]{1,0:T(8,128)(2,1)S(1)}, u32[]{:S(2)}, u32[]{:S(2)}) collective-permute-start(bf16[16,1152]{1,0:T(8,128)(2,1)S(1)} %pad_maximum_fusion.1), channel_id=1, source_target_pairs={{32,64},{64,32},{96,128},{128,96},{160,192},{192,160},{224,256},{2... | collective-permute-start | bytes 110600 | tf_op jit(solution)/shard_map/ppermute | solution.py:543
  27.8 0.0 copy-done
  27.8 0.1 tile.10.refs_6_
  27.9 0.1 copy.12.refs_5_
  28.7 1.8 %shard_map.103 = (bf16[2048,128]{1,0:T(8,128)(2,1)S(1)}, bf16[128,2048]{1,0:T(8,128)(2,1)S(1)}, f32[16,2048]{1,0:T(8,128)S(1)}, f32[16,128]{1,0:T(8,128)S(1)}, s...) custom-call(s32[1,1]{1,0:T(1,128)S(6)} %copy.18.refs_0_, s32[15]{0:T(128)} %refs_1_.1, ...), custom_call_target="tpu_custom_call" | custom-call | flops 16777216 | bytes 1048576 | tf_op jit(solution)/shard_map/pallas_call | solution.py:587
  30.5 2.0 %shard_map.105 = (bf16[2048,128]{1,0:T(8,128)(2,1)S(1)}, bf16[128,2048]{1,0:T(8,128)(2,1)S(1)}, f32[16,2048]{1,0:T(8,128)S(1)}, f32[16,4096]{1,0:T(8,128)S(1)}, ...) custom-call(bf16[4096,128]{1,0:T(8,128)(2,1)} %bitcast.15, bf16[40,4096]{1,0:T(8,128)(2,1)} %bitcast.17, ...), custom_call_target="tpu_custom_call" | custom-call | flops 16777216 | bytes 1048576 | tf_op jit(solution)/shard_map/pallas_call | solution.py:608
  32.5 0.0 collective-permute-done.2.rya.oya
  32.5 0.0 collective-permute-done.3.ryb.oyb
  32.5 2.7 %shard_map.106 = (bf16[16,1664]{1,0:T(8,128)(2,1)S(1)}, bf16[16,1664]{1,0:T(8,128)(2,1)S(1)}, bf16[16,384]{1,0:T(8,128)(2,1)S(1)}, bf16[16,384]{1,0:T(8,128)(2,1...) custom-call(s32[1,128]{1,0:T(1,128)S(1)} %get-tuple-element.33.geo_in, ...), custom_call_target="tpu_custom_call" | custom-call | flops 268435456 | bytes 1048576 | tf_op jit(solution)/shard_map/pallas_call | solution.py:618
  35.2 1.9 %collective-permute-start.4 = (bf16[16,1664]{1,0:T(8,128)(2,1)S(1)}, bf16[16,1664]{1,0:T(8,128)(2,1)S(1)}, u32[]{:S(2)}, u32[]{:S(2)}) collective-permute-start(bf16[16,1664]{1,0:T(8,128)(2,1)S(1)} %get-tuple-element.52), channel_id=1, source_target_pairs={{0,1},{1,0},{2,3},{3,2},{4,5},{5,4},{6,7},{7,6},{8,9},{9,8},{10,11... | collective-permute-start | bytes 159752 | tf_op jit(solution)/shard_map/ppermute | solution.py:543
  37.1 3.8 %collective-permute-start.5 = (bf16[16,1664]{1,0:T(8,128)(2,1)S(1)}, bf16[16,1664]{1,0:T(8,128)(2,1)S(1)}, u32[]{:S(2)}, u32[]{:S(2)}) collective-permute-start(bf16[16,1664]{1,0:T(8,128)(2,1)S(1)} %get-tuple-element.53), channel_id=1, source_target_pairs={{1,2},{2,1},{3,4},{4,3},{5,6},{6,5},{7,8},{8,7},{9,10},{10,9},{11,... | collective-permute-start | bytes 159752 | tf_op jit(solution)/shard_map/ppermute | solution.py:543
  40.9 0.0 collective-permute-done.4.rxa
  41.0 4.3 %collective-permute-done.5.rxb = bf16[16,1664]{1,0:T(8,128)(2,1)S(1)} collective-permute-done((bf16[16,1664]{1,0:T(8,128)(2,1)S(1)}, bf16[16,1664]{1,0:T(8,128)(2,1)S(1)}, u32[]{:S(2)}, u32[]{:S(2)}) %collective-permute-start.5) | collective-permute-done | bytes 53280 | tf_op jit(solution)/shard_map/ppermute | solution.py:543
  45.3 6.0 %collective-permute-start.7 = (bf16[16,1152]{1,0:T(8,128)(2,1)S(1)}, bf16[16,1152]{1,0:T(8,128)(2,1)S(1)}, u32[]{:S(2)}, u32[]{:S(2)}) collective-permute-start(bf16[16,1152]{1,0:T(8,128)(2,1)S(1)} %pad_maximum_fusion.3), channel_id=1, source_target_pairs={{32,64},{64,32},{96,128},{128,96},{160,192},{192,160},{224,256},{2... | collective-permute-start | bytes 110600 | tf_op jit(solution)/shard_map/ppermute | solution.py:543
  51.3 1.9 %collective-permute-start.6 = (bf16[16,1152]{1,0:T(8,128)(2,1)S(1)}, bf16[16,1152]{1,0:T(8,128)(2,1)S(1)}, u32[]{:S(2)}, u32[]{:S(2)}) collective-permute-start(bf16[16,1152]{1,0:T(8,128)(2,1)S(1)} %pad_maximum_fusion.2), channel_id=1, source_target_pairs={{0,32},{32,0},{64,96},{96,64},{128,160},{160,128},{192,224},{224,1... | collective-permute-start | bytes 110600 | tf_op jit(solution)/shard_map/ppermute | solution.py:543
  53.9 2.3 %shard_map.107 = (bf16[40,4096]{1,0:T(8,128)(2,1)}, f32[40,128]{1,0:T(8,128)S(1)}, f32[16,1536]{1,0:T(8,128)S(1)}, f32[16,1536]{1,0:T(8,128)S(1)}, f32[24,40]{1,0:T(8,128)}) custom-call(s32[1,1]{1,0:T(1,128)S(6)} %copy.19.comp, bf16[40,4096]{1,0:T(8,128)(2,1)} %bitcast.18, bf16[40,128]{1,0:T(8,128)(2,1)} %bitcast.22, s32[1,128]{1,0:T(1,128)S(1)} %get-tuple-element.33.geo_in, ...), custom_call_target="tpu_custom_call" | custom-call | flops 16777216 | bytes 1048576 | tf_op jit(solution)/shard_map/pallas_call | solution.py:628
  56.2 0.0 collective-permute-done.7.ryb
  56.2 0.0 collective-permute-done.6.rya
  56.2 1.6 %shard_map.108 = (bf16[40,4096]{1,0:T(8,128)(2,1)}, bf16[40,128]{1,0:T(8,128)(2,1)}) custom-call(s32[1,128]{1,0:T(1,128)S(1)} %get-tuple-element.33.geo_in, bf16[40,4096]{1,0:T(8,128)(2,1)} %get-tuple-element.54.base, f32[40,128]{1,0:T(8,128)S(1)} %get-tuple-element.55.tbase, ...), custom_call_target="tpu_custom_call", output_to_operand_aliasing={{0}: (1, {})} | custom-call | flops 67108864 | bytes 1048576 | tf_op jit(solution)/shard_map/pallas_call | solution.py:648
  (10 shorter events, 0.0 us)
Async XLA Ops:
  1.9 8.0 %collective-permute-start = (bf16[16,1664]{1,0:T(8,128)(2,1)S(1)}, bf16[16,1664]{1,0:T(8,128)(2,1)S(1)}, u32[]{:S(2)}, u32[]{:S(2)}) collective-permute-start(bf16[16,1664]{1,0:T(8,128)(2,1)S(1)} %get-tuple-element.40), channel_id=1, source_target_pairs={{0,1},{1,0},{2,3},{3,2},{4,5},{5,4},{6,7},{7,6},{8,9},{9,8},{10,11... | collective-permute-start | bytes 159752 | tf_op jit(solution)/shard_map/ppermute | solution.py:543
  4.5 8.2 %collective-permute-start.1 = (bf16[16,1664]{1,0:T(8,128)(2,1)S(1)}, bf16[16,1664]{1,0:T(8,128)(2,1)S(1)}, u32[]{:S(2)}, u32[]{:S(2)}) collective-permute-start(bf16[16,1664]{1,0:T(8,128)(2,1)S(1)} %get-tuple-element.41), channel_id=1, source_target_pairs={{1,2},{2,1},{3,4},{4,3},{5,6},{6,5},{7,8},{8,7},{9,10},{10,9},{11,... | collective-permute-start | bytes 159752 | tf_op jit(solution)/shard_map/ppermute | solution.py:543
  12.7 19.8 %collective-permute-start.2 = (bf16[16,1152]{1,0:T(8,128)(2,1)S(1)}, bf16[16,1152]{1,0:T(8,128)(2,1)S(1)}, u32[]{:S(2)}, u32[]{:S(2)}) collective-permute-start(bf16[16,1152]{1,0:T(8,128)(2,1)S(1)} %pad_maximum_fusion), channel_id=1, source_target_pairs={{0,32},{32,0},{64,96},{96,64},{128,160},{160,128},{192,224},{224,1... | collective-permute-start | bytes 110600 | tf_op jit(solution)/shard_map/ppermute | solution.py:543
  16.7 11.1 %copy-start = (s32[1,1,16,3]{2,1,3,0:T(1,128)S(1)}, s32[1,1,16,3]{2,1,3,0:T(1,128)}, u32[]{:S(2)}) copy-start(s32[1,1,16,3]{2,1,3,0:T(1,128)} %param.11) | copy-start | bytes 580
  16.7 15.8 %collective-permute-start.3 = (bf16[16,1152]{1,0:T(8,128)(2,1)S(1)}, bf16[16,1152]{1,0:T(8,128)(2,1)S(1)}, u32[]{:S(2)}, u32[]{:S(2)}) collective-permute-start(bf16[16,1152]{1,0:T(8,128)(2,1)S(1)} %pad_maximum_fusion.1), channel_id=1, source_target_pairs={{32,64},{64,32},{96,128},{128,96},{160,192},{192,160},{224,256},{2... | collective-permute-start | bytes 110600 | tf_op jit(solution)/shard_map/ppermute | solution.py:543
  35.2 5.7 %collective-permute-start.4 = (bf16[16,1664]{1,0:T(8,128)(2,1)S(1)}, bf16[16,1664]{1,0:T(8,128)(2,1)S(1)}, u32[]{:S(2)}, u32[]{:S(2)}) collective-permute-start(bf16[16,1664]{1,0:T(8,128)(2,1)S(1)} %get-tuple-element.52), channel_id=1, source_target_pairs={{0,1},{1,0},{2,3},{3,2},{4,5},{5,4},{6,7},{7,6},{8,9},{9,8},{10,11... | collective-permute-start | bytes 159752 | tf_op jit(solution)/shard_map/ppermute | solution.py:543
  37.1 8.2 %collective-permute-start.5 = (bf16[16,1664]{1,0:T(8,128)(2,1)S(1)}, bf16[16,1664]{1,0:T(8,128)(2,1)S(1)}, u32[]{:S(2)}, u32[]{:S(2)}) collective-permute-start(bf16[16,1664]{1,0:T(8,128)(2,1)S(1)} %get-tuple-element.53), channel_id=1, source_target_pairs={{1,2},{2,1},{3,4},{4,3},{5,6},{6,5},{7,8},{8,7},{9,10},{10,9},{11,... | collective-permute-start | bytes 159752 | tf_op jit(solution)/shard_map/ppermute | solution.py:543
  45.3 10.9 %collective-permute-start.7 = (bf16[16,1152]{1,0:T(8,128)(2,1)S(1)}, bf16[16,1152]{1,0:T(8,128)(2,1)S(1)}, u32[]{:S(2)}, u32[]{:S(2)}) collective-permute-start(bf16[16,1152]{1,0:T(8,128)(2,1)S(1)} %pad_maximum_fusion.3), channel_id=1, source_target_pairs={{32,64},{64,32},{96,128},{128,96},{160,192},{192,160},{224,256},{2... | collective-permute-start | bytes 110600 | tf_op jit(solution)/shard_map/ppermute | solution.py:543
  51.3 4.9 %collective-permute-start.6 = (bf16[16,1152]{1,0:T(8,128)(2,1)S(1)}, bf16[16,1152]{1,0:T(8,128)(2,1)S(1)}, u32[]{:S(2)}, u32[]{:S(2)}) collective-permute-start(bf16[16,1152]{1,0:T(8,128)(2,1)S(1)} %pad_maximum_fusion.2), channel_id=1, source_target_pairs={{0,32},{32,0},{64,96},{96,64},{128,160},{160,128},{192,224},{224,1... | collective-permute-start | bytes 110600 | tf_op jit(solution)/shard_map/ppermute | solution.py:543

commit v4 on v3

--- a/solution.py
+++ b/solution.py
@@ -224,10 +224,10 @@
 NT = (((1,), (1,)), ((), ()))
 
 
-HALF = NPIX // 2
-
-
-def load_half(res_in, start, res, sem):
+HEAD = 512
+
+
+def load_part(res_in, start, res, sem):
     width = 512
     return [
         begin(
@@ -237,11 +237,11 @@
                 sem.at[n],
             )
         )
-        for n in range(HALF // width)
+        for n in range(res.shape[0] // width)
     ]
 
 
-def turn_half(loads, c_own, res, rest, first):
+def turn_part(loads, c_own, res, rest, first):
     width = 512
     eye = hot(iota((CH, CH), 0) == iota((CH, CH), 1))
     both = jnp.concatenate([c_own.astype(bf16), eye], axis=0)
@@ -258,7 +258,7 @@
     res, rest, first, ctr, slots, across, geo, tr, row_ref, col_ref, sem, rsem,
 ):
     small = begin((tr_in, tr, sem.at[0]))
-    loads = load_half(res_in, 0, res, rsem)
+    loads = load_part(res_in, 0, res, rsem)
     scalars = begin((row_in, row_ref, sem.at[1]), (col_in, col_ref, sem.at[2]))
     row, col, _, _ = sides()
     total = count[0, 0]
@@ -276,7 +276,7 @@
     small()
     c_own = dot(own_hot, tr[...])
     ctr[...] = c_own
-    turn_half(loads, c_own, res, rest, first)
+    turn_part(loads, c_own, res, rest, first)
     scalars()
     up = row_ref[jnp.clip(row - 1, 0, rows - 2)]
     down = row_ref[jnp.clip(row, 0, rows - 2)]
@@ -291,7 +291,7 @@
 def side_kernel(
     res_in, foot_in, geo_in, ctr, slots, rxa, rxb, res, rest, first, own, side, crem, foot, geo, sem, rsem
 ):
-    loads = load_half(res_in, HALF, res, rsem)
+    loads = load_part(res_in, HEAD, res, rsem)
     load = begin((foot_in, foot, sem.at[1]))
     ready = begin((geo_in, geo, sem.at[0]))
     _, _, _, sx = sides()
@@ -300,7 +300,7 @@
     crem[...] = tail[:, 0:F]
     for m in range(32):
         side[:, CH * m : CH * (m + 1)] = whole[MP * m : MP * (m + 1)]
-    turn_half(loads, ctr[...], res, rest, first)
+    turn_part(loads, ctr[...], res, rest, first)
     load()
     own[...] = dot(own_hot, foot[...])
 
@@ -331,11 +331,13 @@
         cr = jnp.sum(c_rem * trace, axis=1, keepdims=True)
         scale = 1.0 / (jnp.sum(trace * trace, axis=1, keepdims=True) + epsilon * F)
         lanes = [slice(step * n, step * (n + 1)) for n in range(NPIX // step)]
-        halves = [slice(step * n, step * (n + 1)) for n in range(HALF // step)]
+        cuts = [
+            [slice(step * n, step * (n + 1)) for n in range(size // step)] for size in (HEAD, NPIX - HEAD)
+        ]
         if it == 0:
-            across = [f[:, cut] for f in (first_l, first_h) for cut in halves]
+            across = [f[:, cut] for f, some in zip((first_l, first_h), cuts) for cut in some]
         else:
-            across = [dot(tb, r[:, cut]) for r in (rest_l, rest_h) for cut in halves]
+            across = [dot(tb, r[:, cut]) for r, some in zip((rest_l, rest_h), cuts) for cut in some]
         sa = jnp.zeros((MP, CH), f32)
         sr = jnp.zeros((MP, CH), f32)
         ss = jnp.zeros((MP, CH), f32)
@@ -355,7 +357,7 @@
                 sa = sa + pa[:, part]
                 sr = sr + pr[:, part]
                 ss = ss + ps[:, part]
-        parts = [r[cut, :] for r in (res_l, res_h) for cut in halves]
+        parts = [r[cut, :] for r, some in zip((res_l, res_h), cuts) for cut in some]
         down = sum(dot(now, part) for now, part in zip(shapes, parts))
         down = (
             down
@@ -583,10 +585,12 @@
     def own(*refs):
         own_kernel(rows, cols, *refs)
 
-    half = (shape(HALF, F), shape(F, HALF), shape(MP, HALF, dtype=f32))
+    def part(size):
+        return (shape(size, F), shape(F, size), shape(MP, size, dtype=f32))
+
     *prepared, slots, across, geo = call(
         own,
-        half
+        part(HEAD)
         + (
             shape(MP, F, dtype=f32),
             shape(MP, CH, dtype=i32),
@@ -600,18 +604,18 @@
             pltpu.SMEM((rows - 1,), i32),
             pltpu.SMEM((cols - 1,), i32),
             dma((3,)),
-            dma((4,)),
+            dma((HEAD // 512,)),
         ],
         1 << 24,
     )(pair_counts, row_far, col_far, res, tr, table, wide)
 
     placed = call(
         side_kernel,
-        half
+        part(NPIX - HEAD)
         + (shape(MP, NPIX, dtype=f32), shape(MP, NPIX, dtype=f32), shape(MP, F, dtype=f32)),
         [HBM] * 2 + [VMEM] * 5,
         (VMEM,) * 6,
-        [pltpu.VMEM((K, NPIX), bf16), pltpu.SMEM((1, CH), i32), dma((2,)), dma((4,))],
+        [pltpu.VMEM((K, NPIX), bf16), pltpu.SMEM((1, CH), i32), dma((2,)), dma(((NPIX - HEAD) // 512,))],
         1 << 24,
     )(res, foot, geo, prepared[-1], slots, rxa, rxb)
 

time: 58.3 us -> 58.3 us (level)
  no operation moved by 1% of the time
where the time goes in v4:
time: 58.3 us; the launch traced here: 57.9 us
  starting transfers between devices  36.6 us (63%)
  Pallas kernels  11.8 us (20%)
  waiting for transfers between devices  7.1 us (12%)
  between operations  2.15 us (4%)
    ppermute x8, starting transfers between devices, swap(): return lax.ppermute(value, axis, pairs)  36.6 us
    ppermute x8, waiting for transfers between devices, swap(): return lax.ppermute(value, axis, pairs)  7.1 us
    pallas_call x1, Pallas kernels, body(): call(refit_kernel, PACKETS + (shape(MP, NPIX), shape(MP, F)), [VMEM] * 15...  2.7 us
    pallas_call x1, Pallas kernels, body(): call(side_kernel, part(NPIX - HEAD) + (shape(MP, NPIX, dtype=f32), shape(...  2.66 us
    pallas_call x1, Pallas kernels, body(): call(before_kernel, (shape(K, NPIX), shape(K, F, dtype=f32), shape(16, BA...  2.29 us
    pallas_call x1, Pallas kernels, body(): call(final_kernel, (shape(K, NPIX), shape(K, F)), [VMEM, HBM] + [VMEM] *...  1.65 us
    pallas_call x1, Pallas kernels, body(): call(pack_kernel, PACKETS, [HBM] * 2, (VMEM,) * 4, [pltpu.VMEM((32, NPIX)...  1.29 us
    pallas_call x1, Pallas kernels, body(): call(own, part(HEAD) + (shape(MP, F, dtype=f32), shape(MP, CH, dtype=i32)...  1.19 us
  transfers between devices with their start and end apart: 8, of which 2 were waited for; matrix products, arithmetic and copies ran while one was open for 0% of the time, Pallas kernels for 11%

profile of v4, /device:TPU:57, one launch (start us, length us, event | category | flops | bytes accessed | tf_op | source)
XLA Modules:
  0.0 57.9 jit_solution(3011046994455022709)
XLA Ops:
  0.6 1.3 %shard_map.104 = (bf16[16,1664]{1,0:T(8,128)(2,1)S(1)}, bf16[16,1664]{1,0:T(8,128)(2,1)S(1)}, bf16[16,384]{1,0:T(8,128)(2,1)S(1)}, bf16[16,384]{1,0:T(8,128)(2,1)S(1)}) custom-call(bf16[40,4096]{1,0:T(8,128)(2,1)} %bitcast.16, bf16[40,128]{1,0:T(8,128)(2,1)} %bitcast.20), custom_call_target="tpu_custom_call" | custom-call | flops 16777216 | bytes 1048576 | tf_op jit(solution)/shard_map/pallas_call | solution.py:575
  1.9 2.6 %collective-permute-start = (bf16[16,1664]{1,0:T(8,128)(2,1)S(1)}, bf16[16,1664]{1,0:T(8,128)(2,1)S(1)}, u32[]{:S(2)}, u32[]{:S(2)}) collective-permute-start(bf16[16,1664]{1,0:T(8,128)(2,1)S(1)} %get-tuple-element.40), channel_id=1, source_target_pairs={{0,1},{1,0},{2,3},{3,2},{4,5},{5,4},{6,7},{7,6},{8,9},{9,8},{10,11... | collective-permute-start | bytes 159752 | tf_op jit(solution)/shard_map/ppermute | solution.py:545
  4.5 5.4 %collective-permute-start.1 = (bf16[16,1664]{1,0:T(8,128)(2,1)S(1)}, bf16[16,1664]{1,0:T(8,128)(2,1)S(1)}, u32[]{:S(2)}, u32[]{:S(2)}) collective-permute-start(bf16[16,1664]{1,0:T(8,128)(2,1)S(1)} %get-tuple-element.41), channel_id=1, source_target_pairs={{1,2},{2,1},{3,4},{4,3},{5,6},{6,5},{7,8},{8,7},{9,10},{10,9},{11,... | collective-permute-start | bytes 159752 | tf_op jit(solution)/shard_map/ppermute | solution.py:545
  9.9 0.0 collective-permute-done.rxa.oxa
  9.9 2.7 %collective-permute-done.1.rxb.oxb = bf16[16,1664]{1,0:T(8,128)(2,1)S(1)} collective-permute-done((bf16[16,1664]{1,0:T(8,128)(2,1)S(1)}, bf16[16,1664]{1,0:T(8,128)(2,1)S(1)}, u32[]{:S(2)}, u32[]{:S(2)}) %collective-permute-start.1) | collective-permute-done | bytes 53280 | tf_op jit(solution)/shard_map/ppermute | solution.py:545
  12.7 4.0 %collective-permute-start.2 = (bf16[16,1152]{1,0:T(8,128)(2,1)S(1)}, bf16[16,1152]{1,0:T(8,128)(2,1)S(1)}, u32[]{:S(2)}, u32[]{:S(2)}) collective-permute-start(bf16[16,1152]{1,0:T(8,128)(2,1)S(1)} %pad_maximum_fusion), channel_id=1, source_target_pairs={{0,32},{32,0},{64,96},{96,64},{128,160},{160,128},{192,224},{224,1... | collective-permute-start | bytes 110600 | tf_op jit(solution)/shard_map/ppermute | solution.py:545
  16.7 0.0 copy-start
  16.7 11.1 %collective-permute-start.3 = (bf16[16,1152]{1,0:T(8,128)(2,1)S(1)}, bf16[16,1152]{1,0:T(8,128)(2,1)S(1)}, u32[]{:S(2)}, u32[]{:S(2)}) collective-permute-start(bf16[16,1152]{1,0:T(8,128)(2,1)S(1)} %pad_maximum_fusion.1), channel_id=1, source_target_pairs={{32,64},{64,32},{96,128},{128,96},{160,192},{192,160},{224,256},{2... | collective-permute-start | bytes 110600 | tf_op jit(solution)/shard_map/ppermute | solution.py:545
  27.8 0.0 copy-done
  27.8 0.1 tile.10.refs_6_
  27.9 0.1 copy.12.refs_5_
  28.7 1.2 %shard_map.103 = (bf16[512,128]{1,0:T(8,128)(2,1)S(1)}, bf16[128,512]{1,0:T(8,128)(2,1)S(1)}, f32[16,512]{1,0:T(8,128)S(1)}, f32[16,128]{1,0:T(8,128)S(1)}, s32[...) custom-call(s32[1,1]{1,0:T(1,128)S(6)} %copy.18.refs_0_, s32[15]{0:T(128)} %refs_1_.1, s32[31]{0:T(128)} %refs_2_.1, ...), custom_call_target="tpu_custom_call" | custom-call | flops 16777216 | bytes 1048576 | tf_op jit(solution)/shard_map/pallas_call | solution.py:591
  29.9 2.7 %shard_map.105 = (bf16[3584,128]{1,0:T(8,128)(2,1)S(1)}, bf16[128,3584]{1,0:T(8,128)(2,1)S(1)}, f32[16,3584]{1,0:T(8,128)S(1)}, f32[16,4096]{1,0:T(8,128)S(1)}, ...) custom-call(bf16[4096,128]{1,0:T(8,128)(2,1)} %bitcast.15, bf16[40,4096]{1,0:T(8,128)(2,1)} %bitcast.17, ...), custom_call_target="tpu_custom_call" | custom-call | flops 16777216 | bytes 1048576 | tf_op jit(solution)/shard_map/pallas_call | solution.py:612
  32.5 0.0 collective-permute-done.2.rya.oya
  32.5 0.0 collective-permute-done.3.ryb.oyb
  32.5 2.7 %shard_map.106 = (bf16[16,1664]{1,0:T(8,128)(2,1)S(1)}, bf16[16,1664]{1,0:T(8,128)(2,1)S(1)}, bf16[16,384]{1,0:T(8,128)(2,1)S(1)}, bf16[16,384]{1,0:T(8,128)(2,1...) custom-call(s32[1,128]{1,0:T(1,128)S(1)} %get-tuple-element.33.geo_in, ...), custom_call_target="tpu_custom_call" | custom-call | flops 268435456 | bytes 1048576 | tf_op jit(solution)/shard_map/pallas_call | solution.py:622
  35.3 1.9 %collective-permute-start.4 = (bf16[16,1664]{1,0:T(8,128)(2,1)S(1)}, bf16[16,1664]{1,0:T(8,128)(2,1)S(1)}, u32[]{:S(2)}, u32[]{:S(2)}) collective-permute-start(bf16[16,1664]{1,0:T(8,128)(2,1)S(1)} %get-tuple-element.52), channel_id=1, source_target_pairs={{0,1},{1,0},{2,3},{3,2},{4,5},{5,4},{6,7},{7,6},{8,9},{9,8},{10,11... | collective-permute-start | bytes 159752 | tf_op jit(solution)/shard_map/ppermute | solution.py:545
  37.2 3.8 %collective-permute-start.5 = (bf16[16,1664]{1,0:T(8,128)(2,1)S(1)}, bf16[16,1664]{1,0:T(8,128)(2,1)S(1)}, u32[]{:S(2)}, u32[]{:S(2)}) collective-permute-start(bf16[16,1664]{1,0:T(8,128)(2,1)S(1)} %get-tuple-element.53), channel_id=1, source_target_pairs={{1,2},{2,1},{3,4},{4,3},{5,6},{6,5},{7,8},{8,7},{9,10},{10,9},{11,... | collective-permute-start | bytes 159752 | tf_op jit(solution)/shard_map/ppermute | solution.py:545
  41.0 0.0 collective-permute-done.4.rxa
  41.0 4.3 %collective-permute-done.5.rxb = bf16[16,1664]{1,0:T(8,128)(2,1)S(1)} collective-permute-done((bf16[16,1664]{1,0:T(8,128)(2,1)S(1)}, bf16[16,1664]{1,0:T(8,128)(2,1)S(1)}, u32[]{:S(2)}, u32[]{:S(2)}) %collective-permute-start.5) | collective-permute-done | bytes 53280 | tf_op jit(solution)/shard_map/ppermute | solution.py:545
  45.4 6.0 %collective-permute-start.7 = (bf16[16,1152]{1,0:T(8,128)(2,1)S(1)}, bf16[16,1152]{1,0:T(8,128)(2,1)S(1)}, u32[]{:S(2)}, u32[]{:S(2)}) collective-permute-start(bf16[16,1152]{1,0:T(8,128)(2,1)S(1)} %pad_maximum_fusion.3), channel_id=1, source_target_pairs={{32,64},{64,32},{96,128},{128,96},{160,192},{192,160},{224,256},{2... | collective-permute-start | bytes 110600 | tf_op jit(solution)/shard_map/ppermute | solution.py:545
  51.3 1.9 %collective-permute-start.6 = (bf16[16,1152]{1,0:T(8,128)(2,1)S(1)}, bf16[16,1152]{1,0:T(8,128)(2,1)S(1)}, u32[]{:S(2)}, u32[]{:S(2)}) collective-permute-start(bf16[16,1152]{1,0:T(8,128)(2,1)S(1)} %pad_maximum_fusion.2), channel_id=1, source_target_pairs={{0,32},{32,0},{64,96},{96,64},{128,160},{160,128},{192,224},{224,1... | collective-permute-start | bytes 110600 | tf_op jit(solution)/shard_map/ppermute | solution.py:545
  53.9 2.3 %shard_map.107 = (bf16[40,4096]{1,0:T(8,128)(2,1)}, f32[40,128]{1,0:T(8,128)S(1)}, f32[16,1536]{1,0:T(8,128)S(1)}, f32[16,1536]{1,0:T(8,128)S(1)}, f32[24,40]{1,0:T(8,128)}) custom-call(s32[1,1]{1,0:T(1,128)S(6)} %copy.19.comp, bf16[40,4096]{1,0:T(8,128)(2,1)} %bitcast.18, bf16[40,128]{1,0:T(8,128)(2,1)} %bitcast.22, s32[1,128]{1,0:T(1,128)S(1)} %get-tuple-element.33.geo_in, ...), custom_call_target="tpu_custom_call" | custom-call | flops 16777216 | bytes 1048576 | tf_op jit(solution)/shard_map/pallas_call | solution.py:632
  56.2 0.0 collective-permute-done.7.ryb
  56.2 0.0 collective-permute-done.6.rya
  56.2 1.7 %shard_map.108 = (bf16[40,4096]{1,0:T(8,128)(2,1)}, bf16[40,128]{1,0:T(8,128)(2,1)}) custom-call(s32[1,128]{1,0:T(1,128)S(1)} %get-tuple-element.33.geo_in, bf16[40,4096]{1,0:T(8,128)(2,1)} %get-tuple-element.54.base, f32[40,128]{1,0:T(8,128)S(1)} %get-tuple-element.55.tbase, ...), custom_call_target="tpu_custom_call", output_to_operand_aliasing={{0}: (1, {})} | custom-call | flops 67108864 | bytes 1048576 | tf_op jit(solution)/shard_map/pallas_call | solution.py:652
  (10 shorter events, 0.0 us)
Async XLA Ops:
  1.9 8.0 %collective-permute-start = (bf16[16,1664]{1,0:T(8,128)(2,1)S(1)}, bf16[16,1664]{1,0:T(8,128)(2,1)S(1)}, u32[]{:S(2)}, u32[]{:S(2)}) collective-permute-start(bf16[16,1664]{1,0:T(8,128)(2,1)S(1)} %get-tuple-element.40), channel_id=1, source_target_pairs={{0,1},{1,0},{2,3},{3,2},{4,5},{5,4},{6,7},{7,6},{8,9},{9,8},{10,11... | collective-permute-start | bytes 159752 | tf_op jit(solution)/shard_map/ppermute | solution.py:545
  4.5 8.2 %collective-permute-start.1 = (bf16[16,1664]{1,0:T(8,128)(2,1)S(1)}, bf16[16,1664]{1,0:T(8,128)(2,1)S(1)}, u32[]{:S(2)}, u32[]{:S(2)}) collective-permute-start(bf16[16,1664]{1,0:T(8,128)(2,1)S(1)} %get-tuple-element.41), channel_id=1, source_target_pairs={{1,2},{2,1},{3,4},{4,3},{5,6},{6,5},{7,8},{8,7},{9,10},{10,9},{11,... | collective-permute-start | bytes 159752 | tf_op jit(solution)/shard_map/ppermute | solution.py:545
  12.7 19.9 %collective-permute-start.2 = (bf16[16,1152]{1,0:T(8,128)(2,1)S(1)}, bf16[16,1152]{1,0:T(8,128)(2,1)S(1)}, u32[]{:S(2)}, u32[]{:S(2)}) collective-permute-start(bf16[16,1152]{1,0:T(8,128)(2,1)S(1)} %pad_maximum_fusion), channel_id=1, source_target_pairs={{0,32},{32,0},{64,96},{96,64},{128,160},{160,128},{192,224},{224,1... | collective-permute-start | bytes 110600 | tf_op jit(solution)/shard_map/ppermute | solution.py:545
  16.7 11.1 %copy-start = (s32[1,1,16,3]{2,1,3,0:T(1,128)S(1)}, s32[1,1,16,3]{2,1,3,0:T(1,128)}, u32[]{:S(2)}) copy-start(s32[1,1,16,3]{2,1,3,0:T(1,128)} %param.11) | copy-start | bytes 580
  16.7 15.8 %collective-permute-start.3 = (bf16[16,1152]{1,0:T(8,128)(2,1)S(1)}, bf16[16,1152]{1,0:T(8,128)(2,1)S(1)}, u32[]{:S(2)}, u32[]{:S(2)}) collective-permute-start(bf16[16,1152]{1,0:T(8,128)(2,1)S(1)} %pad_maximum_fusion.1), channel_id=1, source_target_pairs={{32,64},{64,32},{96,128},{128,96},{160,192},{192,160},{224,256},{2... | collective-permute-start | bytes 110600 | tf_op jit(solution)/shard_map/ppermute | solution.py:545
  35.3 5.7 %collective-permute-start.4 = (bf16[16,1664]{1,0:T(8,128)(2,1)S(1)}, bf16[16,1664]{1,0:T(8,128)(2,1)S(1)}, u32[]{:S(2)}, u32[]{:S(2)}) collective-permute-start(bf16[16,1664]{1,0:T(8,128)(2,1)S(1)} %get-tuple-element.52), channel_id=1, source_target_pairs={{0,1},{1,0},{2,3},{3,2},{4,5},{5,4},{6,7},{7,6},{8,9},{9,8},{10,11... | collective-permute-start | bytes 159752 | tf_op jit(solution)/shard_map/ppermute | solution.py:545
  37.2 8.2 %collective-permute-start.5 = (bf16[16,1664]{1,0:T(8,128)(2,1)S(1)}, bf16[16,1664]{1,0:T(8,128)(2,1)S(1)}, u32[]{:S(2)}, u32[]{:S(2)}) collective-permute-start(bf16[16,1664]{1,0:T(8,128)(2,1)S(1)} %get-tuple-element.53), channel_id=1, source_target_pairs={{1,2},{2,1},{3,4},{4,3},{5,6},{6,5},{7,8},{8,7},{9,10},{10,9},{11,... | collective-permute-start | bytes 159752 | tf_op jit(solution)/shard_map/ppermute | solution.py:545
  45.4 10.9 %collective-permute-start.7 = (bf16[16,1152]{1,0:T(8,128)(2,1)S(1)}, bf16[16,1152]{1,0:T(8,128)(2,1)S(1)}, u32[]{:S(2)}, u32[]{:S(2)}) collective-permute-start(bf16[16,1152]{1,0:T(8,128)(2,1)S(1)} %pad_maximum_fusion.3), channel_id=1, source_target_pairs={{32,64},{64,32},{96,128},{128,96},{160,192},{192,160},{224,256},{2... | collective-permute-start | bytes 110600 | tf_op jit(solution)/shard_map/ppermute | solution.py:545
  51.3 4.9 %collective-permute-start.6 = (bf16[16,1152]{1,0:T(8,128)(2,1)S(1)}, bf16[16,1152]{1,0:T(8,128)(2,1)S(1)}, u32[]{:S(2)}, u32[]{:S(2)}) collective-permute-start(bf16[16,1152]{1,0:T(8,128)(2,1)S(1)} %pad_maximum_fusion.2), channel_id=1, source_target_pairs={{0,32},{32,0},{64,96},{96,64},{128,160},{160,128},{192,224},{224,1... | collective-permute-start | bytes 110600 | tf_op jit(solution)/shard_map/ppermute | solution.py:545

commit v5 on v4

--- a/solution.py
+++ b/solution.py
@@ -254,25 +254,14 @@
 
 
 def own_kernel(
-    rows, cols, count, row_in, col_in, res_in, tr_in, table, wide,
-    res, rest, first, ctr, slots, across, geo, tr, row_ref, col_ref, sem, rsem,
+    rows, cols, row_in, col_in, res_in, tr_in, table,
+    res, rest, first, ctr, geo, tr, row_ref, col_ref, sem, rsem,
 ):
     small = begin((tr_in, tr, sem.at[0]))
     loads = load_part(res_in, 0, res, rsem)
     scalars = begin((row_in, row_ref, sem.at[1]), (col_in, col_ref, sem.at[2]))
     row, col, _, _ = sides()
-    total = count[0, 0]
-    ids = table[:, 0:1]
-    live = iota((MP, CH), 0) < total
-    idx = NBR * table[:, 1:2] + table[:, 2:3]
-    place = iota((MP, CH), 1)
-    dead = jnp.where(live, jnp.where(place == 0, ids, idx), -100)
-    slots[...] = jnp.where(place == 2, ids, dead)
-    line = iota((8, CH), 0)
-    alive = (iota((8, CH), 1) & 15) < total
-    pair = NBR * wide[1:2, :] + wide[2:3, :]
-    across[...] = jnp.where(alive, jnp.where(line == 0, wide[0:1, :], pair), -100)
-    own_hot = hot(ids == iota((MP, K), 1))
+    own_hot = hot(table[:, 0:1] == iota((MP, K), 1))
     small()
     c_own = dot(own_hot, tr[...])
     ctr[...] = c_own
@@ -289,13 +278,23 @@
 
 
 def side_kernel(
-    res_in, foot_in, geo_in, ctr, slots, rxa, rxb, res, rest, first, own, side, crem, foot, geo, sem, rsem
+    count, res_in, foot_in, geo_in, ctr, table, wide, rxa, rxb,
+    res, rest, first, own, side, crem, slots, across, foot, geo, sem, rsem,
 ):
     loads = load_part(res_in, HEAD, res, rsem)
     load = begin((foot_in, foot, sem.at[1]))
     ready = begin((geo_in, geo, sem.at[0]))
     _, _, _, sx = sides()
-    own_hot = hot(slots[:, 2:3] == iota((MP, K), 1))
+    total = count[0, 0]
+    ids = table[:, 0:1]
+    live = iota((MP, CH), 0) < total
+    idx = NBR * table[:, 1:2] + table[:, 2:3]
+    slots[...] = jnp.where(live, jnp.where(iota((MP, CH), 1) == 0, ids, idx), -100)
+    line = iota((8, CH), 0)
+    alive = (iota((8, CH), 1) & 15) < total
+    pair = NBR * wide[1:2, :] + wide[2:3, :]
+    across[...] = jnp.where(alive, jnp.where(line == 0, wide[0:1, :], pair), -100)
+    own_hot = hot(ids == iota((MP, K), 1))
     whole, tail = receive_sides(slot_select(slots), MP, (rxa, rxb), sx, geo, ready)
     crem[...] = tail[:, 0:F]
     for m in range(32):
@@ -588,17 +587,15 @@
     def part(size):
         return (shape(size, F), shape(F, size), shape(MP, size, dtype=f32))
 
-    *prepared, slots, across, geo = call(
+    *prepared, geo = call(
         own,
         part(HEAD)
         + (
             shape(MP, F, dtype=f32),
-            shape(MP, CH, dtype=i32),
-            shape(8, CH, dtype=i32),
             shape(1, CH, dtype=i32),
         ),
-        [SMEM] + [HBM] * 4 + [VMEM] * 2,
-        (VMEM,) * 7,
+        [HBM] * 4 + [VMEM],
+        (VMEM,) * 5,
         [
             pltpu.VMEM((K, F), bf16),
             pltpu.SMEM((rows - 1,), i32),
@@ -607,17 +604,23 @@
             dma((HEAD // 512,)),
         ],
         1 << 24,
-    )(pair_counts, row_far, col_far, res, tr, table, wide)
-
-    placed = call(
+    )(row_far, col_far, res, tr, table)
+
+    *placed, slots, across = call(
         side_kernel,
         part(NPIX - HEAD)
-        + (shape(MP, NPIX, dtype=f32), shape(MP, NPIX, dtype=f32), shape(MP, F, dtype=f32)),
-        [HBM] * 2 + [VMEM] * 5,
-        (VMEM,) * 6,
+        + (
+            shape(MP, NPIX, dtype=f32),
+            shape(MP, NPIX, dtype=f32),
+            shape(MP, F, dtype=f32),
+            shape(MP, CH, dtype=i32),
+            shape(8, CH, dtype=i32),
+        ),
+        [SMEM] + [HBM] * 2 + [VMEM] * 6,
+        (VMEM,) * 8,
         [pltpu.VMEM((K, NPIX), bf16), pltpu.SMEM((1, CH), i32), dma((2,)), dma(((NPIX - HEAD) // 512,))],
         1 << 24,
-    )(res, foot, geo, prepared[-1], slots, rxa, rxb)
+    )(pair_counts, res, foot, geo, prepared[-1], table, wide, rxa, rxb)
 
     xa, xb, va, vb, merged, mtrace = call(
         refit_kernel,

time: 58.3 us -> 58.3 us (level)
  no operation moved by 1% of the time
where the time goes in v5:
time: 58.3 us; the launch traced here: 57.9 us
  starting transfers between devices  36.5 us (63%)
  Pallas kernels  11.9 us (20%)
  waiting for transfers between devices  7.1 us (12%)
  between operations  2.14 us (4%)
    ppermute x8, starting transfers between devices, swap(): return lax.ppermute(value, axis, pairs)  36.5 us
    ppermute x8, waiting for transfers between devices, swap(): return lax.ppermute(value, axis, pairs)  7.1 us
    pallas_call x1, Pallas kernels, body(): call(side_kernel, part(NPIX - HEAD) + (shape(MP, NPIX, dtype=f32), shape(...  2.8 us
    pallas_call x1, Pallas kernels, body(): call(refit_kernel, PACKETS + (shape(MP, NPIX), shape(MP, F)), [VMEM] * 15...  2.68 us
    pallas_call x1, Pallas kernels, body(): call(before_kernel, (shape(K, NPIX), shape(K, F, dtype=f32), shape(16, BA...  2.29 us
    pallas_call x1, Pallas kernels, body(): call(final_kernel, (shape(K, NPIX), shape(K, F)), [VMEM, HBM] + [VMEM] *...  1.65 us
    pallas_call x1, Pallas kernels, body(): call(pack_kernel, PACKETS, [HBM] * 2, (VMEM,) * 4, [pltpu.VMEM((32, NPIX)...  1.29 us
    pallas_call x1, Pallas kernels, body(): call(own, part(HEAD) + (shape(MP, F, dtype=f32), shape(1, CH, dtype=i32))...  1.19 us
  transfers between devices with their start and end apart: 8, of which 2 were waited for; matrix products, arithmetic and copies ran while one was open for 0% of the time, Pallas kernels for 11%

profile of v5, /device:TPU:57, one launch (start us, length us, event | category | flops | bytes accessed | tf_op | source)
XLA Modules:
  0.0 57.9 jit_solution(6550984558334856126)
XLA Ops:
  0.6 1.3 %shard_map.104 = (bf16[16,1664]{1,0:T(8,128)(2,1)S(1)}, bf16[16,1664]{1,0:T(8,128)(2,1)S(1)}, bf16[16,384]{1,0:T(8,128)(2,1)S(1)}, bf16[16,384]{1,0:T(8,128)(2,1)S(1)}) custom-call(bf16[40,4096]{1,0:T(8,128)(2,1)} %bitcast.16, bf16[40,128]{1,0:T(8,128)(2,1)} %bitcast.20), custom_call_target="tpu_custom_call" | custom-call | flops 16777216 | bytes 1048576 | tf_op jit(solution)/shard_map/pallas_call | solution.py:574
  1.9 2.6 %collective-permute-start = (bf16[16,1664]{1,0:T(8,128)(2,1)S(1)}, bf16[16,1664]{1,0:T(8,128)(2,1)S(1)}, u32[]{:S(2)}, u32[]{:S(2)}) collective-permute-start(bf16[16,1664]{1,0:T(8,128)(2,1)S(1)} %get-tuple-element.35), channel_id=1, source_target_pairs={{0,1},{1,0},{2,3},{3,2},{4,5},{5,4},{6,7},{7,6},{8,9},{9,8},{10,11... | collective-permute-start | bytes 159752 | tf_op jit(solution)/shard_map/ppermute | solution.py:544
  4.5 5.4 %collective-permute-start.1 = (bf16[16,1664]{1,0:T(8,128)(2,1)S(1)}, bf16[16,1664]{1,0:T(8,128)(2,1)S(1)}, u32[]{:S(2)}, u32[]{:S(2)}) collective-permute-start(bf16[16,1664]{1,0:T(8,128)(2,1)S(1)} %get-tuple-element.36), channel_id=1, source_target_pairs={{1,2},{2,1},{3,4},{4,3},{5,6},{6,5},{7,8},{8,7},{9,10},{10,9},{11,... | collective-permute-start | bytes 159752 | tf_op jit(solution)/shard_map/ppermute | solution.py:544
  9.9 0.0 collective-permute-done.rxa.oxa
  9.9 2.7 %collective-permute-done.1.rxb.oxb = bf16[16,1664]{1,0:T(8,128)(2,1)S(1)} collective-permute-done((bf16[16,1664]{1,0:T(8,128)(2,1)S(1)}, bf16[16,1664]{1,0:T(8,128)(2,1)S(1)}, u32[]{:S(2)}, u32[]{:S(2)}) %collective-permute-start.1) | collective-permute-done | bytes 53280 | tf_op jit(solution)/shard_map/ppermute | solution.py:544
  12.7 4.0 %collective-permute-start.2 = (bf16[16,1152]{1,0:T(8,128)(2,1)S(1)}, bf16[16,1152]{1,0:T(8,128)(2,1)S(1)}, u32[]{:S(2)}, u32[]{:S(2)}) collective-permute-start(bf16[16,1152]{1,0:T(8,128)(2,1)S(1)} %pad_maximum_fusion), channel_id=1, source_target_pairs={{0,32},{32,0},{64,96},{96,64},{128,160},{160,128},{192,224},{224,1... | collective-permute-start | bytes 110600 | tf_op jit(solution)/shard_map/ppermute | solution.py:544
  16.7 0.0 copy-start
  16.7 11.1 %collective-permute-start.3 = (bf16[16,1152]{1,0:T(8,128)(2,1)S(1)}, bf16[16,1152]{1,0:T(8,128)(2,1)S(1)}, u32[]{:S(2)}, u32[]{:S(2)}) collective-permute-start(bf16[16,1152]{1,0:T(8,128)(2,1)S(1)} %pad_maximum_fusion.1), channel_id=1, source_target_pairs={{32,64},{64,32},{96,128},{128,96},{160,192},{192,160},{224,256},{2... | collective-permute-start | bytes 110600 | tf_op jit(solution)/shard_map/ppermute | solution.py:544
  27.8 0.0 copy-done
  27.8 0.1 copy.12.refs_4_.table
  27.9 0.1 tile.10.wide
  28.7 1.2 %shard_map.103 = (bf16[512,128]{1,0:T(8,128)(2,1)S(1)}, bf16[128,512]{1,0:T(8,128)(2,1)S(1)}, f32[16,512]{1,0:T(8,128)S(1)}, f32[16,128]{1,0:T(8,128)S(1)}, s32[1,128]{1,0:T(1,128)S(1)}) custom-call(s32[15]{0:T(128)} %refs_0_.1, s32[31]{0:T(128)} %refs_1_.1, bf16[4096,128]{1,0:T(8,128)(2,1)} %bitcast.14, bf16[40,128]{1,0:T(8,128)(2,1)} %bitcast.21, ...), custom_call_target="tpu_custom_call" | custom-call | flops 16777216 | bytes 1048576 | tf_op jit(solution)/shard_map/pallas_call | solution.py:590
  29.9 2.8 %shard_map.105 = (bf16[3584,128]{1,0:T(8,128)(2,1)S(1)}, bf16[128,3584]{1,0:T(8,128)(2,1)S(1)}, f32[16,3584]{1,0:T(8,128)S(1)}, f32[16,4096]{1,0:T(8,128)S(1)}, ...) custom-call(s32[1,1]{1,0:T(1,128)S(6)} %copy.19.count, ...), custom_call_target="tpu_custom_call" | custom-call | flops 16777216 | bytes 1048576 | tf_op jit(solution)/shard_map/pallas_call | solution.py:609
  32.7 0.0 collective-permute-done.2.rya.oya
  32.7 0.0 collective-permute-done.3.ryb.oyb
  32.7 2.7 %shard_map.106 = (bf16[16,1664]{1,0:T(8,128)(2,1)S(1)}, bf16[16,1664]{1,0:T(8,128)(2,1)S(1)}, bf16[16,384]{1,0:T(8,128)(2,1)S(1)}, bf16[16,384]{1,0:T(8,128)(2,1...) custom-call(s32[1,128]{1,0:T(1,128)S(1)} %get-tuple-element.33.geo_in, ...), custom_call_target="tpu_custom_call" | custom-call | flops 268435456 | bytes 1048576 | tf_op jit(solution)/shard_map/pallas_call | solution.py:625
  35.4 1.9 %collective-permute-start.4 = (bf16[16,1664]{1,0:T(8,128)(2,1)S(1)}, bf16[16,1664]{1,0:T(8,128)(2,1)S(1)}, u32[]{:S(2)}, u32[]{:S(2)}) collective-permute-start(bf16[16,1664]{1,0:T(8,128)(2,1)S(1)} %get-tuple-element.52), channel_id=1, source_target_pairs={{0,1},{1,0},{2,3},{3,2},{4,5},{5,4},{6,7},{7,6},{8,9},{9,8},{10,11... | collective-permute-start | bytes 159752 | tf_op jit(solution)/shard_map/ppermute | solution.py:544
  37.3 3.8 %collective-permute-start.5 = (bf16[16,1664]{1,0:T(8,128)(2,1)S(1)}, bf16[16,1664]{1,0:T(8,128)(2,1)S(1)}, u32[]{:S(2)}, u32[]{:S(2)}) collective-permute-start(bf16[16,1664]{1,0:T(8,128)(2,1)S(1)} %get-tuple-element.53), channel_id=1, source_target_pairs={{1,2},{2,1},{3,4},{4,3},{5,6},{6,5},{7,8},{8,7},{9,10},{10,9},{11,... | collective-permute-start | bytes 159752 | tf_op jit(solution)/shard_map/ppermute | solution.py:544
  41.1 0.0 collective-permute-done.4.rxa
  41.1 4.3 %collective-permute-done.5.rxb = bf16[16,1664]{1,0:T(8,128)(2,1)S(1)} collective-permute-done((bf16[16,1664]{1,0:T(8,128)(2,1)S(1)}, bf16[16,1664]{1,0:T(8,128)(2,1)S(1)}, u32[]{:S(2)}, u32[]{:S(2)}) %collective-permute-start.5) | collective-permute-done | bytes 53280 | tf_op jit(solution)/shard_map/ppermute | solution.py:544
  45.5 5.8 %collective-permute-start.7 = (bf16[16,1152]{1,0:T(8,128)(2,1)S(1)}, bf16[16,1152]{1,0:T(8,128)(2,1)S(1)}, u32[]{:S(2)}, u32[]{:S(2)}) collective-permute-start(bf16[16,1152]{1,0:T(8,128)(2,1)S(1)} %pad_maximum_fusion.3), channel_id=1, source_target_pairs={{32,64},{64,32},{96,128},{128,96},{160,192},{192,160},{224,256},{2... | collective-permute-start | bytes 110600 | tf_op jit(solution)/shard_map/ppermute | solution.py:544
  51.3 1.9 %collective-permute-start.6 = (bf16[16,1152]{1,0:T(8,128)(2,1)S(1)}, bf16[16,1152]{1,0:T(8,128)(2,1)S(1)}, u32[]{:S(2)}, u32[]{:S(2)}) collective-permute-start(bf16[16,1152]{1,0:T(8,128)(2,1)S(1)} %pad_maximum_fusion.2), channel_id=1, source_target_pairs={{0,32},{32,0},{64,96},{96,64},{128,160},{160,128},{192,224},{224,1... | collective-permute-start | bytes 110600 | tf_op jit(solution)/shard_map/ppermute | solution.py:544
  53.9 2.3 %shard_map.107 = (bf16[40,4096]{1,0:T(8,128)(2,1)}, f32[40,128]{1,0:T(8,128)S(1)}, f32[16,1536]{1,0:T(8,128)S(1)}, f32[16,1536]{1,0:T(8,128)S(1)}, f32[24,40]{1,0:T(8,128)}) custom-call(s32[1,1]{1,0:T(1,128)S(6)} %copy.20.comp, bf16[40,4096]{1,0:T(8,128)(2,1)} %bitcast.18, bf16[40,128]{1,0:T(8,128)(2,1)} %bitcast.22, s32[1,128]{1,0:T(1,128)S(1)} %get-tuple-element.33.geo_in, ...), custom_call_target="tpu_custom_call" | custom-call | flops 16777216 | bytes 1048576 | tf_op jit(solution)/shard_map/pallas_call | solution.py:635
  56.2 0.0 collective-permute-done.7.ryb
  56.2 0.0 collective-permute-done.6.rya
  56.2 1.6 %shard_map.108 = (bf16[40,4096]{1,0:T(8,128)(2,1)}, bf16[40,128]{1,0:T(8,128)(2,1)}) custom-call(s32[1,128]{1,0:T(1,128)S(1)} %get-tuple-element.33.geo_in, bf16[40,4096]{1,0:T(8,128)(2,1)} %get-tuple-element.54.base, f32[40,128]{1,0:T(8,128)S(1)} %get-tuple-element.55.tbase, ...), custom_call_target="tpu_custom_call", output_to_operand_aliasing={{0}: (1, {})} | custom-call | flops 67108864 | bytes 1048576 | tf_op jit(solution)/shard_map/pallas_call | solution.py:655
  (10 shorter events, 0.0 us)
Async XLA Ops:
  1.9 8.0 %collective-permute-start = (bf16[16,1664]{1,0:T(8,128)(2,1)S(1)}, bf16[16,1664]{1,0:T(8,128)(2,1)S(1)}, u32[]{:S(2)}, u32[]{:S(2)}) collective-permute-start(bf16[16,1664]{1,0:T(8,128)(2,1)S(1)} %get-tuple-element.35), channel_id=1, source_target_pairs={{0,1},{1,0},{2,3},{3,2},{4,5},{5,4},{6,7},{7,6},{8,9},{9,8},{10,11... | collective-permute-start | bytes 159752 | tf_op jit(solution)/shard_map/ppermute | solution.py:544
  4.5 8.2 %collective-permute-start.1 = (bf16[16,1664]{1,0:T(8,128)(2,1)S(1)}, bf16[16,1664]{1,0:T(8,128)(2,1)S(1)}, u32[]{:S(2)}, u32[]{:S(2)}) collective-permute-start(bf16[16,1664]{1,0:T(8,128)(2,1)S(1)} %get-tuple-element.36), channel_id=1, source_target_pairs={{1,2},{2,1},{3,4},{4,3},{5,6},{6,5},{7,8},{8,7},{9,10},{10,9},{11,... | collective-permute-start | bytes 159752 | tf_op jit(solution)/shard_map/ppermute | solution.py:544
  12.7 20.0 %collective-permute-start.2 = (bf16[16,1152]{1,0:T(8,128)(2,1)S(1)}, bf16[16,1152]{1,0:T(8,128)(2,1)S(1)}, u32[]{:S(2)}, u32[]{:S(2)}) collective-permute-start(bf16[16,1152]{1,0:T(8,128)(2,1)S(1)} %pad_maximum_fusion), channel_id=1, source_target_pairs={{0,32},{32,0},{64,96},{96,64},{128,160},{160,128},{192,224},{224,1... | collective-permute-start | bytes 110600 | tf_op jit(solution)/shard_map/ppermute | solution.py:544
  16.7 11.1 %copy-start = (s32[1,1,16,3]{2,1,3,0:T(1,128)S(1)}, s32[1,1,16,3]{2,1,3,0:T(1,128)}, u32[]{:S(2)}) copy-start(s32[1,1,16,3]{2,1,3,0:T(1,128)} %param.11) | copy-start | bytes 580
  16.7 16.0 %collective-permute-start.3 = (bf16[16,1152]{1,0:T(8,128)(2,1)S(1)}, bf16[16,1152]{1,0:T(8,128)(2,1)S(1)}, u32[]{:S(2)}, u32[]{:S(2)}) collective-permute-start(bf16[16,1152]{1,0:T(8,128)(2,1)S(1)} %pad_maximum_fusion.1), channel_id=1, source_target_pairs={{32,64},{64,32},{96,128},{128,96},{160,192},{192,160},{224,256},{2... | collective-permute-start | bytes 110600 | tf_op jit(solution)/shard_map/ppermute | solution.py:544
  35.4 5.7 %collective-permute-start.4 = (bf16[16,1664]{1,0:T(8,128)(2,1)S(1)}, bf16[16,1664]{1,0:T(8,128)(2,1)S(1)}, u32[]{:S(2)}, u32[]{:S(2)}) collective-permute-start(bf16[16,1664]{1,0:T(8,128)(2,1)S(1)} %get-tuple-element.52), channel_id=1, source_target_pairs={{0,1},{1,0},{2,3},{3,2},{4,5},{5,4},{6,7},{7,6},{8,9},{9,8},{10,11... | collective-permute-start | bytes 159752 | tf_op jit(solution)/shard_map/ppermute | solution.py:544
  37.3 8.2 %collective-permute-start.5 = (bf16[16,1664]{1,0:T(8,128)(2,1)S(1)}, bf16[16,1664]{1,0:T(8,128)(2,1)S(1)}, u32[]{:S(2)}, u32[]{:S(2)}) collective-permute-start(bf16[16,1664]{1,0:T(8,128)(2,1)S(1)} %get-tuple-element.53), channel_id=1, source_target_pairs={{1,2},{2,1},{3,4},{4,3},{5,6},{6,5},{7,8},{8,7},{9,10},{10,9},{11,... | collective-permute-start | bytes 159752 | tf_op jit(solution)/shard_map/ppermute | solution.py:544
  45.5 10.7 %collective-permute-start.7 = (bf16[16,1152]{1,0:T(8,128)(2,1)S(1)}, bf16[16,1152]{1,0:T(8,128)(2,1)S(1)}, u32[]{:S(2)}, u32[]{:S(2)}) collective-permute-start(bf16[16,1152]{1,0:T(8,128)(2,1)S(1)} %pad_maximum_fusion.3), channel_id=1, source_target_pairs={{32,64},{64,32},{96,128},{128,96},{160,192},{192,160},{224,256},{2... | collective-permute-start | bytes 110600 | tf_op jit(solution)/shard_map/ppermute | solution.py:544
  51.3 4.9 %collective-permute-start.6 = (bf16[16,1152]{1,0:T(8,128)(2,1)S(1)}, bf16[16,1152]{1,0:T(8,128)(2,1)S(1)}, u32[]{:S(2)}, u32[]{:S(2)}) collective-permute-start(bf16[16,1152]{1,0:T(8,128)(2,1)S(1)} %pad_maximum_fusion.2), channel_id=1, source_target_pairs={{0,32},{32,0},{64,96},{96,64},{128,160},{160,128},{192,224},{224,1... | collective-permute-start | bytes 110600 | tf_op jit(solution)/shard_map/ppermute | solution.py:544
